TPU v7x, 32 devices: a whole 2x2x4 slice. The times are simulated.
32 devices in a mesh: dp: 2 (over x), context: 4 (over z), experts: 4 (over y, core).
Axes of the slice: x: 2, y: 2, z: 4, core: 2. Of those that a mesh axis runs over, the one named last changes fastest.
Arguments:
- tokens: bfloat16 [2, 1024, 2048], P('dp', 'context'), may hold values from -6 to 6
- positions: int32 [2, 1024], P('dp', 'context'), may hold values from 0 to 1023
- routes: int32 [2, 1024, 4], P('dp', 'context'), may hold values from 0 to 7, all different within a row; in each aligned block of 64 rows (0 to 63, 64 to 127, ..., all dimensions but the last counted through in order) at most 48 rows name the same one
- out_grad: bfloat16 [2, 1024, 2048], P('dp', 'context'), may hold values from -6 to 6
- norm1_gain: bfloat16 [2048], replicated, may hold values from 0.25 to 1.75
- qkv_weight: bfloat16 [2048, 3, 2048], P(('dp', 'context'), None, 'experts'), may hold values from -0.125 to 0.125
- qkv_bias: bfloat16 [3, 2048], P(None, 'experts'), may hold values from -0.59765625 to 0.59765625
- out_weight: bfloat16 [2048, 2048], P('experts', ('dp', 'context')), may hold values from -0.5 to 0.5
- norm2_gain: bfloat16 [2048], replicated, may hold values from 0.25 to 1.75
- router_weight: bfloat16 [2048, 8], replicated, may hold values from -0.25 to 0.25
- expert_gate: bfloat16 [8, 2048, 1408], P('experts', ('dp', 'context')), may hold values from -0.125 to 0.125
- expert_up: bfloat16 [8, 2048, 1408], P('experts', ('dp', 'context')), may hold values from -0.125 to 0.125
- expert_down: bfloat16 [8, 1408, 2048], P('experts', None, ('dp', 'context')), may hold values from -0.3125 to 0.3125
- shared_gate: bfloat16 [2048], replicated, may hold values from -0.125 to 0.125
- shared_w_gate: bfloat16 [2048, 5632], P(('dp', 'context'), 'experts'), may hold values from -0.125 to 0.125
- shared_w_up: bfloat16 [2048, 5632], P(('dp', 'context'), 'experts'), may hold values from -0.125 to 0.125
- shared_w_down: bfloat16 [5632, 2048], P('experts', ('dp', 'context')), may hold values from -0.15625 to 0.15625
Outputs:
- block_out: bfloat16 [2, 1024, 2048], P('dp', 'context')
- tokens_grad: float32 [2, 1024, 2048], P('dp', 'context')
- norm1_gain_grad: float32 [2048], replicated
- qkv_weight_grad: float32 [2048, 3, 2048], P(('dp', 'context'), None, 'experts')
- qkv_bias_grad: float32 [3, 2048], P(None, 'experts')
- out_weight_grad: float32 [2048, 2048], P('experts', ('dp', 'context'))
- norm2_gain_grad: float32 [2048], replicated
- router_weight_grad: float32 [2048, 8], replicated
- expert_gate_grad: float32 [8, 2048, 1408], P('experts', ('dp', 'context'))
- expert_up_grad: float32 [8, 2048, 1408], P('experts', ('dp', 'context'))
- expert_down_grad: float32 [8, 1408, 2048], P('experts', None, ('dp', 'context'))
- shared_gate_grad: float32 [2048], replicated
- shared_w_gate_grad: float32 [2048, 5632], P(('dp', 'context'), 'experts')
- shared_w_up_grad: float32 [2048, 5632], P(('dp', 'context'), 'experts')
- shared_w_down_grad: float32 [5632, 2048], P('experts', ('dp', 'context'))
Inputs may be any that keep to these rules, and one draw needn't show every extreme that they name: `routes`: in each aligned block of 64 rows of the flattened sequences and positions, no expert is named by more than 48 rows, a bound that some block reaches.
All inputs are finite; a program needn't handle non-finite values.
Results may differ from a plain program's by a relative error of at most 0.025.
Values may be sent and summed in bfloat16 or wider, within the bound.
A program may use at most 320 MiB of HBM per device.

v0:
```python
import jax
import jax.numpy as jnp
from jax import lax
from jax.sharding import PartitionSpec as P

HEAD_DIM = 128


EPSILON = 1e-06
ROPE_BASE = 1000000.0
MASKED = -1e30
PRECISE = lax.Precision.HIGHEST


def rope_tables(position_ids):
    half_dim = HEAD_DIM // 2
    inverse = ROPE_BASE ** (-2.0 * jnp.arange(half_dim, dtype=jnp.float32) / HEAD_DIM)
    angles = position_ids.astype(jnp.float32)[:, None] * inverse[None, :]
    cosine = jnp.cos(angles)
    sine_part = jnp.sin(angles)
    return (
        jnp.concatenate([cosine, cosine], -1)[:, None, :],
        jnp.concatenate([sine_part, sine_part], -1)[:, None, :],
    )


def rotate(value):
    half_dim = value.shape[-1] // 2
    return jnp.concatenate([-value[..., half_dim:], value[..., :half_dim]], -1)


def rotate_back(value):
    half_dim = value.shape[-1] // 2
    return jnp.concatenate([value[..., half_dim:], -value[..., :half_dim]], -1)


def silu_grad(gate_vals):
    sigmoid_vals = jax.nn.sigmoid(gate_vals)
    return sigmoid_vals * (1.0 + gate_vals * (1.0 - sigmoid_vals))


def block_rank(route_rows, expert_count):
    hits = (
        route_rows[:, :, None] == jnp.arange(expert_count, dtype=jnp.int32)[None, None, :]
    ).astype(jnp.int32)
    flat_hits = hits.reshape(-1, expert_count)
    earlier = jnp.cumsum(flat_hits, axis=0) - flat_hits
    return jnp.sum(earlier * flat_hits, -1).reshape(route_rows.shape)


def block_width_of():
    return 512


def gather_weights(shard_set):
    return (
        lax.all_gather(shard_set[0], ("dp", "context"), axis=0, tiled=True),
        lax.all_gather(shard_set[1], ("dp", "context"), axis=1, tiled=True),
        lax.all_gather(shard_set[2], ("dp", "context"), axis=1, tiled=True),
        lax.all_gather(shard_set[3], ("dp", "context"), axis=1, tiled=True),
        lax.all_gather(shard_set[4], ("dp", "context"), axis=2, tiled=True),
        lax.all_gather(shard_set[5], ("dp", "context"), axis=0, tiled=True),
        lax.all_gather(shard_set[6], ("dp", "context"), axis=0, tiled=True),
        lax.all_gather(shard_set[7], ("dp", "context"), axis=1, tiled=True),
    )


def forward_fold(query, query_first, scale, carry, piece):
    row_count, head_count, head_size = query.shape
    query_index = query_first + jnp.arange(row_count, dtype=jnp.int32)
    query_last = query_first + row_count - 1
    key_part, value_part = piece
    piece_rows = key_part.shape[0]
    block_width = block_width_of()
    block_count = piece_rows // block_width
    key_blocks = key_part.reshape(block_count, block_width, head_count, head_size)
    value_blocks = value_part.reshape(block_count, block_width, head_count, head_size)
    offsets = block_width * jnp.arange(block_count, dtype=jnp.int32)

    def forward_visit(state, item):
        key_block, value_block, first_key = item

        def forward_compute(current):
            run_max, run_sum, accum = current
            scores = (
                jnp.einsum("qhd,khd->hqk", query, key_block, preferred_element_type=jnp.float32)
                * scale
            )
            key_index = first_key + jnp.arange(block_width, dtype=jnp.int32)
            allowed = key_index[None, None, :] <= query_index[None, :, None]
            new_max = jnp.maximum(run_max, jnp.max(jnp.where(allowed, scores, MASKED), -1))
            weights = jnp.where(allowed, jnp.exp(scores - new_max[..., None]), 0.0)
            factor = jnp.exp(run_max - new_max)
            new_sum = run_sum * factor + jnp.sum(weights, -1)
            new_accum = accum * factor[..., None] + jnp.einsum(
                "hqk,khd->hqd",
                weights.astype(jnp.bfloat16),
                value_block,
                preferred_element_type=jnp.float32,
            )
            return (new_max, new_sum, new_accum)

        return (
            lax.cond(first_key > query_last, lambda current: current, forward_compute, state),
            None,
        )

    carry, _ = lax.scan(forward_visit, carry, (key_blocks, value_blocks, offsets))
    return carry


def key_grad_fold(key_rows, value_rows, key_first, scale, carry, piece):
    row_count, head_count, head_size = key_rows.shape
    key_index = key_first + jnp.arange(row_count, dtype=jnp.int32)
    query_part, dout_part, lse_part, delta_part = piece
    piece_rows = query_part.shape[0]
    block_width = block_width_of()
    block_count = piece_rows // block_width
    query_blocks = query_part.reshape(block_count, block_width, head_count, head_size)
    dout_blocks = dout_part.reshape(block_count, block_width, head_count, head_size)
    lse_blocks = lse_part.reshape(block_count, block_width, head_count)
    delta_blocks = delta_part.reshape(block_count, block_width, head_count)
    offsets = block_width * jnp.arange(block_count, dtype=jnp.int32)

    def key_visit(state, item):
        query_block, dout_block, lse_block, delta_block, first_query = item

        def key_compute(current):
            dkey_sum, dvalue_sum = current
            query_b = query_block.astype(jnp.bfloat16)
            dout_b = dout_block.astype(jnp.bfloat16)
            scores = (
                jnp.einsum("qhd,khd->hqk", query_b, key_rows, preferred_element_type=jnp.float32)
                * scale
            )
            query_index = first_query + jnp.arange(block_width, dtype=jnp.int32)
            allowed = key_index[None, None, :] <= query_index[None, :, None]
            prob_att = jnp.where(
                allowed, jnp.exp(scores - jnp.transpose(lse_block)[:, :, None]), 0.0
            )
            dvalue_sum = dvalue_sum + jnp.einsum(
                "hqk,qhd->hkd",
                prob_att.astype(jnp.bfloat16),
                dout_b,
                preferred_element_type=jnp.float32,
            )
            dprob = jnp.einsum(
                "qhd,khd->hqk", dout_b, value_rows, preferred_element_type=jnp.float32
            )
            dscore = (prob_att * (dprob - jnp.transpose(delta_block)[:, :, None])).astype(
                jnp.bfloat16
            )
            dkey_sum = (
                dkey_sum
                + jnp.einsum("hqk,qhd->hkd", dscore, query_b, preferred_element_type=jnp.float32)
                * scale
            )
            return (dkey_sum, dvalue_sum)

        return (
            lax.cond(
                first_query + block_width - 1 < key_first,
                lambda current: current,
                key_compute,
                state,
            ),
            None,
        )

    carry, _ = lax.scan(
        key_visit, carry, (query_blocks, dout_blocks, lse_blocks, delta_blocks, offsets)
    )
    return carry


def query_grad_fold(query, dattended, lse_heads, delta_heads, query_first, scale, carry, piece):
    row_count, head_count, head_size = query.shape
    query_index = query_first + jnp.arange(row_count, dtype=jnp.int32)
    query_last = query_first + row_count - 1
    key_part, value_part = piece
    piece_rows = key_part.shape[0]
    block_width = block_width_of()
    block_count = piece_rows // block_width
    key_blocks = key_part.reshape(block_count, block_width, head_count, head_size)
    value_blocks = value_part.reshape(block_count, block_width, head_count, head_size)
    offsets = block_width * jnp.arange(block_count, dtype=jnp.int32)

    def query_visit(state, item):
        key_block, value_block, first_key = item

        def query_compute(current):
            scores = (
                jnp.einsum("qhd,khd->hqk", query, key_block, preferred_element_type=jnp.float32)
                * scale
            )
            key_index = first_key + jnp.arange(block_width, dtype=jnp.int32)
            allowed = key_index[None, None, :] <= query_index[None, :, None]
            prob_att = jnp.where(allowed, jnp.exp(scores - lse_heads[:, :, None]), 0.0)
            dprob = jnp.einsum(
                "qhd,khd->hqk", dattended, value_block, preferred_element_type=jnp.float32
            )
            dscore = (prob_att * (dprob - delta_heads[:, :, None])).astype(jnp.bfloat16)
            return (
                current
                + jnp.einsum("hqk,khd->hqd", dscore, key_block, preferred_element_type=jnp.float32)
                * scale
            )

        return (
            lax.cond(first_key > query_last, lambda current: current, query_compute, state),
            None,
        )

    carry, _ = lax.scan(query_visit, carry, (key_blocks, value_blocks, offsets))
    return carry


def body(
    tokens,
    positions,
    routes,
    out_grad,
    norm1_gain,
    qkv_weight,
    qkv_bias,
    out_weight,
    norm2_gain,
    router_weight,
    expert_gate,
    expert_up,
    expert_down,
    shared_gate,
    shared_w_gate,
    shared_w_up,
    shared_w_down,
):
    row_count = tokens.shape[1]
    model_width = tokens.shape[2]
    head_span = qkv_bias.shape[1]
    heads_here = head_span // HEAD_DIM
    local_experts = expert_gate.shape[0]
    group_size = lax.axis_size("experts")
    quarter = row_count // group_size
    capacity = 3 * quarter // 4
    expert_count = local_experts * group_size
    group_index = lax.axis_index("experts")
    scale = HEAD_DIM ** (-0.5)
    shard_set = (
        qkv_weight,
        out_weight,
        expert_gate,
        expert_up,
        expert_down,
        shared_w_gate,
        shared_w_up,
        shared_w_down,
    )
    qkv_full, out_full, gate_full, up_full, down_full, sgate_full, sup_full, sdown_full = (
        gather_weights(shard_set)
    )
    token_float = tokens[0].astype(jnp.float32)
    inverse1 = lax.rsqrt(jnp.mean(token_float * token_float, -1, keepdims=True) + EPSILON)
    normed1 = token_float * inverse1
    gain1 = norm1_gain.astype(jnp.float32)
    normed1_b = (normed1 * gain1).astype(jnp.bfloat16)
    qkv_flat = qkv_full.reshape(model_width, 3 * head_span)
    qkv = (
        jnp.dot(normed1_b, qkv_flat, preferred_element_type=jnp.float32).reshape(
            row_count, 3, head_span
        )
        + qkv_bias.astype(jnp.float32)[None]
    )
    cosine, sine_part = rope_tables(positions[0])
    query_raw = qkv[:, 0].reshape(row_count, heads_here, HEAD_DIM)
    key_raw = qkv[:, 1].reshape(row_count, heads_here, HEAD_DIM)
    query = (query_raw * cosine + rotate(query_raw) * sine_part).astype(jnp.bfloat16)
    key_rows = (key_raw * cosine + rotate(key_raw) * sine_part).astype(jnp.bfloat16)
    value_flat = qkv[:, 2].astype(jnp.bfloat16)
    key_flat = key_rows.reshape(row_count, head_span)
    value_rows = value_flat.reshape(row_count, heads_here, HEAD_DIM)
    query_first = lax.axis_index("context") * row_count
    start_state = (
        jnp.full((heads_here, row_count), MASKED, jnp.float32),
        jnp.zeros((heads_here, row_count), jnp.float32),
        jnp.zeros((heads_here, row_count, HEAD_DIM), jnp.float32),
    )
    run_max, run_sum, accum = forward_fold(
        query,
        query_first,
        scale,
        start_state,
        (
            lax.all_gather(key_flat, "context", axis=0, tiled=True),
            lax.all_gather(value_flat, "context", axis=0, tiled=True),
        ),
    )
    attended = jnp.transpose(accum / run_sum[..., None], (1, 0, 2)).astype(jnp.bfloat16)
    lse_heads = run_max + jnp.log(run_sum)
    attended_flat = attended.reshape(row_count, head_span)
    head_part = jnp.dot(attended_flat, out_full, preferred_element_type=jnp.float32)
    hidden = token_float + lax.psum(head_part, "experts")
    inverse2 = lax.rsqrt(jnp.mean(hidden * hidden, -1, keepdims=True) + EPSILON)
    normed2 = hidden * inverse2
    gain2 = norm2_gain.astype(jnp.float32)
    normed2_b = (normed2 * gain2).astype(jnp.bfloat16)
    first_row = group_index * quarter
    normed2_q = lax.dynamic_slice_in_dim(normed2_b, first_row, quarter, 0)
    route_q = lax.dynamic_slice_in_dim(routes[0], first_row, quarter, 0)
    logits = jnp.dot(normed2_q, router_weight, preferred_element_type=jnp.float32)
    prob = jax.nn.softmax(logits, -1)
    gate_k = jnp.take_along_axis(prob, route_q, 1)
    slot_ids = route_q * capacity + block_rank(route_q, expert_count)
    slot_hits = (
        slot_ids[:, :, None] == jnp.arange(expert_count * capacity, dtype=jnp.int32)[None, None, :]
    )
    placer = jnp.sum(slot_hits.astype(jnp.bfloat16), 1)
    send_rows = (
        jnp.dot(placer.T, normed2_q, preferred_element_type=jnp.float32)
        .astype(jnp.bfloat16)
        .reshape(group_size, local_experts, capacity, model_width)
    )
    arrived = lax.all_to_all(send_rows, "experts", split_axis=0, concat_axis=0, tiled=True)
    expert_gvals = jnp.einsum(
        "secd,edf->secf", arrived, gate_full, preferred_element_type=jnp.float32
    )
    expert_uvals = jnp.einsum(
        "secd,edf->secf", arrived, up_full, preferred_element_type=jnp.float32
    )
    expert_act = (jax.nn.silu(expert_gvals) * expert_uvals).astype(jnp.bfloat16)
    expert_out = jnp.einsum(
        "secf,efd->secd", expert_act, down_full, preferred_element_type=jnp.float32
    ).astype(jnp.bfloat16)
    returned = lax.all_to_all(
        expert_out, "experts", split_axis=0, concat_axis=0, tiled=True
    ).reshape(expert_count * capacity, model_width)
    picked = returned[slot_ids].astype(jnp.float32)
    routed = jnp.sum(gate_k[:, :, None] * picked, 1)
    shared_sig = jax.nn.sigmoid(
        jnp.dot(normed2_b, shared_gate[:, None], preferred_element_type=jnp.float32)[:, 0]
    )
    shared_gvals = jnp.dot(normed2_b, sgate_full, preferred_element_type=jnp.float32)
    shared_uvals = jnp.dot(normed2_b, sup_full, preferred_element_type=jnp.float32)
    shared_act = (jax.nn.silu(shared_gvals) * shared_uvals).astype(jnp.bfloat16)
    shared_part = jnp.dot(shared_act, sdown_full, preferred_element_type=jnp.float32)
    routed_pad = lax.dynamic_update_slice_in_dim(
        jnp.zeros((row_count, model_width), jnp.float32), routed, first_row, 0
    )
    branch_total = lax.psum(
        (shared_sig[:, None] * shared_part + routed_pad).astype(jnp.bfloat16), "experts"
    ).astype(jnp.float32)
    block_out = (hidden + branch_total).astype(jnp.bfloat16)
    held = lax.optimization_barrier((shard_set, block_out))
    qkv_full, out_full, gate_full, up_full, down_full, sgate_full, sup_full, sdown_full = (
        gather_weights(held[0])
    )
    qkv_flat = qkv_full.reshape(model_width, 3 * head_span)
    grad_float = out_grad[0].astype(jnp.float32)
    grad_q = lax.dynamic_slice_in_dim(grad_float, first_row, quarter, 0)
    dgate_k = jnp.sum(grad_q[:, None, :] * picked, -1)
    weighted = jnp.sum(slot_hits.astype(jnp.float32) * gate_k[:, :, None], 1)
    dsend = (
        jnp.dot(weighted.T, grad_q, precision=PRECISE)
        .astype(jnp.bfloat16)
        .reshape(group_size, local_experts, capacity, model_width)
    )
    darrived = lax.all_to_all(dsend, "experts", split_axis=0, concat_axis=0, tiled=True)
    expert_dact = jnp.einsum(
        "secd,efd->secf", darrived, down_full, preferred_element_type=jnp.float32
    )
    down_grad = jnp.einsum(
        "secf,secd->efd", expert_act, darrived, preferred_element_type=jnp.float32
    )
    expert_dgate = (expert_dact * expert_uvals * silu_grad(expert_gvals)).astype(jnp.bfloat16)
    expert_dup = (expert_dact * jax.nn.silu(expert_gvals)).astype(jnp.bfloat16)
    gate_grad = jnp.einsum(
        "secd,secf->edf", arrived, expert_dgate, preferred_element_type=jnp.float32
    )
    up_grad = jnp.einsum("secd,secf->edf", arrived, expert_dup, preferred_element_type=jnp.float32)
    expert_din = (
        jnp.einsum("secf,edf->secd", expert_dgate, gate_full, preferred_element_type=jnp.float32)
        + jnp.einsum("secf,edf->secd", expert_dup, up_full, preferred_element_type=jnp.float32)
    ).astype(jnp.bfloat16)
    dreturned = lax.all_to_all(
        expert_din, "experts", split_axis=0, concat_axis=0, tiled=True
    ).reshape(expert_count * capacity, model_width)
    dnormed2_q = jnp.dot(placer, dreturned, preferred_element_type=jnp.float32)
    route_hits = (
        route_q[:, :, None] == jnp.arange(expert_count, dtype=jnp.int32)[None, None, :]
    ).astype(jnp.float32)
    dprob = jnp.sum(route_hits * dgate_k[:, :, None], 1)
    dlogit = prob * (dprob - jnp.sum(prob * dprob, -1, keepdims=True))
    router_part = jnp.dot(normed2_q.astype(jnp.float32).T, dlogit, precision=PRECISE)
    dnormed2_q = dnormed2_q + jnp.dot(
        dlogit, router_weight.astype(jnp.float32).T, precision=PRECISE
    )
    shared_dout = (shared_sig[:, None] * grad_float).astype(jnp.bfloat16)
    shared_dact = jnp.dot(shared_dout, sdown_full.T, preferred_element_type=jnp.float32)
    sdown_grad = jnp.dot(shared_act.T, shared_dout, preferred_element_type=jnp.float32)
    shared_dgate = (shared_dact * shared_uvals * silu_grad(shared_gvals)).astype(jnp.bfloat16)
    shared_dup = (shared_dact * jax.nn.silu(shared_gvals)).astype(jnp.bfloat16)
    sgate_grad = jnp.dot(normed2_b.T, shared_dgate, preferred_element_type=jnp.float32)
    sup_grad = jnp.dot(normed2_b.T, shared_dup, preferred_element_type=jnp.float32)
    row_dots = jnp.sum(grad_float * shared_part, -1)
    dnormed2_part = jnp.dot(
        shared_dgate, sgate_full.T, preferred_element_type=jnp.float32
    ) + jnp.dot(shared_dup, sup_full.T, preferred_element_type=jnp.float32)
    dnormed2_part = dnormed2_part + lax.dynamic_update_slice_in_dim(
        jnp.zeros((row_count, model_width), jnp.float32), dnormed2_q, first_row, 0
    )
    dnormed2, row_dots, router_grad = lax.psum((dnormed2_part, row_dots, router_part), "experts")
    coef = shared_sig * (1.0 - shared_sig) * row_dots
    dnormed2 = dnormed2 + coef[:, None] * shared_gate.astype(jnp.float32)[None, :]
    shared_gate_grad = jnp.dot(coef, normed2_b.astype(jnp.float32), precision=PRECISE)
    norm2_grad = jnp.sum(dnormed2 * normed2, 0)
    dscaled2 = dnormed2 * gain2
    dhidden = grad_float + inverse2 * (
        dscaled2 - normed2 * jnp.mean(dscaled2 * normed2, -1, keepdims=True)
    )
    dhidden_b = dhidden.astype(jnp.bfloat16)
    out_grad_part = jnp.dot(attended_flat.T, dhidden_b, preferred_element_type=jnp.float32)
    dattended = jnp.dot(dhidden_b, out_full.T, preferred_element_type=jnp.float32).astype(
        jnp.bfloat16
    )
    dattended3 = dattended.reshape(row_count, heads_here, HEAD_DIM)
    delta = jnp.sum(dattended3.astype(jnp.float32) * attended.astype(jnp.float32), -1)
    zero_state = jnp.zeros((heads_here, row_count, HEAD_DIM), jnp.float32)
    dkey_sum, dvalue_sum = key_grad_fold(
        key_rows,
        value_rows,
        query_first,
        scale,
        (zero_state, zero_state),
        (
            lax.all_gather(
                query.reshape(row_count, head_span).astype(jnp.float32),
                "context",
                axis=0,
                tiled=True,
            ),
            lax.all_gather(dattended.astype(jnp.float32), "context", axis=0, tiled=True),
            lax.all_gather(jnp.transpose(lse_heads), "context", axis=0, tiled=True),
            lax.all_gather(delta, "context", axis=0, tiled=True),
        ),
    )
    dquery_sum = query_grad_fold(
        query,
        dattended3,
        lse_heads,
        jnp.transpose(delta),
        query_first,
        scale,
        zero_state,
        (
            lax.all_gather(key_flat, "context", axis=0, tiled=True),
            lax.all_gather(value_flat, "context", axis=0, tiled=True),
        ),
    )
    dquery = jnp.transpose(dquery_sum, (1, 0, 2))
    dkey = jnp.transpose(dkey_sum, (1, 0, 2))
    dvalue = jnp.transpose(dvalue_sum, (1, 0, 2))
    dquery_raw = dquery * cosine + rotate_back(dquery * sine_part)
    dkey_raw = dkey * cosine + rotate_back(dkey * sine_part)
    dqkv = jnp.stack(
        [
            dquery_raw.reshape(row_count, head_span),
            dkey_raw.reshape(row_count, head_span),
            dvalue.reshape(row_count, head_span),
        ],
        1,
    )
    bias_grad = jnp.sum(dqkv, 0)
    dqkv_b = dqkv.astype(jnp.bfloat16).reshape(row_count, 3 * head_span)
    qkv_grad = jnp.dot(normed1_b.T, dqkv_b, preferred_element_type=jnp.float32).reshape(
        model_width, 3, head_span
    )
    dnormed1 = lax.psum(
        jnp.dot(dqkv_b, qkv_flat.T, preferred_element_type=jnp.float32).astype(jnp.bfloat16),
        "experts",
    ).astype(jnp.float32)
    norm1_grad = jnp.sum(dnormed1 * normed1, 0)
    dscaled1 = dnormed1 * gain1
    tokens_grad = dhidden + inverse1 * (
        dscaled1 - normed1 * jnp.mean(dscaled1 * normed1, -1, keepdims=True)
    )
    small_sums = (
        lax.psum(norm1_grad.astype(jnp.bfloat16), ("dp", "context")).astype(jnp.float32),
        lax.psum(norm2_grad.astype(jnp.bfloat16), ("dp", "context")).astype(jnp.float32),
        lax.psum(router_grad.astype(jnp.bfloat16), ("dp", "context")).astype(jnp.float32),
        lax.psum(shared_gate_grad.astype(jnp.bfloat16), ("dp", "context")).astype(jnp.float32),
        lax.psum(bias_grad.astype(jnp.bfloat16), ("dp", "context")).astype(jnp.float32),
    )
    large_sums = (
        lax.psum_scatter(
            qkv_grad.astype(jnp.bfloat16), ("dp", "context"), scatter_dimension=0, tiled=True
        ).astype(jnp.float32),
        lax.psum_scatter(
            out_grad_part.astype(jnp.bfloat16), ("dp", "context"), scatter_dimension=1, tiled=True
        ).astype(jnp.float32),
        lax.psum_scatter(
            gate_grad.astype(jnp.bfloat16), ("dp", "context"), scatter_dimension=1, tiled=True
        ).astype(jnp.float32),
        lax.psum_scatter(
            up_grad.astype(jnp.bfloat16), ("dp", "context"), scatter_dimension=1, tiled=True
        ).astype(jnp.float32),
        lax.psum_scatter(
            down_grad.astype(jnp.bfloat16), ("dp", "context"), scatter_dimension=2, tiled=True
        ).astype(jnp.float32),
        lax.psum_scatter(
            sgate_grad.astype(jnp.bfloat16), ("dp", "context"), scatter_dimension=0, tiled=True
        ).astype(jnp.float32),
        lax.psum_scatter(
            sup_grad.astype(jnp.bfloat16), ("dp", "context"), scatter_dimension=0, tiled=True
        ).astype(jnp.float32),
        lax.psum_scatter(
            sdown_grad.astype(jnp.bfloat16), ("dp", "context"), scatter_dimension=1, tiled=True
        ).astype(jnp.float32),
    )
    return (
        block_out[None],
        tokens_grad[None],
        small_sums[0],
        large_sums[0],
        small_sums[4],
        large_sums[1],
        small_sums[1],
        small_sums[2],
        large_sums[2],
        large_sums[3],
        large_sums[4],
        small_sums[3],
        large_sums[5],
        large_sums[6],
        large_sums[7],
    )


def solution(mesh):
    return jax.shard_map(
        body,
        mesh=mesh,
        in_specs=(
            P("dp", "context", None),
            P("dp", "context"),
            P("dp", "context", None),
            P("dp", "context", None),
            P(),
            P(("dp", "context"), None, "experts"),
            P(None, "experts"),
            P("experts", ("dp", "context")),
            P(),
            P(),
            P("experts", ("dp", "context"), None),
            P("experts", ("dp", "context"), None),
            P("experts", None, ("dp", "context")),
            P(),
            P(("dp", "context"), "experts"),
            P(("dp", "context"), "experts"),
            P("experts", ("dp", "context")),
        ),
        out_specs=(
            P("dp", "context", None),
            P("dp", "context", None),
            P(),
            P(("dp", "context"), None, "experts"),
            P(None, "experts"),
            P("experts", ("dp", "context")),
            P(),
            P(),
            P("experts", ("dp", "context"), None),
            P("experts", ("dp", "context"), None),
            P("experts", None, ("dp", "context")),
            P(),
            P(("dp", "context"), "experts"),
            P(("dp", "context"), "experts"),
            P("experts", ("dp", "context")),
        ),
        check_vma=False,
    )
```

profile of v0, /device:TPU:16, one launch (start us, length us, event | category | flops | bytes accessed | tf_op | source)
XLA Modules:
  0.0 3338.5 jit_solution(17531489854084487848)
XLA Ops:
  11.5 98.9 %all-gather.22.cloned.1.call-done = bf16[2048,3,512]{0,2,1:T(8,128)(2,1)} async-done(((bf16[256,3,512]{0,2,1:T(8,128)(2,1)}), bf16[2048,3,512]{0,2,1:T(8,128)(2,1)}) %all-gather.22.cloned.1.call-update) | async-done | bytes 6291472 | tf_op jit(solution)/shard_map/all_gather | solution.py:57
  122.5 24.1 all-gather.24.cloned.1.call-done
  148.1 27.5 all-gather.60.cloned.1.call-done
  186.9 40.0 %all-gather.26.cloned.1.call-done = bf16[512,2048]{1,0:T(8,128)(2,1)} async-done(((bf16[512,256]{1,0:T(8,128)(2,1)}), bf16[512,2048]{1,0:T(8,128)(2,1)}) %all-gather.26.cloned.1.call-update) | async-done | bytes 2097168 | tf_op jit(solution)/shard_map/all_gather | solution.py:58
  238.7 42.6 %all-reduce.7.cloned.1.call-done = f32[256,2048]{1,0:T(8,128)} async-done(((f32[256,2048]{1,0:T(8,128)}), f32[256,2048]{1,0:T(8,128)}) %all-reduce.7.cloned.1.call-update) | async-done | bytes 2097168 | tf_op jit(solution)/shard_map/psum | solution.py:301
  292.5 82.3 %all-gather.28.cloned.1.call-done = bf16[2048,1408]{1,0:T(8,128)(2,1)} async-done(((bf16[256,1408]{1,0:T(8,128)(2,1)}), bf16[2048,1408]{1,0:T(8,128)(2,1)}) %all-gather.28.cloned.1.call-update) | async-done | bytes 5767184 | tf_op jit(solution)/shard_map/all_gather | solution.py:62
  380.3 158.1 %all-gather.34.cloned.1.call-done = bf16[2,2048,1408]{2,1,0:T(8,128)(2,1)} async-done(((bf16[2,256,1408]{2,1,0:T(8,128)(2,1)}), bf16[2,2048,1408]{2,1,0:T(8,128)(2,1)}) %all-gather.34.cloned.1.call-update) | async-done | bytes 11534352 | tf_op jit(solution)/shard_map/all_gather | solution.py:59
  546.7 155.4 %all-gather.36.cloned.1.call-done = bf16[2,2048,1408]{2,1,0:T(8,128)(2,1)} async-done(((bf16[2,256,1408]{2,1,0:T(8,128)(2,1)}), bf16[2,2048,1408]{2,1,0:T(8,128)(2,1)}) %all-gather.36.cloned.1.call-update) | async-done | bytes 11534352 | tf_op jit(solution)/shard_map/all_gather | solution.py:60
  711.4 154.3 %all-gather.38.cloned.1.call-done = bf16[2,1408,2048]{2,1,0:T(8,128)(2,1)} async-done(((bf16[2,1408,256]{2,1,0:T(8,128)(2,1)}), bf16[2,1408,2048]{2,1,0:T(8,128)(2,1)}) %all-gather.38.cloned.1.call-update) | async-done | bytes 11534352 | tf_op jit(solution)/shard_map/all_gather | solution.py:61
  878.3 79.8 %all-gather.30.cloned.1.call-done = bf16[2048,1408]{1,0:T(8,128)(2,1)} async-done(((bf16[256,1408]{1,0:T(8,128)(2,1)}), bf16[2048,1408]{1,0:T(8,128)(2,1)}) %all-gather.30.cloned.1.call-update) | async-done | bytes 5767184 | tf_op jit(solution)/shard_map/all_gather | solution.py:63
  964.4 87.1 %all-gather.32.cloned.1.call-done = bf16[1408,2048]{1,0:T(8,128)(2,1)} async-done(((bf16[1408,256]{1,0:T(8,128)(2,1)}), bf16[1408,2048]{1,0:T(8,128)(2,1)}) %all-gather.32.cloned.1.call-update) | async-done | bytes 5767184 | tf_op jit(solution)/shard_map/all_gather | solution.py:64
  1084.7 35.6 %all-reduce.9.cloned.1.call-done = bf16[256,2048]{1,0:T(8,128)(2,1)} async-done(((bf16[256,2048]{1,0:T(8,128)(2,1)}), bf16[256,2048]{1,0:T(8,128)(2,1)}) %all-reduce.9.cloned.1.call-update) | async-done | bytes 1048592 | tf_op jit(solution)/shard_map/psum | solution.py:348
  1154.1 131.8 %all-gather.48.cloned.1.call-done = bf16[2,1408,2048]{2,1,0:T(8,128)(2,1)} async-done(((bf16[2,1408,256]{2,1,0:T(8,128)(2,1)}), bf16[2,1408,2048]{2,1,0:T(8,128)(2,1)}) %all-gather.48.cloned.1.call-update) | async-done | bytes 11534352 | tf_op jit(solution)/shard_map/all_gather | solution.py:61
  1297.2 152.2 %all-gather.50.cloned.1.call-done = bf16[2,2048,1408]{2,1,0:T(8,128)(2,1)} async-done(((bf16[2,256,1408]{2,1,0:T(8,128)(2,1)}), bf16[2,2048,1408]{2,1,0:T(8,128)(2,1)}) %all-gather.50.cloned.1.call-update) | async-done | bytes 11534352 | tf_op jit(solution)/shard_map/all_gather | solution.py:60
  1459.6 153.3 %all-gather.46.cloned.1.call-done = bf16[2,2048,1408]{2,1,0:T(8,128)(2,1)} async-done(((bf16[2,256,1408]{2,1,0:T(8,128)(2,1)}), bf16[2,2048,1408]{2,1,0:T(8,128)(2,1)}) %all-gather.46.cloned.1.call-update) | async-done | bytes 11534352 | tf_op jit(solution)/shard_map/all_gather | solution.py:59
  1631.0 75.1 %all-gather.40.cloned.1.call-done = bf16[1408,2048]{1,0:T(8,128)(2,1)} async-done(((bf16[1408,256]{1,0:T(8,128)(2,1)}), bf16[1408,2048]{1,0:T(8,128)(2,1)}) %all-gather.40.cloned.1.call-update) | async-done | bytes 5767184 | tf_op jit(solution)/shard_map/all_gather | solution.py:64
  1713.1 85.5 %all-gather.42.cloned.1.call-done = bf16[2048,1408]{1,0:T(8,128)(2,1)} async-done(((bf16[256,1408]{1,0:T(8,128)(2,1)}), bf16[2048,1408]{1,0:T(8,128)(2,1)}) %all-gather.42.cloned.1.call-update) | async-done | bytes 5767184 | tf_op jit(solution)/shard_map/all_gather | solution.py:62
  1804.6 86.5 %all-gather.44.cloned.1.call-done = bf16[2048,1408]{1,0:T(8,128)(2,1)} async-done(((bf16[256,1408]{1,0:T(8,128)(2,1)}), bf16[2048,1408]{1,0:T(8,128)(2,1)}) %all-gather.44.cloned.1.call-update) | async-done | bytes 5767184 | tf_op jit(solution)/shard_map/all_gather | solution.py:63
  1902.0 49.2 %all-reduce.11.cloned.1.call-done = f32[256,2048]{1,0:T(8,128)} async-done(((f32[256,2048]{1,0:T(8,128)}), f32[256,2048]{1,0:T(8,128)}) %all-reduce.11.cloned.1.call-update) | async-done | bytes 2097168 | tf_op jit(solution)/shard_map/psum | solution.py:410
  1956.0 46.7 %all-gather.52.cloned.1.call-done = bf16[512,2048]{1,0:T(8,128)(2,1)} async-done(((bf16[512,256]{1,0:T(8,128)(2,1)}), bf16[512,2048]{1,0:T(8,128)(2,1)}) %all-gather.52.cloned.1.call-update) | async-done | bytes 2097168 | tf_op jit(solution)/shard_map/all_gather | solution.py:58
  2049.6 19.6 all_gather.88
  2106.7 61.2 %all-gather.58.cloned.1.call-done = bf16[2048,3,512]{2,0,1:T(8,128)(2,1)} async-done(((bf16[256,3,512]{2,0,1:T(8,128)(2,1)}), bf16[2048,3,512]{2,0,1:T(8,128)(2,1)}) %all-gather.58.cloned.1.call-update) | async-done | bytes 6291472 | tf_op jit(solution)/shard_map/all_gather | solution.py:57
  2204.2 76.6 %reduce-scatter.23.cloned.1.call-done = bf16[1408,256]{1,0:T(8,128)(2,1)} async-done(((bf16[1408,2048]{1,0:T(8,128)(2,1)}), bf16[1408,256]{1,0:T(8,128)(2,1)}) %reduce-scatter.23.cloned.1.call-update) | async-done | bytes 720912 | tf_op jit(solution)/shard_map/reduce_scatter | solution.py:514
  2283.2 193.6 %reduce-scatter.17.cloned.1.call-done = bf16[2,1408,256]{2,1,0:T(8,128)(2,1)} async-done(((bf16[2,1408,2048]{2,1,0:T(8,128)(2,1)}), bf16[2,1408,256]{2,1,0:T(8,128)(2,1)}) %reduce-scatter.17.cloned.1.call-update) | async-done | bytes 1441808 | tf_op jit(solution)/shard_map/reduce_scatter | solution.py:505
  2480.0 110.3 %reduce-scatter.19.cloned.1.call-done = bf16[256,1408]{1,0:T(8,128)(2,1)} async-done(((bf16[2048,1408]{1,0:T(8,128)(2,1)}), bf16[256,1408]{1,0:T(8,128)(2,1)}) %reduce-scatter.19.cloned.1.call-update) | async-done | bytes 720912 | tf_op jit(solution)/shard_map/reduce_scatter | solution.py:508
  2592.6 111.2 %reduce-scatter.21.cloned.1.call-done = bf16[256,1408]{1,0:T(8,128)(2,1)} async-done(((bf16[2048,1408]{1,0:T(8,128)(2,1)}), bf16[256,1408]{1,0:T(8,128)(2,1)}) %reduce-scatter.21.cloned.1.call-update) | async-done | bytes 720912 | tf_op jit(solution)/shard_map/reduce_scatter | solution.py:511
  2706.0 37.0 %all-reduce.13.cloned.1.call-done = bf16[256,2048]{1,0:T(8,128)(2,1)} async-done(((bf16[256,2048]{1,0:T(8,128)(2,1)}), bf16[256,2048]{1,0:T(8,128)(2,1)}) %all-reduce.13.cloned.1.call-update) | async-done | bytes 1048592 | tf_op jit(solution)/shard_map/psum | solution.py:476
  2745.1 35.8 %all-reduce.1 = (bf16[2048]{0:T(1024)(128)(2,1)S(1)}, bf16[3,512]{1,0:T(4,128)(2,1)S(1)}, bf16[2048]{0:T(1024)(128)(2,1)S(1)}, bf16[2048,8]{0,1:T(8,128)(2,1)S(1)}, bf16[2048]{0:T(1024)(128)(2,1)S(1)}) all-reduce(bf16[2048]{0:T(1024)(128)(2,1)S(1)} %get-tuple-element.980, ...), channel_id=1, replica_groups=mesh['dp'=2,'context'=4,'experts'=4] {'dp','context'}, use_global_device_ids=true, to_apply=%region_37.38 | all-reduce | flops 24064 | bytes 96256 | tf_op jit(solution)/shard_map/psum | solution.py:486
  2787.1 29.1 reduce-scatter.11.cloned.1.call-done
  2817.9 119.5 %reduce-scatter.9.cloned.1.call-done = bf16[256,3,512]{2,0,1:T(8,128)(2,1)} async-done(((bf16[2048,3,512]{2,0,1:T(8,128)(2,1)}), bf16[256,3,512]{2,0,1:T(8,128)(2,1)}) %reduce-scatter.9.cloned.1.call-update) | async-done | bytes 786448 | tf_op jit(solution)/shard_map/reduce_scatter | solution.py:493
  2939.9 193.1 %reduce-scatter.13.cloned.1.call-done = bf16[2,256,1408]{2,1,0:T(8,128)(2,1)} async-done(((bf16[2,2048,1408]{2,1,0:T(8,128)(2,1)}), bf16[2,256,1408]{2,1,0:T(8,128)(2,1)}) %reduce-scatter.13.cloned.1.call-update) | async-done | bytes 1441808 | tf_op jit(solution)/shard_map/reduce_scatter | solution.py:499
  3136.2 192.4 %reduce-scatter.15.cloned.1.call-done = bf16[2,256,1408]{2,1,0:T(8,128)(2,1)} async-done(((bf16[2,2048,1408]{2,1,0:T(8,128)(2,1)}), bf16[2,256,1408]{2,1,0:T(8,128)(2,1)}) %reduce-scatter.15.cloned.1.call-update) | async-done | bytes 1441808 | tf_op jit(solution)/shard_map/reduce_scatter | solution.py:502
  (399 shorter events, 434.3 us)
Async XLA Ops:
  7.2 103.1 %all-gather.22.cloned.1.call-start = ((), (), s32[]{:S(2)}) async-start(), calls=%async_computation.12 | async-start | bytes 7077888 | tf_op jit(solution)/shard_map/all_gather | solution.py:57
  9.7 137.0 %all-gather.24.cloned.1.call-start = ((), (), s32[]{:S(2)}) async-start(), calls=%async_computation.13 | async-start | bytes 1310720 | tf_op jit(solution)/shard_map/all_gather | solution.py:293
  121.9 105.1 %all-gather.26.cloned.1.call-start = ((), (), s32[]{:S(2)}) async-start(), calls=%async_computation.14 | async-start | bytes 2359296 | tf_op jit(solution)/shard_map/all_gather | solution.py:58
  122.5 158.8 %all-reduce.7.cloned.1.call-start = ((), (), s32[]{:S(2)}) async-start(), calls=%async_computation.15 | async-start | bytes 4194304 | tf_op jit(solution)/shard_map/psum | solution.py:301
  230.6 144.2 %all-gather.28.cloned.1.call-start = ((), (), s32[]{:S(2)}) async-start(), calls=%async_computation.16 | async-start | bytes 6488064 | tf_op jit(solution)/shard_map/all_gather | solution.py:62
  231.2 307.2 %all-gather.34.cloned.1.call-start = ((), (), s32[]{:S(2)}) async-start(), calls=%async_computation.19 | async-start | bytes 12976128 | tf_op jit(solution)/shard_map/all_gather | solution.py:59
  232.0 470.1 %all-gather.36.cloned.1.call-start = ((), (), s32[]{:S(2)}) async-start(), calls=%async_computation.20 | async-start | bytes 12976128 | tf_op jit(solution)/shard_map/all_gather | solution.py:60
  232.7 632.9 %all-gather.38.cloned.1.call-start = ((), (), s32[]{:S(2)}) async-start(), calls=%async_computation.21 | async-start | bytes 12976128 | tf_op jit(solution)/shard_map/all_gather | solution.py:61
  233.5 724.7 %all-gather.30.cloned.1.call-start = ((), (), s32[]{:S(2)}) async-start(), calls=%async_computation.17 | async-start | bytes 6488064 | tf_op jit(solution)/shard_map/all_gather | solution.py:63
  234.1 817.4 %all-gather.32.cloned.1.call-start = ((), (), s32[]{:S(2)}) async-start(), calls=%async_computation.18 | async-start | bytes 6488064 | tf_op jit(solution)/shard_map/all_gather | solution.py:64
  874.2 184.1 %all-to-all-start.1 = ((bf16[4,2,48,2048]{3,2,1,0:T(8,128)(2,1)}), bf16[4,2,48,2048]{3,2,1,0:T(8,128)(2,1)S(1)}, u32[]{:S(2)}, u32[]{:S(2)}) async-start(bf16[4,2,48,2048]{3,2,1,0:T(8,128)(2,1)} %copy.269), calls=%async_computation.1 | async-start | bytes 3145728 | tf_op jit(solution)/shard_map/all_to_all | solution.py:333
  877.9 242.4 %all-reduce.9.cloned.1.call-start = ((), (), s32[]{:S(2)}) async-start(), calls=%async_computation.22 | async-start | bytes 2097152 | tf_op jit(solution)/shard_map/psum | solution.py:348
  1084.7 201.2 %all-gather.48.cloned.1.call-start = ((), (), s32[]{:S(2)}) async-start(), calls=%async_computation.27 | async-start | bytes 12976128 | tf_op jit(solution)/shard_map/all_gather | solution.py:61
  1122.8 326.6 %all-gather.50.cloned.1.call-start = ((), (), s32[]{:S(2)}) async-start(), calls=%async_computation.28 | async-start | bytes 12976128 | tf_op jit(solution)/shard_map/all_gather | solution.py:60
  1123.4 489.5 %all-gather.46.cloned.1.call-start = ((), (), s32[]{:S(2)}) async-start(), calls=%async_computation.26 | async-start | bytes 12976128 | tf_op jit(solution)/shard_map/all_gather | solution.py:59
  1124.0 582.2 %all-gather.40.cloned.1.call-start = ((), (), s32[]{:S(2)}) async-start(), calls=%async_computation.23 | async-start | bytes 6488064 | tf_op jit(solution)/shard_map/all_gather | solution.py:64
  1124.5 674.1 %all-gather.42.cloned.1.call-start = ((), (), s32[]{:S(2)}) async-start(), calls=%async_computation.24 | async-start | bytes 6488064 | tf_op jit(solution)/shard_map/all_gather | solution.py:62
  1125.1 766.0 %all-gather.44.cloned.1.call-start = ((), (), s32[]{:S(2)}) async-start(), calls=%async_computation.25 | async-start | bytes 6488064 | tf_op jit(solution)/shard_map/all_gather | solution.py:63
  1626.4 271.3 %all-to-all-start.3 = ((bf16[4,2,48,2048]{3,2,1,0:T(8,128)(2,1)}), bf16[4,2,48,2048]{3,2,1,0:T(8,128)(2,1)}, u32[]{:S(2)}, u32[]{:S(2)}) async-start(bf16[4,2,48,2048]{3,2,1,0:T(8,128)(2,1)} %copy.271), calls=%async_computation.3 | async-start | bytes 3145728 | tf_op jit(solution)/shard_map/all_to_all | solution.py:383
  1630.8 320.5 %all-reduce.11.cloned.1.call-start = ((), (), s32[]{:S(2)}) async-start(), calls=%async_computation.29 | async-start | bytes 4194304 | tf_op jit(solution)/shard_map/psum | solution.py:410
  1901.2 132.9 %all-gather.54.cloned.1.call-start = ((), (), s32[]{:S(2)}) async-start(), calls=%async_computation.31 | async-start | bytes 1310720 | tf_op jit(solution)/shard_map/all_gather | solution.py:434
  1902.0 184.1 %all-gather.56.cloned.1.call-start = ((), (), s32[]{:S(2)}) async-start(), calls=%async_computation.32 | async-start | bytes 1310720 | tf_op jit(solution)/shard_map/all_gather | solution.py:440
  2006.4 161.5 %all-gather.58.cloned.1.call-start = ((), (), s32[]{:S(2)}) async-start(), calls=%async_computation.33 | async-start | bytes 7077888 | tf_op jit(solution)/shard_map/all_gather | solution.py:57
  2007.1 273.7 %reduce-scatter.23.cloned.1.call-start = ((), (), s32[]{:S(2)}) async-start(), calls=%async_computation.42 | async-start | bytes 6488064 | tf_op jit(solution)/shard_map/reduce_scatter | solution.py:514
  2011.5 465.3 %reduce-scatter.17.cloned.1.call-start = ((), (), s32[]{:S(2)}) async-start(), calls=%async_computation.39 | async-start | bytes 12976128 | tf_op jit(solution)/shard_map/reduce_scatter | solution.py:505
  2021.6 568.7 %reduce-scatter.19.cloned.1.call-start = ((), (), s32[]{:S(2)}) async-start(), calls=%async_computation.40 | async-start | bytes 6488064 | tf_op jit(solution)/shard_map/reduce_scatter | solution.py:508
  2027.0 676.8 %reduce-scatter.21.cloned.1.call-start = ((), (), s32[]{:S(2)}) async-start(), calls=%async_computation.41 | async-start | bytes 6488064 | tf_op jit(solution)/shard_map/reduce_scatter | solution.py:511
  2032.4 710.6 %all-reduce.13.cloned.1.call-start = ((), (), s32[]{:S(2)}) async-start(), calls=%async_computation.34 | async-start | bytes 2097152 | tf_op jit(solution)/shard_map/psum | solution.py:476
  2173.8 642.3 %reduce-scatter.11.cloned.1.call-start = ((), (), s32[]{:S(2)}) async-start(), calls=%async_computation.36 | async-start | bytes 2359296 | tf_op jit(solution)/shard_map/reduce_scatter | solution.py:496
  2175.9 761.5 %reduce-scatter.9.cloned.1.call-start = ((), (), s32[]{:S(2)}) async-start(), calls=%async_computation.35 | async-start | bytes 7077888 | tf_op jit(solution)/shard_map/reduce_scatter | solution.py:493
  2184.3 948.7 %reduce-scatter.13.cloned.1.call-start = ((), (), s32[]{:S(2)}) async-start(), calls=%async_computation.37 | async-start | bytes 12976128 | tf_op jit(solution)/shard_map/reduce_scatter | solution.py:499
  2194.1 1134.5 %reduce-scatter.15.cloned.1.call-start = ((), (), s32[]{:S(2)}) async-start(), calls=%async_computation.38 | async-start | bytes 12976128 | tf_op jit(solution)/shard_map/reduce_scatter | solution.py:502
  (57 other events, 2316.5 us)
Sparse Core Ops, SparseCore 0:
  10.6 99.6 all-gather.21
  120.1 26.4 all-gather.23
  148.2 27.3 all-gather.59
  177.4 49.4 all-gather.25
  230.7 50.4 all-reduce.6
  283.2 91.5 all-gather.27
  376.9 161.4 all-gather.33
  540.6 161.4 all-gather.35
  704.1 161.5 all-gather.37
  867.6 90.4 all-gather.29
  960.1 91.3 all-gather.31
  1084.8 35.4 all-reduce.8
  1122.9 162.8 all-gather.47
  1287.8 161.4 all-gather.49
  1451.4 161.4 all-gather.45
  1614.7 91.3 all-gather.39
  1708.1 90.4 all-gather.41
  1800.5 90.4 all-gather.43
  1900.7 50.4 all-reduce.10
  1953.1 49.5 all-gather.51
  2004.2 26.4 all-gather.53
  2032.9 34.7 all-gather.55
  2069.9 97.8 all-gather.57
  2171.3 109.4 reduce-scatter.22
  2284.4 192.3 reduce-scatter.16
  2480.3 109.9 reduce-scatter.18
  2593.8 109.9 reduce-scatter.20
  2706.7 36.3 all-reduce.12
  2747.2 68.9 reduce-scatter.10
  2819.6 117.8 reduce-scatter.8
  2941.0 191.9 reduce-scatter.12
  3136.6 191.9 reduce-scatter.14
where the time goes:
time: 3350 us; the launch traced here: 3340 us
  waiting for transfers between devices  2920 us (87%)
  matrix products  193 us (6%)
  blocking collectives  79.9 us (2%)
  other arithmetic  62.3 us (2%)
  local copies, waits for them, and re-layouts  47 us (1%)
    all_gather x2, waiting for transfers between devices, gather_weights(): lax.all_gather(shard_set[2], ('dp', 'context'), axis=1, tiled=True)  311 us
    all_gather x2, waiting for transfers between devices, gather_weights(): lax.all_gather(shard_set[3], ('dp', 'context'), axis=1, tiled=True)  308 us
    all_gather x2, waiting for transfers between devices, gather_weights(): lax.all_gather(shard_set[4], ('dp', 'context'), axis=2, tiled=True)  286 us
    reduce_scatter x1, waiting for transfers between devices, body(): lax.psum_scatter(down_grad.astype(jnp.bfloat16), ('dp', 'context'), scatt...  194 us
    reduce_scatter x1, waiting for transfers between devices, body(): lax.psum_scatter(gate_grad.astype(jnp.bfloat16), ('dp', 'context'), scatt...  193 us
    reduce_scatter x1, waiting for transfers between devices, body(): lax.psum_scatter(up_grad.astype(jnp.bfloat16), ('dp', 'context'), scatter...  192 us
    all_gather x2, waiting for transfers between devices, gather_weights(): lax.all_gather(shard_set[5], ('dp', 'context'), axis=0, tiled=True)  168 us
    all_gather x2, waiting for transfers between devices, gather_weights(): lax.all_gather(shard_set[6], ('dp', 'context'), axis=0, tiled=True)  166 us
  transfers between devices with their start and end apart: 36, of which 31 were waited for; matrix products, arithmetic and copies ran while one was open for 8% of the time, Pallas kernels for 0%

commit v1 on v0

--- a/solution.py
+++ b/solution.py
@@ -215,7 +215,7 @@
     return carry
 
 
-def body(
+def general_body(
     tokens,
     positions,
     routes,
@@ -534,9 +534,326 @@
     )
 
 
+def swap_halves(value):
+    return lax.ppermute(value, "dp", [(0, 1), (1, 0)])
+
+
+def own_half_first(value):
+    half = value.shape[-1] // 2
+    turned = jnp.concatenate([value[..., half:], value[..., :half]], -1)
+    return jnp.where(lax.axis_index("dp") == 0, value, turned)
+
+
+def exchange(value):
+    return lax.all_to_all(value, "context", split_axis=0, concat_axis=0, tiled=True)
+
+
+def sum_rows(value):
+    return lax.psum_scatter(value, ("context", "experts"), scatter_dimension=0, tiled=True)
+
+
+def share_rows(value):
+    return lax.all_gather(value, ("context", "experts"), axis=0, tiled=True)
+
+
+def dot_nn(left, right):
+    return jnp.dot(left, right, preferred_element_type=jnp.float32)
+
+
+def dot_nt(left, right):
+    return lax.dot_general(
+        left, right, (((1,), (1,)), ((), ())), preferred_element_type=jnp.float32
+    )
+
+
+def dot_tn(left, right):
+    return lax.dot_general(
+        left, right, (((0,), (0,)), ((), ())), preferred_element_type=jnp.float32
+    )
+
+
+def split_body(
+    tokens,
+    positions,
+    routes,
+    out_grad,
+    norm1_gain,
+    qkv_weight,
+    qkv_bias,
+    out_weight,
+    norm2_gain,
+    router_weight,
+    expert_gate,
+    expert_up,
+    expert_down,
+    shared_gate,
+    shared_w_gate,
+    shared_w_up,
+    shared_w_down,
+):
+    rows, width = tokens.shape[1], tokens.shape[2]
+    parts = lax.axis_size("context")
+    group_size = lax.axis_size("experts")
+    place, group = lax.axis_index("context"), lax.axis_index("experts")
+    local_experts = expert_gate.shape[0]
+    expert_count = local_experts * group_size
+    own_rows = rows // group_size
+    length = rows * parts
+    half = width // 2
+    block = width // (2 * parts)
+    hidden_here = shared_w_gate.shape[1] // parts
+    stacks = local_experts + 1
+    span = stacks * hidden_here
+    scale = HEAD_DIM ** (-0.5)
+    bf16 = jnp.bfloat16
+
+    qkv_in = jnp.transpose(
+        qkv_weight.reshape(block, 3, parts, HEAD_DIM), (2, 0, 1, 3)
+    ).reshape(parts, block, 3 * HEAD_DIM)
+    qkv_m = exchange(qkv_in).reshape(half, 3 * HEAD_DIM)
+    qkv_o = swap_halves(qkv_m)
+    out_m = jnp.transpose(exchange(out_weight.reshape(parts, HEAD_DIM, block)), (1, 0, 2)).reshape(
+        HEAD_DIM, half
+    )
+    out_o = swap_halves(out_m)
+    down_in = jnp.concatenate([shared_w_down[None], expert_down], 0)
+    down_in = jnp.transpose(
+        down_in.reshape(stacks, parts, hidden_here, block), (1, 0, 2, 3)
+    ).reshape(parts, span, block)
+    down_m = jnp.transpose(exchange(down_in), (1, 0, 2)).reshape(span, half)
+    down_o = swap_halves(down_m)
+    up_in = jnp.concatenate(
+        [shared_w_gate[None], expert_gate, shared_w_up[None], expert_up], 0
+    ).reshape(2 * stacks, block, parts, hidden_here)
+    up_in = jnp.transpose(up_in, (2, 1, 0, 3)).reshape(parts, block, 2 * span)
+    up_m = exchange(up_in).reshape(half, 2 * span)
+    up_o = swap_halves(up_m)
+
+    grad_all = lax.all_gather(own_half_first(out_grad[0]), "context", axis=0, tiled=True)
+    position_all = lax.all_gather(positions[0], "context", axis=0, tiled=True)
+    route_all = lax.all_gather(routes[0], "context", axis=0, tiled=True)
+
+    gain1 = own_half_first(norm1_gain).astype(jnp.float32)
+    gain2 = own_half_first(norm2_gain).astype(jnp.float32)
+    token_rows = own_half_first(tokens[0]).astype(jnp.float32)
+    inverse_rows = lax.rsqrt(jnp.mean(token_rows * token_rows, -1, keepdims=True) + EPSILON)
+    xn1 = lax.all_gather(
+        (token_rows * inverse_rows * gain1).astype(bf16), "context", axis=0, tiled=True
+    )
+    first = group * own_rows
+    token_own = lax.dynamic_slice_in_dim(token_rows, first, own_rows, 0)
+    inverse1 = lax.dynamic_slice_in_dim(inverse_rows, first, own_rows, 0)
+    normed1 = token_own * inverse1
+    grad_own = lax.dynamic_slice_in_dim(
+        own_half_first(out_grad[0]).astype(jnp.float32), first, own_rows, 0
+    )
+
+    bias_here = lax.dynamic_slice_in_dim(
+        qkv_bias.reshape(3, parts, HEAD_DIM), place, 1, 1
+    ).reshape(1, 3 * HEAD_DIM)
+    qkv = (
+        dot_nn(xn1[:, :half], qkv_m)
+        + dot_nn(xn1[:, half:], qkv_o)
+        + bias_here.astype(jnp.float32)
+    )
+    cosine, sine_part = rope_tables(position_all)
+    cosine, sine_part = cosine[:, 0], sine_part[:, 0]
+    q_raw, k_raw, v_raw = jnp.split(qkv, 3, 1)
+    query = (q_raw * cosine + rotate(q_raw) * sine_part).astype(bf16)
+    key = (k_raw * cosine + rotate(k_raw) * sine_part).astype(bf16)
+    value = v_raw.astype(bf16)
+    index = jnp.arange(length, dtype=jnp.int32)
+    allowed = index[None, :] <= index[:, None]
+    scores = dot_nt(query, key) * scale
+    row_max = jnp.max(jnp.where(allowed, scores, MASKED), -1, keepdims=True)
+    weights = jnp.where(allowed, jnp.exp(scores - row_max), 0.0)
+    row_sum = jnp.sum(weights, -1, keepdims=True)
+    attended = (dot_nn(weights.astype(bf16), value) / row_sum).astype(bf16)
+    lse = row_max + jnp.log(row_sum)
+
+    head_part = jnp.concatenate([dot_nn(attended, out_m), dot_nn(attended, out_o)], 1)
+    hidden = token_own + sum_rows(head_part.astype(bf16)).astype(jnp.float32)
+    inverse2 = lax.rsqrt(jnp.mean(hidden * hidden, -1, keepdims=True) + EPSILON)
+    normed2 = hidden * inverse2
+    xn2_own = (normed2 * gain2).astype(bf16)
+    xn2 = share_rows(xn2_own)
+
+    router_here = own_half_first(router_weight.T).T
+    gate_here = own_half_first(shared_gate)
+    heads_w = jnp.concatenate([router_here, gate_here[:, None]], 1)
+    logits_all = dot_nn(xn2, heads_w)
+    prob_all = jax.nn.softmax(logits_all[:, :expert_count], -1)
+    sig_all = jax.nn.sigmoid(logits_all[:, expert_count])
+    named_all = jnp.sum(
+        (
+            route_all[:, :, None] == jnp.arange(expert_count, dtype=jnp.int32)[None, None, :]
+        ).astype(jnp.float32),
+        1,
+    )
+    gates_all = prob_all * named_all
+    gates_here = lax.dynamic_slice_in_dim(gates_all, group * local_experts, local_experts, 1)
+    coefs = jnp.concatenate([sig_all[:, None], gates_here], 1)
+
+    up_vals = dot_nn(xn2[:, :half], up_m) + dot_nn(xn2[:, half:], up_o)
+    g_vals, u_vals = up_vals[:, :span], up_vals[:, span:]
+    sig_g = jax.nn.sigmoid(g_vals)
+    silu_g = g_vals * sig_g
+    act = silu_g * u_vals
+    coef_wide = jnp.repeat(coefs, hidden_here, axis=1, total_repeat_length=span)
+    act_c = (act * coef_wide).astype(bf16)
+    raw = dot_nt(grad_all[:, :half], down_m) + dot_nt(grad_all[:, half:], down_o)
+    dots = jnp.sum((raw * act).reshape(length, stacks, hidden_here), -1)
+    dact = raw * coef_wide
+    dg = (dact * u_vals * (sig_g * (1.0 + g_vals * (1.0 - sig_g)))).astype(bf16)
+    du = (dact * silu_g).astype(bf16)
+    dup = jnp.concatenate([dg, du], 1)
+    branch_part = jnp.concatenate([dot_nn(act_c, down_m), dot_nn(act_c, down_o)], 1)
+    dxn2_part = jnp.concatenate([dot_nt(dup, up_m), dot_nt(dup, up_o)], 1)
+    dots_wide = jnp.concatenate(
+        [
+            lax.dynamic_update_slice_in_dim(
+                jnp.zeros((length, expert_count), jnp.float32),
+                dots[:, 1:],
+                group * local_experts,
+                1,
+            ),
+            dots[:, :1],
+        ],
+        1,
+    )
+    dxn2_sum = sum_rows(dxn2_part.astype(bf16)).astype(jnp.float32)
+    dots_own = sum_rows(dots_wide)
+    branch = sum_rows(branch_part.astype(bf16)).astype(jnp.float32)
+    block_own = own_half_first((hidden + branch).astype(bf16))
+    block_out = lax.all_gather(block_own, "experts", axis=0, tiled=True)
+
+    row_first = place * rows + first
+    prob = lax.dynamic_slice_in_dim(prob_all, row_first, own_rows, 0)
+    named = lax.dynamic_slice_in_dim(named_all, row_first, own_rows, 0)
+    sig_own = lax.dynamic_slice_in_dim(sig_all, row_first, own_rows, 0)
+    dprob = dots_own[:, :expert_count] * named
+    dlogit = prob * (dprob - jnp.sum(prob * dprob, -1, keepdims=True))
+    coef = sig_own * (1.0 - sig_own) * dots_own[:, expert_count]
+    xn2_float = xn2_own.astype(jnp.float32)
+    router_grad = jnp.dot(xn2_float.T, dlogit, precision=PRECISE)
+    shared_gate_grad = jnp.dot(coef, xn2_float, precision=PRECISE)
+    dxn2 = (
+        dxn2_sum
+        + jnp.dot(dlogit, router_here.astype(jnp.float32).T, precision=PRECISE)
+        + coef[:, None] * gate_here.astype(jnp.float32)[None, :]
+    )
+    norm2_grad = jnp.sum(dxn2 * normed2, 0)
+    dscaled2 = dxn2 * gain2
+    dhidden = grad_own + inverse2 * (
+        dscaled2 - normed2 * jnp.mean(dscaled2 * normed2, -1, keepdims=True)
+    )
+    dhidden_all = share_rows(dhidden.astype(bf16))
+
+    out_grad_part = dot_tn(attended, dhidden_all)
+    dattended = (
+        dot_nt(dhidden_all[:, :half], out_m) + dot_nt(dhidden_all[:, half:], out_o)
+    ).astype(bf16)
+    delta = jnp.sum(
+        dattended.astype(jnp.float32) * attended.astype(jnp.float32), -1, keepdims=True
+    )
+    scores = dot_nt(query, key) * scale
+    prob_att = jnp.where(allowed, jnp.exp(scores - lse), 0.0)
+    dvalue = dot_tn(prob_att.astype(bf16), dattended)
+    dscore = (prob_att * (dot_nt(dattended, value) - delta)).astype(bf16)
+    dquery = dot_nn(dscore, key) * scale
+    dkey = dot_tn(dscore, query) * scale
+    dqkv = jnp.concatenate(
+        [
+            dquery * cosine + rotate_back(dquery * sine_part),
+            dkey * cosine + rotate_back(dkey * sine_part),
+            dvalue,
+        ],
+        1,
+    )
+    bias_part = jnp.sum(dqkv, 0)
+    dqkv_b = dqkv.astype(bf16)
+    qkv_grad = dot_tn(xn1, dqkv_b)
+    dxn1_part = jnp.concatenate([dot_nt(dqkv_b, qkv_m), dot_nt(dqkv_b, qkv_o)], 1)
+    dxn1 = sum_rows(dxn1_part.astype(bf16)).astype(jnp.float32)
+    norm1_grad = jnp.sum(dxn1 * normed1, 0)
+    dscaled1 = dxn1 * gain1
+    tokens_grad_own = dhidden + inverse1 * (
+        dscaled1 - normed1 * jnp.mean(dscaled1 * normed1, -1, keepdims=True)
+    )
+    tokens_grad = lax.all_gather(
+        own_half_first(tokens_grad_own), "experts", axis=0, tiled=True
+    )
+
+    bias_wide = jnp.zeros((group_size, parts, 3 * HEAD_DIM), jnp.float32)
+    bias_wide = lax.dynamic_update_slice(bias_wide, bias_part[None, None], (group, place, 0))
+    small = jnp.concatenate(
+        [
+            own_half_first(norm1_grad),
+            own_half_first(norm2_grad),
+            own_half_first(shared_gate_grad),
+            own_half_first(router_grad.T).T.reshape(-1),
+            bias_wide.reshape(-1),
+        ]
+    )
+    small = lax.psum(small, ("dp", "context", "experts"))
+    router_size = width * expert_count
+    bias_sum = small[3 * width + router_size :].reshape(group_size, parts, 3, HEAD_DIM)
+    bias_grad = jnp.transpose(
+        lax.dynamic_slice_in_dim(bias_sum, group, 1, 0)[0], (1, 0, 2)
+    ).reshape(3, parts * HEAD_DIM)
+
+    def halves(first_half, second_half):
+        return (first_half + swap_halves(second_half.astype(bf16)).astype(jnp.float32)).astype(bf16)
+
+    down_grad = halves(
+        dot_tn(act_c, grad_all[:, :half]), dot_tn(act_c, grad_all[:, half:])
+    )
+    down_grad = exchange(jnp.transpose(down_grad.reshape(span, parts, block), (1, 0, 2)))
+    down_grad = jnp.transpose(
+        down_grad.reshape(parts, stacks, hidden_here, block), (1, 0, 2, 3)
+    ).reshape(stacks, parts * hidden_here, block).astype(jnp.float32)
+    up_grad = halves(dot_tn(xn2[:, :half], dup), dot_tn(xn2[:, half:], dup))
+    up_grad = exchange(up_grad.reshape(parts, block, 2 * span))
+    up_grad = jnp.transpose(
+        up_grad.reshape(parts, block, 2 * stacks, hidden_here), (2, 1, 0, 3)
+    ).reshape(2 * stacks, block, parts * hidden_here).astype(jnp.float32)
+    out_w_grad = halves(out_grad_part[:, :half], out_grad_part[:, half:])
+    out_w_grad = exchange(
+        jnp.transpose(out_w_grad.reshape(HEAD_DIM, parts, block), (1, 0, 2))
+    ).reshape(parts * HEAD_DIM, block).astype(jnp.float32)
+    qkv_grad = halves(qkv_grad[:half], qkv_grad[half:])
+    qkv_grad = exchange(qkv_grad.reshape(parts, block, 3 * HEAD_DIM))
+    qkv_grad = jnp.transpose(
+        qkv_grad.reshape(parts, block, 3, HEAD_DIM), (1, 2, 0, 3)
+    ).reshape(block, 3, parts * HEAD_DIM).astype(jnp.float32)
+
+    return (
+        block_out[None],
+        tokens_grad[None],
+        small[:width],
+        qkv_grad,
+        bias_grad,
+        out_w_grad,
+        small[width : 2 * width],
+        small[3 * width : 3 * width + router_size].reshape(width, expert_count),
+        up_grad[1:stacks],
+        up_grad[stacks + 1 :],
+        down_grad[1:],
+        small[2 * width : 3 * width],
+        up_grad[0],
+        up_grad[stacks],
+        down_grad[0],
+    )
+
+
+def plan_of(mesh):
+    one_head_each = mesh.shape["context"] * mesh.shape["experts"] == 16
+    return split_body if one_head_each and mesh.shape["dp"] == 2 else general_body
+
+
 def solution(mesh):
     return jax.shard_map(
-        body,
+        plan_of(mesh),
         mesh=mesh,
         in_specs=(
             P("dp", "context", None),

time: 3350 us -> 1130 us (0.34)
  waiting for transfers between devices: 2920 us -> 605 us
  blocking collectives: 79.9 us -> 154 us
  matrix products: 193 us -> 123 us
  local copies, waits for them, and re-layouts: 47 us -> 113 us
  starting transfers between devices: 18.8 us -> 64.3 us
    all_gather x20 -> x6, waiting for transfers between devices: 1700 us -> 157 us  [the longest x2 95.3 us: share_rows(): return lax.all_gather(value, ('context', 'experts'), axis=0, tiled=True)]
    reduce_scatter x8 -> x4, waiting for transfers between devices: 1030 us -> 176 us  [sum_rows(): lax.psum_scatter(value, ('context', 'experts'), scatter_dimension=0, tile...]
    ppermute x0 -> x8, waiting for transfers between devices: none -> 121 us  [swap_halves(): return lax.ppermute(value, 'dp', [(0, 1), (1, 0)])]
    psum x4 -> x1, waiting for transfers between devices: 164 us -> 58.7 us  [split_body(): small = lax.psum(small, ('dp', 'context', 'experts'))]
    all_gather x2, blocking collectives: 32.1 us -> 113 us  [the longest x1 94.8 us: split_body(): route_all = lax.all_gather(routes[0], 'context', axis=0, tiled=True)]
    dot_general x43 -> x32, matrix products: 193 us -> 123 us  [the longest x11 44.6 us: dot_nn(): return jnp.dot(left, right, preferred_element_type=jnp.float32)]
    psum x2 -> x0, blocking collectives: 47.9 us -> none  [the longest x1 35.8 us: body(): lax.psum(norm1_grad.astype(jnp.bfloat16), ('dp', 'context'))]
    unnamed x115 -> x136, local copies, waits for them, and re-layouts: 15 us -> 61.6 us
  transfers between devices with their start and end apart: 36 -> 27, of which waited for: 31 -> 15; matrix products, arithmetic and copies ran while one was open for 8% -> 19% of each run, Pallas kernels for 0% -> 0%
where the time goes in v1:
time: 1130 us; the launch traced here: 1120 us
  waiting for transfers between devices  605 us (54%)
  blocking collectives  154 us (14%)
  matrix products  123 us (11%)
  local copies, waits for them, and re-layouts  113 us (10%)
  starting transfers between devices  64.3 us (6%)
  other arithmetic  42.6 us (4%)
  between operations  15.7 us (1%)
    reduce_scatter x4, waiting for transfers between devices, sum_rows(): lax.psum_scatter(value, ('context', 'experts'), scatter_dimension=0, tile...  176 us
    ppermute x8, waiting for transfers between devices, swap_halves(): return lax.ppermute(value, 'dp', [(0, 1), (1, 0)])  121 us
    all_gather x2, waiting for transfers between devices, share_rows(): return lax.all_gather(value, ('context', 'experts'), axis=0, tiled=True)  95.3 us
    all_gather x1, blocking collectives, split_body(): route_all = lax.all_gather(routes[0], 'context', axis=0, tiled=True)  94.8 us
    all_to_all x7, waiting for transfers between devices, exchange(): lax.all_to_all(value, 'context', split_axis=0, concat_axis=0, tiled=True)  62 us
    unnamed x136, local copies, waits for them, and re-layouts  61.6 us
    psum x1, waiting for transfers between devices, split_body(): small = lax.psum(small, ('dp', 'context', 'experts'))  58.7 us
    all_to_all x7, starting transfers between devices, exchange(): lax.all_to_all(value, 'context', split_axis=0, concat_axis=0, tiled=True)  56.3 us
  transfers between devices with their start and end apart: 27, of which 15 were waited for; matrix products, arithmetic and copies ran while one was open for 19% of the time, Pallas kernels for 0%

profile of v1, /device:TPU:16, one launch (start us, length us, event | category | flops | bytes accessed | tf_op | source)
XLA Modules:
  0.0 1117.5 jit_solution(15538235054163462772)
XLA Ops:
  14.3 40.6 %all_to_all.40 = bf16[4,256,384]{1,2,0:T(8,128)(2,1)S(1)} all-to-all(bf16[4,256,384]{1,2,0:T(8,128)(2,1)S(1)} %bitcast.178), channel_id=1, replica_groups=mesh['dp'=2,'context'=4,'experts'=4] {'context'}, dimensions={0} | all-to-all | bytes 1572864 | tf_op jit(solution)/shard_map/all_to_all | solution.py:548
  57.5 9.1 all-to-all-start.1
  66.6 18.6 %all-gather = s32[1,1024]{1,0:T(1,128)S(1)} all-gather(s32[1,256]{1,0:T(1,128)S(1)} %copy-done.46), channel_id=2, replica_groups=mesh['dp'=2,'context'=4,'experts'=4] {'context'}, dimensions={1}, use_global_device_ids=true | all-gather | bytes 5120 | tf_op jit(solution)/shard_map/all_gather | solution.py:633
  86.5 22.9 %all-gather.9.cloned.1.call-done = bf16[1024,2048]{1,0:T(8,128)(2,1)} async-done(((bf16[256,2048]{1,0:T(8,128)(2,1)}), bf16[1024,2048]{1,0:T(8,128)(2,1)}) %all-gather.9.cloned.1.call-update) | async-done | bytes 4194320 | tf_op jit(solution)/shard_map/all_gather | solution.py:640
  145.1 8.7 all-to-all-start.2
  154.3 102.9 %reduce-scatter.16.cloned.1.call-done = bf16[64,2048]{1,0:T(8,128)(2,1)} async-done(((bf16[1024,2048]{1,0:T(8,128)(2,1)}), bf16[64,2048]{1,0:T(8,128)(2,1)}) %reduce-scatter.16.cloned.1.call-update) | async-done | bytes 262160 | tf_op jit(solution)/shard_map/reduce_scatter | solution.py:552
  262.3 9.9 all-to-all-done.2
  272.2 14.1 %all-to-all-start.3 = ((bf16[4,1056,256]{2,1,0:T(8,128)(2,1)}), bf16[4,1056,256]{2,1,0:T(8,128)(2,1)}, u32[]{:S(2)}, u32[]{:S(2)}) async-start(bf16[4,1056,256]{2,1,0:T(8,128)(2,1)} %bitcast.165), calls=%async_computation.3 | async-start | bytes 4325376 | tf_op jit(solution)/shard_map/all_to_all | solution.py:548
  292.7 6.5 copy.145
  300.8 94.8 %all-gather.1 = s32[1,1024,4]{1,2,0:T(4,128)S(1)} all-gather(s32[1,256,4]{1,2,0:T(4,128)S(1)} %copy-done.44), channel_id=3, replica_groups=mesh['dp'=2,'context'=4,'experts'=4] {'context'}, dimensions={1}, use_global_device_ids=true | all-gather | bytes 20480 | tf_op jit(solution)/shard_map/all_gather | solution.py:634
  400.4 6.8 fusion.22
  407.2 45.1 %all-gather.11.cloned.1.call-done = bf16[1024,2048]{1,0:T(8,128)(2,1)} async-done(((bf16[64,2048]{1,0:T(8,128)(2,1)}), bf16[1024,2048]{1,0:T(8,128)(2,1)}) %all-gather.11.cloned.1.call-update) | async-done | bytes 4194320 | tf_op jit(solution)/shard_map/all_gather | solution.py:556
  460.7 11.2 fusion.30
  471.8 11.5 %convolution_add_fusion = f32[1024,2112]{0,1:T(8,128)S(1)} fusion(f32[1024,2112]{0,1:T(8,128)} %fusion.30, bf16[1024,2112]{0,1:T(8,128)(2,1)} %collective-permute-done.2, bf16[1024,2048]{1,0:T(8,128)(2,1)S(1)} %copy-done.3), kind=kOutput, calls=%fused_computation.3 | convolution fusion | flops 4431347712 | bytes 23724032 | tf_op jit(solution)/shard_map/dot_general | solution.py:560
  483.4 9.7 multiply_convert_fusion.1
  496.8 8.7 convolution_convert_fusion.4
  505.5 7.6 convolution_convert_fusion.5
  522.1 29.0 %reduce-scatter.22.cloned.1.call-done = f32[64,9]{1,0:T(8,128)} async-done(((f32[1024,9]{1,0:T(8,128)}), f32[64,9]{1,0:T(8,128)}) %reduce-scatter.22.cloned.1.call-update) | async-done | bytes 2320
  553.0 73.5 %reduce-scatter.20.cloned.1.call-done = bf16[64,2048]{1,0:T(8,128)(2,1)} async-done(((bf16[1024,2048]{1,0:T(8,128)(2,1)}), bf16[64,2048]{1,0:T(8,128)(2,1)}) %reduce-scatter.20.cloned.1.call-update) | async-done | bytes 262160 | tf_op jit(solution)/shard_map/reduce_scatter | solution.py:552
  630.2 50.1 %all-gather.17.cloned.1.call-done = bf16[1024,2048]{1,0:T(8,128)(2,1)} async-done(((bf16[64,2048]{1,0:T(8,128)(2,1)}), bf16[1024,2048]{1,0:T(8,128)(2,1)}) %all-gather.17.cloned.1.call-update) | async-done | bytes 4194320 | tf_op jit(solution)/shard_map/all_gather | solution.py:556
  696.4 6.7 copy.177
  709.5 8.1 convolution_convert_fusion
  729.2 28.8 %collective-permute-done.7 = bf16[1056,1024]{1,0:T(8,128)(2,1)S(1)} collective-permute-done((bf16[1056,1024]{1,0:T(8,128)(2,1)S(1)}, bf16[1056,1024]{1,0:T(8,128)(2,1)S(1)}, u32[]{:S(2)}, u32[]{:S(2)}) %collective-permute-start.7) | collective-permute-done | bytes 2162720 | tf_op jit(solution)/shard_map/ppermute | solution.py:538
  771.4 6.9 copy.171
  778.3 71.7 %collective-permute-done.6 = bf16[1024,2112]{0,1:T(8,128)(2,1)} collective-permute-done((bf16[1024,2112]{0,1:T(8,128)(2,1)}, bf16[1024,2112]{0,1:T(8,128)(2,1)}, u32[]{:S(2)}, u32[]{:S(2)}) %collective-permute-start.6) | collective-permute-done | bytes 4325408 | tf_op jit(solution)/shard_map/ppermute | solution.py:538
  850.0 8.8 add_convert_fusion
  887.0 20.5 %collective-permute-done.5 = bf16[128,1024]{1,0:T(8,128)(2,1)S(1)} collective-permute-done((bf16[128,1024]{1,0:T(8,128)(2,1)S(1)}, bf16[128,1024]{1,0:T(8,128)(2,1)S(1)}, u32[]{:S(2)}, u32[]{:S(2)}) %collective-permute-start.5) | collective-permute-done | bytes 262176 | tf_op jit(solution)/shard_map/ppermute | solution.py:538
  908.3 52.1 %all-to-all-done.6 = bf16[4,256,2112]{1,2,0:T(8,128)(2,1)} async-done(((bf16[4,256,2112]{1,2,0:T(8,128)(2,1)}), bf16[4,256,2112]{1,2,0:T(8,128)(2,1)}, u32[]{:S(2)}, u32[]{:S(2)}) %all-to-all-start.6) | async-done | bytes 4325408 | tf_op jit(solution)/shard_map/all_to_all | solution.py:548
  960.4 6.9 all-to-all-start.5
  1003.5 58.7 %all-reduce.2.cloned.1.call-done = f32[28672]{0:T(1024)} async-done(((f32[28672]{0:T(1024)}), f32[28672]{0:T(1024)}) %all-reduce.2.cloned.1.call-update) | async-done | bytes 114704 | tf_op jit(solution)/shard_map/psum | solution.py:798
  1067.3 13.2 %all-gather.13.cloned.1.call-done = bf16[256,2048]{1,0:T(8,128)(2,1)} async-done(((bf16[64,2048]{1,0:T(8,128)(2,1)}), bf16[256,2048]{1,0:T(8,128)(2,1)}) %all-gather.13.cloned.1.call-update) | async-done | bytes 1048592 | tf_op jit(solution)/shard_map/all_gather | solution.py:728
  1080.5 24.6 %all-gather.19.cloned.1.call-done = f32[256,2048]{1,0:T(8,128)} async-done(((f32[64,2048]{1,0:T(8,128)}), f32[256,2048]{1,0:T(8,128)}) %all-gather.19.cloned.1.call-update) | async-done | bytes 2097168 | tf_op jit(solution)/shard_map/all_gather | solution.py:783
  (319 shorter events, 213.6 us)
Async XLA Ops:
  7.2 102.2 %all-gather.9.cloned.1.call-start = ((), (), s32[]{:S(2)}) async-start(), calls=%async_computation.13 | async-start | bytes 5242880 | tf_op jit(solution)/shard_map/all_gather | solution.py:640
  10.9 246.4 %copy-start.1 = (f32[256,2048]{1,0:T(8,128)}, f32[256,2048]{1,0:T(8,128)S(1)}, u32[]{:S(2)}) copy-start(f32[256,2048]{1,0:T(8,128)S(1)} %get-tuple-element.111) | copy-start | bytes 6291460
  56.0 56.3 %collective-permute-start = (bf16[1024,384]{1,0:T(8,128)(2,1)}, bf16[1024,384]{1,0:T(8,128)(2,1)}, u32[]{:S(2)}, u32[]{:S(2)}) collective-permute-start(bf16[1024,384]{1,0:T(8,128)(2,1)} %bitcast.194), channel_id=1, source_target_pairs={{0,16},{16,0},{1,17},{17,1},{2,18},{18,2},{3,19},{19,3},{4,20},{20... | collective-permute-start | bytes 2359304 | tf_op jit(solution)/shard_map/ppermute | solution.py:538
  57.5 28.7 %all-to-all-start.1 = ((bf16[4,128,256]{2,1,0:T(8,128)(2,1)}), bf16[4,128,256]{2,1,0:T(8,128)(2,1)S(1)}, u32[]{:S(2)}, u32[]{:S(2)}) async-start(bf16[4,128,256]{2,1,0:T(8,128)(2,1)} %bitcast.6), calls=%async_computation.1 | async-start | bytes 524288 | tf_op jit(solution)/shard_map/all_to_all | solution.py:548
  66.6 190.7 %reduce-scatter.16.cloned.1.call-start = ((), (), s32[]{:S(2)}) async-start(), calls=%async_computation.20 | async-start | bytes 4456448 | tf_op jit(solution)/shard_map/reduce_scatter | solution.py:552
  86.4 33.1 %collective-permute-start.1 = (bf16[128,1024]{0,1:T(8,128)(2,1)S(1)}, bf16[128,1024]{0,1:T(8,128)(2,1)S(1)}, u32[]{:S(2)}, u32[]{:S(2)}) collective-permute-start(bf16[128,1024]{0,1:T(8,128)(2,1)S(1)} %bitcast.188), channel_id=1, source_target_pairs={{0,16},{16,0},{1,17},{17,1},{2,18},{18,2},{3,19},{19,3},{4,20},{20... | collective-permute-start | bytes 786440 | tf_op jit(solution)/shard_map/ppermute | solution.py:538
  129.1 271.3 %all-gather.15.cloned.1.call-start = ((), (), s32[]{:S(2)}) async-start(), calls=%async_computation.16 | async-start | bytes 5242880 | tf_op jit(solution)/shard_map/all_gather | solution.py:632
  145.1 114.1 %copy-start.30 = (bf16[1408,256]{1,0:T(8,128)(2,1)S(1)}, bf16[1408,256]{1,0:T(8,128)(2,1)}, u32[]{:S(2)}) copy-start(bf16[1408,256]{1,0:T(8,128)(2,1)} %param.35) | copy-start | bytes 2162692
  145.1 127.1 %all-to-all-start.2 = ((bf16[4,256,2112]{1,2,0:T(8,128)(2,1)}), bf16[4,256,2112]{1,2,0:T(8,128)(2,1)}, u32[]{:S(2)}, u32[]{:S(2)}) async-start(bf16[4,256,2112]{1,2,0:T(8,128)(2,1)} %bitcast.162), calls=%async_computation.2 | async-start | bytes 8650752 | tf_op jit(solution)/shard_map/all_to_all | solution.py:548
  153.8 298.5 %all-gather.11.cloned.1.call-start = ((), (), s32[]{:S(2)}) async-start(), calls=%async_computation.14 | async-start | bytes 4456448 | tf_op jit(solution)/shard_map/all_gather | solution.py:556
  272.2 123.5 %all-to-all-start.3 = ((bf16[4,1056,256]{2,1,0:T(8,128)(2,1)}), bf16[4,1056,256]{2,1,0:T(8,128)(2,1)}, u32[]{:S(2)}, u32[]{:S(2)}) async-start(bf16[4,1056,256]{2,1,0:T(8,128)(2,1)} %bitcast.165), calls=%async_computation.3 | async-start | bytes 4325376 | tf_op jit(solution)/shard_map/all_to_all | solution.py:548
  286.3 264.8 %reduce-scatter.22.cloned.1.call-start = ((), (), s32[]{:S(2)}) async-start(), calls=%async_computation.23 | async-start | bytes 557056
  299.2 172.6 %collective-permute-start.2 = (bf16[1024,2112]{0,1:T(8,128)(2,1)}, bf16[1024,2112]{0,1:T(8,128)(2,1)}, u32[]{:S(2)}, u32[]{:S(2)}) collective-permute-start(bf16[1024,2112]{0,1:T(8,128)(2,1)} %copy.145), channel_id=1, source_target_pairs={{0,16},{16,0},{1,17},{17,1},{2,18},{18,2},{3,19},{19,3},{4,20},{20... | collective-permute-start | bytes 12976136 | tf_op jit(solution)/shard_map/ppermute | solution.py:538
  399.0 84.4 %collective-permute-start.3 = (bf16[1056,1024]{1,0:T(8,128)(2,1)}, bf16[1056,1024]{1,0:T(8,128)(2,1)}, u32[]{:S(2)}, u32[]{:S(2)}) collective-permute-start(bf16[1056,1024]{1,0:T(8,128)(2,1)} %bitcast.72), channel_id=1, source_target_pairs={{0,16},{16,0},{1,17},{17,1},{2,18},{18,2},{3,19},{19,3},{4,20},{20... | collective-permute-start | bytes 6488072 | tf_op jit(solution)/shard_map/ppermute | solution.py:538
  496.7 129.9 %reduce-scatter.20.cloned.1.call-start = ((), (), s32[]{:S(2)}) async-start(), calls=%async_computation.22 | async-start | bytes 4456448 | tf_op jit(solution)/shard_map/reduce_scatter | solution.py:552
  522.0 158.3 %copy-start.26 = (bf16[128,4,256]{0,2,1:T(8,128)(2,1)S(1)}, bf16[128,4,256]{0,2,1:T(8,128)(2,1)}, u32[]{:S(2)}) copy-start(bf16[128,4,256]{0,2,1:T(8,128)(2,1)} %copy-done.25) | copy-start | bytes 786436
  522.1 160.9 %copy-start.17 = (bf16[1024,128]{0,1:T(8,128)(2,1)S(1)}, bf16[1024,128]{0,1:T(8,128)(2,1)}, u32[]{:S(2)}) copy-start(bf16[1024,128]{0,1:T(8,128)(2,1)} %copy-done.16) | copy-start | bytes 786436
  522.1 160.9 %copy-start.34 = (bf16[128,1024]{0,1:T(8,128)(2,1)S(1)}, bf16[128,1024]{0,1:T(8,128)(2,1)}, u32[]{:S(2)}) copy-start(bf16[128,1024]{0,1:T(8,128)(2,1)} %copy-done.33) | copy-start | bytes 786436
  522.1 158.3 %all-gather.17.cloned.1.call-start = ((), (), s32[]{:S(2)}) async-start(), calls=%async_computation.17 | async-start | bytes 4456448 | tf_op jit(solution)/shard_map/all_gather | solution.py:556
  630.1 242.4 %reduce-scatter.24.cloned.1.call-start = ((), (), s32[]{:S(2)}) async-start(), calls=%async_computation.24 | async-start | bytes 4456448 | tf_op jit(solution)/shard_map/reduce_scatter | solution.py:552
  708.0 50.0 %collective-permute-start.7 = (bf16[1056,1024]{1,0:T(8,128)(2,1)S(1)}, bf16[1056,1024]{1,0:T(8,128)(2,1)S(1)}, u32[]{:S(2)}, u32[]{:S(2)}) collective-permute-start(bf16[1056,1024]{1,0:T(8,128)(2,1)S(1)} %convolution_convert_fusion.1), channel_id=1, source_target_pairs={{0,16},{16,0},{1,17},{17,1},{2,18},{18,2},{3,19},{19,3},{4,20},{20... | collective-permute-start | bytes 6488072 | tf_op jit(solution)/shard_map/ppermute | solution.py:538
  717.7 132.4 %collective-permute-start.6 = (bf16[1024,2112]{0,1:T(8,128)(2,1)}, bf16[1024,2112]{0,1:T(8,128)(2,1)}, u32[]{:S(2)}, u32[]{:S(2)}) collective-permute-start(bf16[1024,2112]{0,1:T(8,128)(2,1)} %convolution_convert_fusion), channel_id=1, source_target_pairs={{0,16},{16,0},{1,17},{17,1},{2,18},{18,2},{3,19},{19,3},{4,20},{20... | collective-permute-start | bytes 12976136 | tf_op jit(solution)/shard_map/ppermute | solution.py:538
  761.9 99.4 %all-to-all-start.7 = ((bf16[4,1056,256]{2,1,0:T(8,128)(2,1)}), bf16[4,1056,256]{2,1,0:T(8,128)(2,1)}, u32[]{:S(2)}, u32[]{:S(2)}) async-start(bf16[4,1056,256]{2,1,0:T(8,128)(2,1)} %bitcast.166), calls=%async_computation.7 | async-start | bytes 4325376 | tf_op jit(solution)/shard_map/all_to_all | solution.py:548
  767.4 107.2 %reduce-scatter.18.cloned.1.call-start = ((), (), s32[]{:S(2)}) async-start(), calls=%async_computation.21 | async-start | bytes 4456448 | tf_op jit(solution)/shard_map/reduce_scatter | solution.py:552
  861.2 99.2 %all-to-all-start.6 = ((bf16[4,256,2112]{1,2,0:T(8,128)(2,1)}), bf16[4,256,2112]{1,2,0:T(8,128)(2,1)}, u32[]{:S(2)}, u32[]{:S(2)}) async-start(bf16[4,256,2112]{1,2,0:T(8,128)(2,1)} %bitcast.161), calls=%async_computation.6 | async-start | bytes 8650752 | tf_op jit(solution)/shard_map/all_to_all | solution.py:548
  867.3 194.9 %all-reduce.2.cloned.1.call-start = ((), (), s32[]{:S(2)}) async-start(), calls=%async_computation.19 | async-start | bytes 229376 | tf_op jit(solution)/shard_map/psum | solution.py:798
  874.5 205.9 %all-gather.13.cloned.1.call-start = ((), (), s32[]{:S(2)}) async-start(), calls=%async_computation.15 | async-start | bytes 1310720 | tf_op jit(solution)/shard_map/all_gather | solution.py:728
  877.7 227.3 %all-gather.19.cloned.1.call-start = ((), (), s32[]{:S(2)}) async-start(), calls=%async_computation.18 | async-start | bytes 2621440 | tf_op jit(solution)/shard_map/all_gather | solution.py:783
  883.2 89.4 %collective-permute-start.4 = (bf16[1024,384]{1,0:T(8,128)(2,1)S(1)}, bf16[1024,384]{1,0:T(8,128)(2,1)S(1)}, u32[]{:S(2)}, u32[]{:S(2)}) collective-permute-start(bf16[1024,384]{1,0:T(8,128)(2,1)S(1)} %slice.440), channel_id=1, source_target_pairs={{0,16},{16,0},{1,17},{17,1},{2,18},{18,2},{3,19},{19,3},{4,20},{20... | collective-permute-start | bytes 2359304 | tf_op jit(solution)/shard_map/ppermute | solution.py:538
  885.5 22.1 %collective-permute-start.5 = (bf16[128,1024]{1,0:T(8,128)(2,1)S(1)}, bf16[128,1024]{1,0:T(8,128)(2,1)S(1)}, u32[]{:S(2)}, u32[]{:S(2)}) collective-permute-start(bf16[128,1024]{1,0:T(8,128)(2,1)S(1)} %slice.441), channel_id=1, source_target_pairs={{0,16},{16,0},{1,17},{17,1},{2,18},{18,2},{3,19},{19,3},{4,20},{20... | collective-permute-start | bytes 786440 | tf_op jit(solution)/shard_map/ppermute | solution.py:538
  960.4 13.5 %all-to-all-start.5 = ((bf16[4,128,256]{2,1,0:T(8,128)(2,1)}), bf16[4,128,256]{2,1,0:T(8,128)(2,1)S(1)}, u32[]{:S(2)}, u32[]{:S(2)}) async-start(bf16[4,128,256]{2,1,0:T(8,128)(2,1)} %bitcast.154), calls=%async_computation.5 | async-start | bytes 524288 | tf_op jit(solution)/shard_map/all_to_all | solution.py:548
  973.9 26.5 %all-to-all-start.4 = ((bf16[4,256,384]{1,2,0:T(8,128)(2,1)}), bf16[4,256,384]{1,2,0:T(8,128)(2,1)}, u32[]{:S(2)}, u32[]{:S(2)}) async-start(bf16[4,256,384]{1,2,0:T(8,128)(2,1)} %copy.153), calls=%async_computation.4 | async-start | bytes 1572864 | tf_op jit(solution)/shard_map/all_to_all | solution.py:548
  (52 other events, 662.7 us)
Sparse Core Ops, SparseCore 0:
  13.0 96.3 all-gather.8
  129.2 127.9 reduce-scatter.15
  259.4 141.0 all-gather.14
  403.0 49.2 all-gather.10
  496.8 54.2 reduce-scatter.21
  554.8 71.6 reduce-scatter.19
  630.3 50.0 all-gather.16
  703.2 81.2 reduce-scatter.23
  788.4 73.0 reduce-scatter.17
  874.6 187.5 all-reduce.1
  1063.8 16.6 all-gather.12
  1082.5 22.5 all-gather.18

commit v2 on v1

--- a/solution.py
+++ b/solution.py
@@ -1,6 +1,10 @@
+import functools
+
 import jax
 import jax.numpy as jnp
 from jax import lax
+from jax.experimental import pallas as pl
+from jax.experimental.pallas import tpu as pltpu
 from jax.sharding import PartitionSpec as P
 
 HEAD_DIM = 128
@@ -534,28 +538,12 @@
     )
 
 
-def swap_halves(value):
-    return lax.ppermute(value, "dp", [(0, 1), (1, 0)])
-
-
 def own_half_first(value):
     half = value.shape[-1] // 2
     turned = jnp.concatenate([value[..., half:], value[..., :half]], -1)
     return jnp.where(lax.axis_index("dp") == 0, value, turned)
 
 
-def exchange(value):
-    return lax.all_to_all(value, "context", split_axis=0, concat_axis=0, tiled=True)
-
-
-def sum_rows(value):
-    return lax.psum_scatter(value, ("context", "experts"), scatter_dimension=0, tiled=True)
-
-
-def share_rows(value):
-    return lax.all_gather(value, ("context", "experts"), axis=0, tiled=True)
-
-
 def dot_nn(left, right):
     return jnp.dot(left, right, preferred_element_type=jnp.float32)
 
@@ -570,6 +558,1045 @@
     return lax.dot_general(
         left, right, (((0,), (0,)), ((), ())), preferred_element_type=jnp.float32
     )
+
+
+MESH = pl.DeviceIdType.MESH
+DMA = pltpu.SemaphoreType.DMA
+
+
+def remote(source, target, send_sem, recv_sem, device):
+    return pltpu.make_async_remote_copy(
+        src_ref=source,
+        dst_ref=target,
+        send_sem=send_sem,
+        recv_sem=recv_sem,
+        device_id=device,
+        device_id_type=MESH,
+    )
+
+
+def rows_at(ref, start, size):
+    return ref.at[pl.ds(pl.multiple_of(start, 16), size), :]
+
+
+def lanes_at(ref, start, size):
+    return ref.at[:, pl.ds(pl.multiple_of(start, 128), size)]
+
+
+class Spot:
+    def __init__(self):
+        self.parts = lax.axis_size("context")
+        self.place, self.group = lax.axis_index("context"), lax.axis_index("experts")
+        self.twin = {"dp": 1 - lax.axis_index("dp")}
+        self.across = lax.rem(self.group + 2, 4)
+        self.beside = self.group + 1 - 2 * lax.rem(self.group, 2)
+        self.corner = lax.rem(self.beside + 2, 4)
+        self.has_left, self.has_right = self.place > 0, self.place < self.parts - 1
+
+    def greet(self, whole_line, twins):
+        barrier = pltpu.get_barrier_semaphore()
+        devices = [{"experts": self.across}, {"experts": self.beside}]
+        if twins:
+            devices.append(self.twin)
+        for device in devices:
+            pl.semaphore_signal(barrier, inc=1, device_id=device, device_id_type=MESH)
+        count = len(devices)
+        if whole_line:
+            for gap in range(1, self.parts):
+                device = {"context": lax.rem(self.place + gap, self.parts)}
+                pl.semaphore_signal(barrier, inc=1, device_id=device, device_id_type=MESH)
+            pl.semaphore_wait(barrier, count + self.parts - 1)
+        else:
+            for step, there in ((-1, self.has_left), (1, self.has_right)):
+
+                @pl.when(there)
+                def _():
+                    device = {"context": self.place + step}
+                    pl.semaphore_signal(barrier, inc=1, device_id=device, device_id_type=MESH)
+
+            ends = jnp.where(self.has_left & self.has_right, 0, 1)
+            pl.semaphore_wait(barrier, count + 2 - ends)
+
+    def far_first(self):
+        upper = self.place // (self.parts // 2)
+        return [3 * (1 - upper), 2 - upper, 1 + 4 * upper - self.place, self.place]
+
+    def others(self, gap, body):
+        @pl.when(self.place >= gap)
+        def _():
+            body(self.place - gap)
+
+        @pl.when(self.place + gap < self.parts)
+        def _():
+            body(self.place + gap)
+
+
+class Share:
+    def __init__(self, spot, own, out, sems):
+        self.spot, self.own, self.out = spot, own, out
+        self.local_sem, self.right_s, self.left_s, self.line_r, self.across_s, self.across_r, self.beside_s, self.beside_r = sems
+
+    @staticmethod
+    def sems(parts):
+        return [DMA, DMA((parts,)), DMA((parts,)), DMA((parts,)), DMA((parts,)), DMA((parts,)), DMA((2 * parts,)), DMA((2 * parts,))]
+
+    def block(self, part, column):
+        rows = self.own.shape[0]
+        return rows_at(self.out, (part * 4 + column) * rows, rows)
+
+    def to_right(self, part, source):
+        s = self.spot
+        return remote(source, self.block(part, s.group), self.right_s.at[part], self.line_r.at[part], {"context": s.place + 1})
+
+    def to_left(self, part, source):
+        s = self.spot
+        return remote(source, self.block(part, s.group), self.left_s.at[part], self.line_r.at[part], {"context": s.place - 1})
+
+    def to_across(self, part, source):
+        s = self.spot
+        return remote(source, self.block(part, s.group), self.across_s.at[part], self.across_r.at[part], {"experts": s.across})
+
+    def to_beside(self, part, column, slot, source):
+        s = self.spot
+        return remote(source, self.block(part, column), self.beside_s.at[slot], self.beside_r.at[slot], {"experts": s.beside})
+
+    def begin(self):
+        s = self.spot
+
+        @pl.when(s.has_right)
+        def _():
+            self.to_right(s.place, self.own).start()
+
+        @pl.when(s.has_left)
+        def _():
+            self.to_left(s.place, self.own).start()
+
+        self.to_across(s.place, self.own).start()
+        self.to_beside(s.place, s.group, s.place, self.own).start()
+        self.local().start()
+
+    def local(self):
+        return pltpu.make_async_copy(self.own, self.block(self.spot.place, self.spot.group), self.local_sem)
+
+    def pass_on(self, part):
+        s = self.spot
+        self.to_across(part, self.block(part, s.group)).wait_recv()
+        self.to_beside(part, s.across, s.parts + part, self.block(part, s.across)).start()
+
+    def arrival(self, part, onward, there):
+        s = self.spot
+        mine = self.block(part, s.group)
+        self.to_right(part, mine).wait_recv()
+
+        @pl.when(there)
+        def _():
+            onward(part, mine).start()
+
+        self.to_across(part, mine).start()
+        self.to_beside(part, s.group, part, mine).start()
+
+    def step(self, gap):
+        s = self.spot
+
+        @pl.when(s.place >= gap)
+        def _():
+            self.arrival(s.place - gap, self.to_right, s.has_right)
+
+        @pl.when(s.place + gap < s.parts)
+        def _():
+            self.arrival(s.place + gap, self.to_left, s.has_left)
+
+        if gap == 1:
+            self.pass_on(s.place)
+        else:
+            s.others(gap - 1, self.pass_on)
+
+    def end(self):
+        s = self.spot
+        s.others(s.parts - 1, self.pass_on)
+        self.local().wait()
+        for part in range(s.parts):
+            self.to_beside(part, s.beside, part, self.own).wait_recv()
+            self.to_beside(part, s.beside, s.parts + part, self.own).wait_recv()
+            self.to_across(part, self.own).wait_send()
+            self.to_beside(part, s.group, part, self.own).wait_send()
+            self.to_beside(part, s.group, s.parts + part, self.own).wait_send()
+
+            @pl.when(s.has_right & (part <= s.place))
+            def _():
+                self.to_right(part, self.own).wait_send()
+
+            @pl.when(s.has_left & (part >= s.place))
+            def _():
+                self.to_left(part, self.own).wait_send()
+
+
+class Sum:
+    def __init__(self, spot, part_ref, out, scratch):
+        self.spot, self.part_ref, self.out = spot, part_ref, out
+        (self.beside_buf, self.across_out, self.across_buf, self.line_out, self.left_buf, self.right_buf,
+         self.beside_s, self.beside_r, self.across_s, self.across_r, self.right_s, self.left_s, self.from_left, self.from_right) = scratch
+        self.order = spot.far_first()
+
+    @staticmethod
+    def scratch(parts, rows, width):
+        one = pltpu.VMEM((parts, rows, width), jnp.bfloat16)
+        two = pltpu.VMEM((2 * parts, rows, width), jnp.bfloat16)
+        return [two, one, one, one, one, one, DMA((2 * parts,)), DMA((2 * parts,))] + [DMA((parts,))] * 6
+
+    def base(self, part, column):
+        rows = self.out.shape[0]
+        return pl.multiple_of((part * 4 + column) * rows, rows)
+
+    def to_beside(self, part, column, slot):
+        source = self.part_ref.at[pl.ds(self.base(part, column), self.out.shape[0]), :]
+        return remote(source, self.beside_buf.at[slot], self.beside_s.at[slot], self.beside_r.at[slot], {"experts": self.spot.beside})
+
+    def to_across(self, part):
+        return remote(self.across_out.at[part], self.across_buf.at[part], self.across_s.at[part], self.across_r.at[part], {"experts": self.spot.across})
+
+    def to_right(self, part):
+        return remote(self.line_out.at[part], self.left_buf.at[part], self.right_s.at[part], self.from_left.at[part], {"context": self.spot.place + 1})
+
+    def to_left(self, part):
+        return remote(self.line_out.at[part], self.right_buf.at[part], self.left_s.at[part], self.from_right.at[part], {"context": self.spot.place - 1})
+
+    def chunks(self, body):
+        step = 16
+
+        def one(index, carry):
+            start = pl.multiple_of(index * step, step)
+            body(pl.ds(start, step), start, step)
+            return carry
+
+        lax.fori_loop(0, self.out.shape[0] // step, one, 0)
+
+    def mine(self, base, start, step):
+        return self.part_ref[pl.ds(pl.multiple_of(base + start, step), step), :].astype(jnp.float32)
+
+    def begin(self):
+        s = self.spot
+        for part in self.order:
+            self.to_beside(part, s.corner, s.parts + part).start()
+        for part in self.order:
+            self.to_beside(part, s.beside, part).start()
+
+    def cross(self, index):
+        s, part = self.spot, self.order[index]
+        self.to_beside(part, s.corner, s.parts + part).wait_recv()
+        base = self.base(part, s.across)
+
+        def add(at, start, step):
+            total = self.mine(base, start, step) + self.beside_buf[s.parts + part, at, :].astype(jnp.float32)
+            self.across_out[part, at, :] = total.astype(jnp.bfloat16)
+
+        self.chunks(add)
+        self.to_across(part).start()
+
+    def line(self, index):
+        s, part = self.spot, self.order[index]
+        self.to_beside(part, s.beside, part).wait_recv()
+        self.to_across(part).wait_recv()
+        base = self.base(part, s.group)
+        f32 = jnp.float32
+
+        def total(at, start, step):
+            return self.mine(base, start, step) + self.beside_buf[part, at, :].astype(f32) + self.across_buf[part, at, :].astype(f32)
+
+        def send(buf):
+            def add(at, start, step):
+                value = total(at, start, step)
+                if buf is not None:
+                    value = value + buf[part, at, :].astype(f32)
+                self.line_out[part, at, :] = value.astype(jnp.bfloat16)
+
+            self.chunks(add)
+
+        if index < s.parts - 1:
+            goes_right = part > s.place
+            goes_left = jnp.logical_not(goes_right)
+
+            @pl.when(goes_right & s.has_left)
+            def _():
+                self.to_right(part).wait_recv()
+                send(self.left_buf)
+
+            @pl.when(goes_left & s.has_right)
+            def _():
+                self.to_left(part).wait_recv()
+                send(self.right_buf)
+
+            @pl.when((goes_right & jnp.logical_not(s.has_left)) | (goes_left & jnp.logical_not(s.has_right)))
+            def _():
+                send(None)
+
+            @pl.when(goes_right)
+            def _():
+                self.to_right(part).start()
+
+            @pl.when(goes_left)
+            def _():
+                self.to_left(part).start()
+        else:
+
+            def keep(at, start, step):
+                self.out[at, :] = total(at, start, step)
+
+            self.chunks(keep)
+            for there, copy, buf in ((s.has_left, self.to_right, self.left_buf), (s.has_right, self.to_left, self.right_buf)):
+
+                @pl.when(there)
+                def _():
+                    copy(part).wait_recv()
+
+                    def add(at, start, step):
+                        self.out[at, :] = self.out[at, :] + buf[part, at, :].astype(f32)
+
+                    self.chunks(add)
+
+    def end(self):
+        s = self.spot
+        for part in range(s.parts):
+            self.to_beside(part, s.corner, s.parts + part).wait_send()
+            self.to_beside(part, s.beside, part).wait_send()
+            self.to_across(part).wait_send()
+
+            @pl.when(part > s.place)
+            def _():
+                self.to_right(part).wait_send()
+
+            @pl.when(part < s.place)
+            def _():
+                self.to_left(part).wait_send()
+
+
+class Move:
+    def __init__(self, spot, items, sems):
+        self.spot, self.items = spot, items
+        self.line_s, self.line_r, self.twin_s, self.twin_r, self.local_sem = sems
+
+    @staticmethod
+    def sems(count, parts):
+        return [DMA((count * parts,))] * 4 + [DMA((count,))]
+
+    def to(self, number, target, source):
+        s, (src, dst) = self.spot, self.items[number]
+        return remote(src(target), dst(0, source), self.line_s.at[number * s.parts + target], self.line_r.at[number * s.parts + source], {"context": target})
+
+    def on(self, number, source, view):
+        s, (_, dst) = self.spot, self.items[number]
+        slot = number * s.parts + source
+        return remote(view, dst(1, source), self.twin_s.at[slot], self.twin_r.at[slot], s.twin)
+
+    def local(self, number):
+        s, (src, dst) = self.spot, self.items[number]
+        return pltpu.make_async_copy(src(s.place), dst(0, s.place), self.local_sem.at[number])
+
+    def own(self, number):
+        s, (src, _) = self.spot, self.items[number]
+        self.on(number, s.place, src(s.place)).start()
+        self.local(number).start()
+
+    def send(self, number):
+        s = self.spot
+        for gap in range(s.parts - 1, 0, -1):
+            s.others(gap, lambda target: self.to(number, target, s.place).start())
+
+    def forward(self, number, gap):
+        s, (_, dst) = self.spot, self.items[number]
+
+        def one(source):
+            self.to(number, s.place, source).wait_recv()
+            self.on(number, source, dst(0, source)).start()
+
+        s.others(gap, one)
+
+    def end(self):
+        s = self.spot
+        for number, (src, dst) in enumerate(self.items):
+            self.local(number).wait()
+            for part in range(s.parts):
+                self.on(number, part, dst(0, part)).wait()
+
+                @pl.when(part != s.place)
+                def _():
+                    self.to(number, part, s.place).wait_send()
+
+
+class Return:
+    def __init__(self, spot, items, got, mine, sems):
+        self.spot, self.items, self.got, self.mine_buf = spot, items, got, mine
+        self.twin_s, self.twin_r, self.load, self.line_s, self.line_r, self.local_sem = sems
+        self.order = spot.far_first()
+        self.bases = []
+        for item in items:
+            self.bases.append(self.bases[-1][1] if self.bases else 0)
+            self.bases[-1] = (self.bases[-1], self.bases[-1] + len(item["pieces"]) * spot.parts)
+
+    @staticmethod
+    def scratch(shapes, pieces, parts):
+        count = len(shapes)
+        buf = [pltpu.VMEM((parts,) + shape, jnp.bfloat16) for shape in shapes]
+        sems = [DMA((count * parts,))] * 3 + [DMA((sum(pieces) * parts,))] * 2 + [DMA((sum(pieces),))]
+        return buf + buf + sems
+
+    def swap(self, number, part):
+        item, slot = self.items[number], number * self.spot.parts + part
+        return remote(item["block"](1, part), self.got[number].at[part], self.twin_s.at[slot], self.twin_r.at[slot], self.spot.twin)
+
+    def fetch(self, number, part):
+        item, slot = self.items[number], number * self.spot.parts + part
+        return pltpu.make_async_copy(item["block"](0, part), self.mine_buf[number].at[part], self.load.at[slot])
+
+    def start(self, number):
+        for part in self.order:
+            self.swap(number, part).start()
+            self.fetch(number, part).start()
+
+    def piece(self, number, which, target, source, short):
+        s = self.spot
+        cut, out = self.items[number]["pieces"][which]
+        slot = self.bases[number][0] + which * s.parts
+        return remote(cut(self.mine_buf[number].at[target], short), out(source, short), self.line_s.at[slot + target], self.line_r.at[slot + source], {"context": target})
+
+    def keep(self, number, which, short):
+        s = self.spot
+        cut, out = self.items[number]["pieces"][which]
+        slot = self.bases[number][0] // s.parts + which
+        return pltpu.make_async_copy(cut(self.mine_buf[number].at[s.place], short), out(s.place, short), self.local_sem.at[slot])
+
+    def by_width(self, source, body):
+        last = source == self.spot.parts - 1
+        if not isinstance(source, int):
+
+            @pl.when(last)
+            def _():
+                body(True)
+
+            @pl.when(jnp.logical_not(last))
+            def _():
+                body(False)
+        else:
+            body(last)
+
+    def reduce(self, number, index):
+        s, part = self.spot, self.order[index]
+        item = self.items[number]
+        self.swap(number, part).wait_recv()
+        self.fetch(number, part).wait()
+        mine, got = self.mine_buf[number], self.got[number]
+        rows, step = mine.shape[1], 32
+
+        def one(at, carry):
+            span = pl.ds(pl.multiple_of(at * step, step), step)
+            total = mine[part, span, :].astype(jnp.float32) + got[part, span, :].astype(jnp.float32)
+            mine[part, span, :] = total.astype(jnp.bfloat16)
+            return carry
+
+        lax.fori_loop(0, rows // step, one, 0)
+        for which in range(len(item["pieces"])):
+            if index < s.parts - 1:
+                self.by_width(s.place, lambda short: self.piece(number, which, part, s.place, short).start())
+            else:
+                self.by_width(s.place, lambda short: self.keep(number, which, short).start())
+
+    def end(self):
+        s = self.spot
+        for number, item in enumerate(self.items):
+            for part in range(s.parts):
+                self.swap(number, part).wait_send()
+                for which in range(len(item["pieces"])):
+
+                    @pl.when(part != s.place)
+                    def _():
+                        self.by_width(s.place, lambda short: self.piece(number, which, part, s.place, short).wait_send())
+                        self.by_width(part, lambda short: self.piece(number, which, s.place, part, short).wait_recv())
+
+            for which in range(len(item["pieces"])):
+                self.by_width(s.place, lambda short: self.keep(number, which, short).wait())
+
+
+def comm_call(kernel, number, name, out_shape, out_specs, in_specs, scratch, bytes_moved):
+    return pl.pallas_call(
+        kernel,
+        out_shape=out_shape,
+        in_specs=in_specs,
+        out_specs=out_specs,
+        scratch_shapes=scratch,
+        compiler_params=pltpu.CompilerParams(collective_id=number, has_side_effects=True),
+        cost_estimate=pl.CostEstimate(flops=0, bytes_accessed=bytes_moved, transcendentals=0),
+        name=name,
+    )
+
+
+IN_VMEM = pl.BlockSpec(memory_space=pltpu.VMEM)
+IN_PLACE = pl.BlockSpec(memory_space=pl.ANY)
+WINDOW = 384
+
+
+def window_of(index, length):
+    return jnp.minimum(index * WINDOW, length - WINDOW)
+
+
+def share_first(value, qkv_in, out_weight, number):
+    parts = lax.axis_size("context")
+    rows, width = value.shape
+    block, span = qkv_in.shape[0] // parts, qkv_in.shape[1]
+    head, lanes = out_weight.shape[0] // parts, out_weight.shape[1]
+    share_sems, move_sems = Share.sems(parts), Move.sems(2, parts)
+
+    def kernel(own_ref, qkv_ref, outw_ref, all_ref, wqkv_ref, wout_ref, *sems):
+        spot = Spot()
+        share = Share(spot, own_ref, all_ref, sems[: len(share_sems)])
+        items = [
+            (
+                lambda target: rows_at(qkv_ref, target * block, block),
+                lambda side, source: rows_at(wqkv_ref, (side * parts + source) * block, block),
+            ),
+            (
+                lambda target: rows_at(outw_ref, target * head, head),
+                lambda side, source: lanes_at(wout_ref, (side * parts + source) * lanes, lanes),
+            ),
+        ]
+        move = Move(spot, items, sems[len(share_sems) :])
+        spot.greet(True, True)
+        share.begin()
+        for item in range(2):
+            move.own(item)
+        move.send(0)
+        share.step(1)
+        move.send(1)
+        move.forward(0, 1)
+        share.step(2)
+        move.forward(0, 2)
+        share.step(3)
+        move.forward(0, 3)
+        for gap in (1, 2, 3):
+            move.forward(1, gap)
+        share.end()
+        move.end()
+
+    bf16 = jnp.bfloat16
+    return comm_call(
+        kernel,
+        number,
+        "share_first",
+        [
+            jax.ShapeDtypeStruct((rows * parts * 4, width), value.dtype),
+            jax.ShapeDtypeStruct((2 * parts * block, span), bf16),
+            jax.ShapeDtypeStruct((head, 2 * parts * lanes), bf16),
+        ],
+        [IN_PLACE] * 3,
+        [IN_VMEM, IN_PLACE, IN_PLACE],
+        share_sems + move_sems,
+        180_000_000,
+    )(value, qkv_in, out_weight)
+
+
+def sum_and_move(value, shared_down, expert_down, number):
+    parts = lax.axis_size("context")
+    total, width = value.shape
+    rows = total // (4 * parts)
+    hidden, lanes = shared_down.shape
+    count = 1 + expert_down.shape[0]
+    sum_scratch, move_sems = Sum.scratch(parts, rows, width), Move.sems(count, parts)
+
+    def kernel(part_ref, shared_ref, expert_ref, out_ref, wd_ref, *scratch):
+        spot = Spot()
+        summed = Sum(spot, part_ref, out_ref, scratch[: len(sum_scratch)])
+
+        def item(k):
+            ref = shared_ref if k == 0 else expert_ref.at[k - 1]
+            return (
+                lambda target: rows_at(ref, window_of(target, hidden), WINDOW),
+                lambda side, source: wd_ref.at[
+                    pl.ds(k * WINDOW, WINDOW),
+                    pl.ds(pl.multiple_of((side * parts + source) * lanes, lanes), lanes),
+                ],
+            )
+
+        move = Move(spot, [item(k) for k in range(count)], scratch[len(sum_scratch) :])
+        spot.greet(True, True)
+        summed.begin()
+        for k in range(count):
+            move.own(k)
+        move.send(0)
+        move.send(1)
+        for index in range(parts):
+            summed.cross(index)
+        for gap in (1, 2, 3):
+            move.forward(0, gap)
+        for index in range(parts):
+            summed.line(index)
+        for k in range(2, count):
+            move.send(k)
+        for k in range(1, count):
+            for gap in (1, 2, 3):
+                move.forward(k, gap)
+        summed.end()
+        move.end()
+
+    return comm_call(
+        kernel,
+        number,
+        "sum_and_move",
+        [
+            jax.ShapeDtypeStruct((rows, width), jnp.float32),
+            jax.ShapeDtypeStruct((count * WINDOW, 2 * parts * lanes), jnp.bfloat16),
+        ],
+        [IN_VMEM, IN_PLACE],
+        [IN_VMEM, IN_PLACE, IN_PLACE],
+        sum_scratch + move_sems,
+        180_000_000,
+    )(value, shared_down, expert_down)
+
+
+def share_and_move(value, shared_gate, shared_up, expert_gate, expert_up, number):
+    parts = lax.axis_size("context")
+    rows, width = value.shape
+    block, hidden = shared_gate.shape
+    stacks = 1 + expert_gate.shape[0]
+    count = 2 * stacks
+    share_sems, move_sems = Share.sems(parts), Move.sems(count, parts)
+
+    def kernel(own_ref, sg_ref, su_ref, eg_ref, eu_ref, all_ref, wgu_ref, *sems):
+        spot = Spot()
+        share = Share(spot, own_ref, all_ref, sems[: len(share_sems)])
+
+        def item(number):
+            k = number // 2
+            shared, expert = (sg_ref, eg_ref) if number % 2 == 0 else (su_ref, eu_ref)
+            ref = shared if k == 0 else expert.at[k - 1]
+            return (
+                lambda target: lanes_at(ref, window_of(target, hidden), WINDOW),
+                lambda side, source: wgu_ref.at[
+                    pl.ds(pl.multiple_of((side * parts + source) * block, block), block),
+                    pl.ds(number * WINDOW, WINDOW),
+                ],
+            )
+
+        move = Move(spot, [item(number) for number in range(count)], sems[len(share_sems) :])
+        spot.greet(True, True)
+        share.begin()
+        for number in range(count):
+            move.own(number)
+        move.send(0)
+        share.step(1)
+        move.send(1)
+        share.step(2)
+        for gap in (1, 2, 3):
+            move.forward(0, gap)
+        share.step(3)
+        for number in range(2, count):
+            move.send(number)
+        for number in range(1, count):
+            for gap in (1, 2, 3):
+                move.forward(number, gap)
+        share.end()
+        move.end()
+
+    return comm_call(
+        kernel,
+        number,
+        "share_and_move",
+        [
+            jax.ShapeDtypeStruct((rows * parts * 4, width), value.dtype),
+            jax.ShapeDtypeStruct((2 * parts * block, count * WINDOW), jnp.bfloat16),
+        ],
+        [IN_PLACE] * 2,
+        [IN_VMEM] + [IN_PLACE] * 4,
+        share_sems + move_sems,
+        300_000_000,
+    )(value, shared_gate, shared_up, expert_gate, expert_up)
+
+
+def up_item(grads_ref, k, gate_ref, up_ref, block, parts):
+    hidden = gate_ref.shape[1]
+    tail = hidden - (parts - 1) * WINDOW
+
+    def cut(offset):
+        return lambda buf, short: buf.at[:, pl.ds(offset + (WINDOW - tail if short else 0), tail if short else WINDOW)]
+
+    def out(ref):
+        return lambda source, short: ref.at[:, pl.ds(hidden - tail, tail)] if short else lanes_at(ref, source * WINDOW, WINDOW)
+
+    return {
+        "block": lambda side, part: grads_ref.at[
+            pl.ds(pl.multiple_of((side * parts + part) * block, block), block), pl.ds(2 * k * WINDOW, 2 * WINDOW)
+        ],
+        "pieces": [(cut(0), out(gate_ref)), (cut(WINDOW), out(up_ref))],
+        "shape": (block, 2 * WINDOW),
+    }
+
+
+def down_item(grads_ref, k, down_ref, parts):
+    hidden, lanes = down_ref.shape
+    tail = hidden - (parts - 1) * WINDOW
+    return {
+        "block": lambda side, part: grads_ref.at[
+            pl.ds(k * WINDOW, WINDOW), pl.ds(pl.multiple_of((side * parts + part) * lanes, lanes), lanes)
+        ],
+        "pieces": [
+            (
+                lambda buf, short: buf.at[pl.ds(WINDOW - tail if short else 0, tail if short else WINDOW), :],
+                lambda source, short: down_ref.at[pl.ds(hidden - tail, tail), :] if short else rows_at(down_ref, source * WINDOW, WINDOW),
+            )
+        ],
+        "shape": (WINDOW, lanes),
+    }
+
+
+def sum_and_return(value, up_grads, k, number):
+    parts = lax.axis_size("context")
+    total, width = value.shape
+    rows = total // (4 * parts)
+    block = up_grads.shape[0] // (2 * parts)
+    hidden = WINDOW * parts - 128
+    sum_scratch = Sum.scratch(parts, rows, width)
+    back_scratch = Return.scratch([(block, 2 * WINDOW)], [2], parts)
+
+    def kernel(part_ref, grads_ref, out_ref, gate_ref, up_ref, *scratch):
+        spot = Spot()
+        summed = Sum(spot, part_ref, out_ref, scratch[: len(sum_scratch)])
+        got, mine, *sems = scratch[len(sum_scratch) :]
+        back = Return(spot, [up_item(grads_ref, k, gate_ref, up_ref, block, parts)], [got], [mine], sems)
+        spot.greet(True, True)
+        summed.begin()
+        back.start(0)
+        for index in range(parts):
+            summed.cross(index)
+        back.reduce(0, 0)
+        back.reduce(0, 1)
+        summed.line(0)
+        summed.line(1)
+        back.reduce(0, 2)
+        back.reduce(0, 3)
+        summed.line(2)
+        summed.line(3)
+        summed.end()
+        back.end()
+
+    piece = jax.ShapeDtypeStruct((block, hidden), jnp.bfloat16)
+    return comm_call(
+        kernel,
+        number,
+        "sum_and_return",
+        [jax.ShapeDtypeStruct((rows, width), jnp.float32), piece, piece],
+        [IN_VMEM, IN_PLACE, IN_PLACE],
+        [IN_VMEM, IN_PLACE],
+        sum_scratch + back_scratch,
+        250_000_000,
+    )(value, up_grads)
+
+
+def share_and_return(value, down_grads, k, number):
+    parts = lax.axis_size("context")
+    rows, width = value.shape
+    lanes = down_grads.shape[1] // (2 * parts)
+    hidden = WINDOW * parts - 128
+    share_sems = Share.sems(parts)
+    back_scratch = Return.scratch([(WINDOW, lanes)], [1], parts)
+
+    def kernel(own_ref, grads_ref, all_ref, down_ref, *scratch):
+        spot = Spot()
+        share = Share(spot, own_ref, all_ref, scratch[: len(share_sems)])
+        got, mine, *sems = scratch[len(share_sems) :]
+        back = Return(spot, [down_item(grads_ref, k, down_ref, parts)], [got], [mine], sems)
+        spot.greet(True, True)
+        share.begin()
+        back.start(0)
+        share.step(1)
+        share.step(2)
+        back.reduce(0, 0)
+        share.step(3)
+        for index in range(1, parts):
+            back.reduce(0, index)
+        share.end()
+        back.end()
+
+    return comm_call(
+        kernel,
+        number,
+        "share_and_return",
+        [
+            jax.ShapeDtypeStruct((rows * parts * 4, width), value.dtype),
+            jax.ShapeDtypeStruct((hidden, lanes), jnp.bfloat16),
+        ],
+        [IN_PLACE, IN_PLACE],
+        [IN_VMEM, IN_PLACE],
+        share_sems + back_scratch,
+        180_000_000,
+    )(value, down_grads)
+
+
+class Group:
+    def __init__(self, spot, own, out, sems):
+        self.spot, self.own, self.out = spot, own, out
+        self.local_sem, self.across_s, self.across_r, self.beside_s, self.beside_r = sems
+
+    @staticmethod
+    def sems():
+        return [DMA, DMA, DMA, DMA((2,)), DMA((2,))]
+
+    def block(self, column):
+        rows = self.own.shape[0]
+        return rows_at(self.out, column * rows, rows)
+
+    def to_across(self):
+        s = self.spot
+        return remote(self.own, self.block(s.group), self.across_s, self.across_r, {"experts": s.across})
+
+    def to_beside(self, slot):
+        s = self.spot
+        column = s.across if slot else s.group
+        source = self.block(column) if slot else self.own
+        return remote(source, self.block(column), self.beside_s.at[slot], self.beside_r.at[slot], {"experts": s.beside})
+
+    def local(self):
+        return pltpu.make_async_copy(self.own, self.block(self.spot.group), self.local_sem)
+
+    def begin(self):
+        self.to_across().start()
+        self.to_beside(0).start()
+        self.local().start()
+
+    def end(self):
+        self.to_across().wait_recv()
+        self.to_beside(1).start()
+        self.local().wait()
+        self.to_across().wait_send()
+        for slot in range(2):
+            self.to_beside(slot).wait()
+
+
+class Total:
+    def __init__(self, spot, value, out, scratch):
+        self.out = out
+        self.sent, self.got, self.send_s, self.recv_s = scratch
+        place = spot.place
+        self.turns = [
+            spot.twin,
+            {"context": place + 1 - 2 * lax.rem(place, 2)},
+            {"context": lax.rem(place + 2, spot.parts)},
+            {"experts": spot.beside},
+            {"experts": spot.across},
+        ]
+        self.value = value
+
+    @staticmethod
+    def scratch(shape):
+        buf = pltpu.VMEM((5,) + shape, jnp.float32)
+        return [buf, buf, DMA((5,)), DMA((5,))]
+
+    def copy(self, index):
+        return remote(self.sent.at[index], self.got.at[index], self.send_s.at[index], self.recv_s.at[index], self.turns[index])
+
+    def begin(self):
+        self.out[...] = self.value[...]
+        self.send(0)
+
+    def send(self, index):
+        self.sent[index] = self.out[...]
+        self.copy(index).start()
+
+    def take(self, index):
+        self.copy(index).wait()
+        self.out[...] = self.out[...] + self.got[index]
+
+
+def last_exchange(up_grads, down_grads, out_grads, qkv_grads, branch, hidden, tokens_grad, small, ups, downs, number):
+    parts = lax.axis_size("context")
+    block = up_grads.shape[0] // (2 * parts)
+    lanes = down_grads.shape[1] // (2 * parts)
+    units = WINDOW * parts - 128
+    head, span = out_grads.shape[0], qkv_grads.shape[1]
+    rows, width = hidden.shape
+    shapes = [(head, lanes), (block, span)] + [(block, 2 * WINDOW)] * len(ups) + [(WINDOW, lanes)] * len(downs)
+    pieces = [1, 1] + [2] * len(ups) + [1] * len(downs)
+    count, bf16 = len(shapes), jnp.bfloat16
+    groups = [
+        Return.scratch(shapes, pieces, parts),
+        Sum.scratch(parts, rows, width) + [pltpu.VMEM((rows, width), jnp.float32), pltpu.VMEM((rows, width), bf16)],
+        Total.scratch(small.shape),
+        Group.sems(),
+        Group.sems(),
+    ]
+    piece, column = jax.ShapeDtypeStruct((block, units), bf16), jax.ShapeDtypeStruct((units, lanes), bf16)
+    out_shape = [jax.ShapeDtypeStruct((parts * head, lanes), bf16), jax.ShapeDtypeStruct((parts * block, span), bf16)]
+    out_shape += [piece] * (2 * len(ups)) + [column] * len(downs)
+    out_shape += [
+        jax.ShapeDtypeStruct((4 * rows, width), bf16),
+        jax.ShapeDtypeStruct((4 * rows, width), jnp.float32),
+        jax.ShapeDtypeStruct(small.shape, jnp.float32),
+    ]
+
+    def kernel(upg_ref, downg_ref, outg_ref, qkvg_ref, branch_ref, hidden_ref, tokens_ref, small_ref, *rest):
+        outs, scratch = rest[: len(out_shape)], list(rest[len(out_shape) :])
+        sets = []
+        for one in groups:
+            sets.append(scratch[: len(one)])
+            scratch = scratch[len(one) :]
+        grads, (block_all, tokens_all, small_out) = outs[:-3], outs[-3:]
+        items = [
+            {
+                "block": lambda side, part: lanes_at(outg_ref, (side * parts + part) * lanes, lanes),
+                "pieces": [(lambda buf, short: buf, lambda source, short: rows_at(grads[0], source * head, head))],
+            },
+            {
+                "block": lambda side, part: rows_at(qkvg_ref, (side * parts + part) * block, block),
+                "pieces": [(lambda buf, short: buf, lambda source, short: rows_at(grads[1], source * block, block))],
+            },
+        ]
+        items += [up_item(upg_ref, k, grads[2 + 2 * i], grads[3 + 2 * i], block, parts) for i, k in enumerate(ups)]
+        items += [down_item(downg_ref, k, grads[2 + 2 * len(ups) + i], parts) for i, k in enumerate(downs)]
+        spot = Spot()
+        back = Return(spot, items, sets[0][:count], sets[0][count : 2 * count], sets[0][2 * count :])
+        total_branch, own_block = sets[1][-2:]
+        summed = Sum(spot, branch_ref, total_branch, sets[1][:-2])
+        total = Total(spot, small_ref, small_out, sets[2])
+        tokens_group = Group(spot, tokens_ref, tokens_all, sets[3])
+        block_group = Group(spot, own_block, block_all, sets[4])
+        spot.greet(True, True)
+        total.begin()
+        summed.begin()
+        back.start(0)
+        back.start(1)
+        total.take(0)
+        total.send(1)
+        for index in range(parts):
+            summed.cross(index)
+        total.take(1)
+        total.send(2)
+        for item in range(2, count):
+            back.start(item)
+        for index in range(parts):
+            back.reduce(0, index)
+        total.take(2)
+        total.send(3)
+        for index in range(parts):
+            back.reduce(1, index)
+        total.take(3)
+        total.send(4)
+        summed.line(0)
+        summed.line(1)
+        total.take(4)
+        tokens_group.begin()
+        back.reduce(2, 0)
+        summed.line(2)
+        back.reduce(2, 1)
+        summed.line(3)
+        half = width // 2
+
+        def finish(at, start, step):
+            value = (hidden_ref[at, :] + total_branch[at, :]).astype(bf16)
+            turned = lax.axis_index("dp") == 0
+
+            @pl.when(turned)
+            def _():
+                own_block[at, :] = value
+
+            @pl.when(jnp.logical_not(turned))
+            def _():
+                own_block[at, :half] = value[:, half:]
+                own_block[at, half:] = value[:, :half]
+
+        summed.chunks(finish)
+        block_group.begin()
+        for index in range(2, parts):
+            back.reduce(2, index)
+        for item in range(3, count):
+            for index in range(parts):
+                back.reduce(item, index)
+        summed.end()
+        tokens_group.end()
+        block_group.end()
+        back.end()
+
+    return comm_call(
+        kernel,
+        number,
+        "last_exchange",
+        out_shape,
+        [IN_PLACE] * (len(out_shape) - 1) + [IN_VMEM],
+        [IN_PLACE] * 4 + [IN_VMEM] * 4,
+        [one for group in groups for one in group],
+        300_000_000,
+    )(up_grads, down_grads, out_grads, qkv_grads, branch, hidden, tokens_grad, small)
+
+
+def hidden_kernel(parts, stacks, units, both_ref, wgu_ref, wd_ref, coef_ref, send_ref, branch_ref, dup_ref, act_ref, dx_acc, out_acc, dot_acc):
+    width = branch_ref.shape[1]
+    f32, bf16 = jnp.float32, jnp.bfloat16
+    repeated = jnp.where(lax.axis_index("context") == parts - 1, WINDOW * parts - units, 0)
+    lane = lax.broadcasted_iota(jnp.int32, (1, WINDOW), 1)
+    fresh = jnp.where(lane >= repeated, 1.0, 0.0)
+    group = lax.axis_index("experts")
+    column = lax.broadcasted_iota(jnp.int32, (1, 128), 1)
+    dot_acc[...] = jnp.zeros_like(dot_acc)
+    for k in range(stacks):
+        up = pl.ds(2 * k * WINDOW, 2 * WINDOW)
+        down = pl.ds(k * WINDOW, WINDOW)
+        vals = jnp.dot(both_ref[:, :width], wgu_ref[:, up], preferred_element_type=f32)
+        raw = dot_nt(both_ref[:, width:], wd_ref[down, :]) * fresh
+        g_vals, u_vals = vals[:, :WINDOW], vals[:, WINDOW:]
+        sig_g = jax.nn.sigmoid(g_vals)
+        silu_g = g_vals * sig_g
+        act = silu_g * u_vals
+        coef = coef_ref[:, k : k + 1]
+        at = (stacks - 1) * 4 if k == 0 else group * (stacks - 1) + k - 1
+        dots = jnp.sum(raw * act, -1, keepdims=True)
+        dot_acc[...] += dots * jnp.where(column == at, 1.0, 0.0)
+        act_ref[:, down] = (act * (coef * fresh)).astype(bf16)
+        dact = raw * coef
+        dup_ref[:, pl.ds(2 * k * WINDOW, WINDOW)] = (dact * u_vals * (sig_g * (1.0 + g_vals * (1.0 - sig_g)))).astype(bf16)
+        dup_ref[:, pl.ds((2 * k + 1) * WINDOW, WINDOW)] = (dact * silu_g).astype(bf16)
+        out_part = jnp.dot(act_ref[:, down], wd_ref[down, :], preferred_element_type=f32)
+        dx_part = dot_nt(dup_ref[:, up], wgu_ref[:, up])
+        if k == 0:
+            out_acc[...] = out_part
+            dx_acc[...] = dx_part
+        elif k < stacks - 1:
+            out_acc[...] += out_part
+            dx_acc[...] += dx_part
+        else:
+            branch_ref[...] = (out_acc[...] + out_part).astype(bf16)
+            send_ref[:, :width] = (dx_acc[...] + dx_part).astype(bf16)
+    send_ref[:, width:] = dot_acc[...].astype(bf16)
+
+
+def hidden_units(both, wgu, wd, coefs, units):
+    length, width = both.shape[0], both.shape[1] // 2
+    stacks = wd.shape[0] // WINDOW
+    step = min(256, length)
+    bf16 = jnp.bfloat16
+
+    def rows_block(columns):
+        return pl.BlockSpec((step, columns), lambda i: (i, 0))
+
+    def whole(array):
+        return pl.BlockSpec(array.shape, lambda i: (0, 0), pipeline_mode=pl.Buffered(1))
+
+    return pl.pallas_call(
+        functools.partial(hidden_kernel, lax.axis_size("context"), stacks, units),
+        grid=(length // step,),
+        in_specs=[rows_block(2 * width), whole(wgu), whole(wd), rows_block(coefs.shape[1])],
+        out_specs=[rows_block(width + 128), rows_block(width), rows_block(wgu.shape[1]), rows_block(wd.shape[0])],
+        out_shape=[
+            jax.ShapeDtypeStruct((length, width + 128), bf16),
+            jax.ShapeDtypeStruct((length, width), bf16),
+            jax.ShapeDtypeStruct((length, wgu.shape[1]), bf16),
+            jax.ShapeDtypeStruct((length, wd.shape[0]), bf16),
+        ],
+        scratch_shapes=[
+            pltpu.VMEM((step, width), jnp.float32),
+            pltpu.VMEM((step, width), jnp.float32),
+            pltpu.VMEM((step, 128), jnp.float32),
+        ],
+        cost_estimate=pl.CostEstimate(
+            flops=6 * length * width * wgu.shape[1], bytes_accessed=40_000_000, transcendentals=length * wd.shape[0]
+        ),
+        name="hidden_units",
+    )(both, wgu, wd, coefs)
 
 
 def split_body(
@@ -603,57 +1630,38 @@
     block = width // (2 * parts)
     hidden_here = shared_w_gate.shape[1] // parts
     stacks = local_experts + 1
-    span = stacks * hidden_here
     scale = HEAD_DIM ** (-0.5)
     bf16 = jnp.bfloat16
 
+    first = group * own_rows
+
+    def own_of(array):
+        return lax.dynamic_slice_in_dim(array, first, own_rows, 0)
+
+    grad_own_b = own_half_first(own_of(out_grad[0]))
+    grad_own = grad_own_b.astype(jnp.float32)
+    gain1 = own_half_first(norm1_gain).astype(jnp.float32)
+    gain2 = own_half_first(norm2_gain).astype(jnp.float32)
+    token_own = own_half_first(own_of(tokens[0])).astype(jnp.float32)
+    inverse1 = lax.rsqrt(jnp.mean(token_own * token_own, -1, keepdims=True) + EPSILON)
+    normed1 = token_own * inverse1
+    places_own = own_of(positions[0])[:, None]
+    facts = jnp.concatenate([places_own // 64, places_own % 64, own_of(routes[0])], 1)
+    facts = jnp.pad(facts, ((0, 0), (0, 128 - facts.shape[1]))).astype(bf16)
+    send1 = jnp.concatenate([(normed1 * gain1).astype(bf16), facts], 1)
     qkv_in = jnp.transpose(
         qkv_weight.reshape(block, 3, parts, HEAD_DIM), (2, 0, 1, 3)
-    ).reshape(parts, block, 3 * HEAD_DIM)
-    qkv_m = exchange(qkv_in).reshape(half, 3 * HEAD_DIM)
-    qkv_o = swap_halves(qkv_m)
-    out_m = jnp.transpose(exchange(out_weight.reshape(parts, HEAD_DIM, block)), (1, 0, 2)).reshape(
-        HEAD_DIM, half
-    )
-    out_o = swap_halves(out_m)
-    down_in = jnp.concatenate([shared_w_down[None], expert_down], 0)
-    down_in = jnp.transpose(
-        down_in.reshape(stacks, parts, hidden_here, block), (1, 0, 2, 3)
-    ).reshape(parts, span, block)
-    down_m = jnp.transpose(exchange(down_in), (1, 0, 2)).reshape(span, half)
-    down_o = swap_halves(down_m)
-    up_in = jnp.concatenate(
-        [shared_w_gate[None], expert_gate, shared_w_up[None], expert_up], 0
-    ).reshape(2 * stacks, block, parts, hidden_here)
-    up_in = jnp.transpose(up_in, (2, 1, 0, 3)).reshape(parts, block, 2 * span)
-    up_m = exchange(up_in).reshape(half, 2 * span)
-    up_o = swap_halves(up_m)
-
-    grad_all = lax.all_gather(own_half_first(out_grad[0]), "context", axis=0, tiled=True)
-    position_all = lax.all_gather(positions[0], "context", axis=0, tiled=True)
-    route_all = lax.all_gather(routes[0], "context", axis=0, tiled=True)
-
-    gain1 = own_half_first(norm1_gain).astype(jnp.float32)
-    gain2 = own_half_first(norm2_gain).astype(jnp.float32)
-    token_rows = own_half_first(tokens[0]).astype(jnp.float32)
-    inverse_rows = lax.rsqrt(jnp.mean(token_rows * token_rows, -1, keepdims=True) + EPSILON)
-    xn1 = lax.all_gather(
-        (token_rows * inverse_rows * gain1).astype(bf16), "context", axis=0, tiled=True
-    )
-    first = group * own_rows
-    token_own = lax.dynamic_slice_in_dim(token_rows, first, own_rows, 0)
-    inverse1 = lax.dynamic_slice_in_dim(inverse_rows, first, own_rows, 0)
-    normed1 = token_own * inverse1
-    grad_own = lax.dynamic_slice_in_dim(
-        own_half_first(out_grad[0]).astype(jnp.float32), first, own_rows, 0
-    )
+    ).reshape(parts * block, 3 * HEAD_DIM)
+    shared1, qkv_w, out_w = share_first(send1, qkv_in, out_weight, 1)
+    xn1, facts = shared1[:, :width], shared1[:, width:].astype(jnp.int32)
+    position_all = facts[:, 0] * 64 + facts[:, 1]
+    route_all = facts[:, 2 : 2 + routes.shape[2]]
 
     bias_here = lax.dynamic_slice_in_dim(
         qkv_bias.reshape(3, parts, HEAD_DIM), place, 1, 1
     ).reshape(1, 3 * HEAD_DIM)
     qkv = (
-        dot_nn(xn1[:, :half], qkv_m)
-        + dot_nn(xn1[:, half:], qkv_o)
+        dot_nn(xn1, qkv_w)
         + bias_here.astype(jnp.float32)
     )
     cosine, sine_part = rope_tables(position_all)
@@ -671,12 +1679,16 @@
     attended = (dot_nn(weights.astype(bf16), value) / row_sum).astype(bf16)
     lse = row_max + jnp.log(row_sum)
 
-    head_part = jnp.concatenate([dot_nn(attended, out_m), dot_nn(attended, out_o)], 1)
-    hidden = token_own + sum_rows(head_part.astype(bf16)).astype(jnp.float32)
+    head_part = dot_nn(attended, out_w).astype(bf16)
+    head_sum, down_w = sum_and_move(head_part, shared_w_down, expert_down, 2)
+    hidden = token_own + head_sum
     inverse2 = lax.rsqrt(jnp.mean(hidden * hidden, -1, keepdims=True) + EPSILON)
     normed2 = hidden * inverse2
     xn2_own = (normed2 * gain2).astype(bf16)
-    xn2 = share_rows(xn2_own)
+    both, up_w = share_and_move(
+        jnp.concatenate([xn2_own, grad_own_b], 1), shared_w_gate, shared_w_up, expert_gate, expert_up, 3
+    )
+    xn2, grad_all = both[:, :width], both[:, width:]
 
     router_here = own_half_first(router_weight.T).T
     gate_here = own_half_first(shared_gate)
@@ -694,38 +1706,14 @@
     gates_here = lax.dynamic_slice_in_dim(gates_all, group * local_experts, local_experts, 1)
     coefs = jnp.concatenate([sig_all[:, None], gates_here], 1)
 
-    up_vals = dot_nn(xn2[:, :half], up_m) + dot_nn(xn2[:, half:], up_o)
-    g_vals, u_vals = up_vals[:, :span], up_vals[:, span:]
-    sig_g = jax.nn.sigmoid(g_vals)
-    silu_g = g_vals * sig_g
-    act = silu_g * u_vals
-    coef_wide = jnp.repeat(coefs, hidden_here, axis=1, total_repeat_length=span)
-    act_c = (act * coef_wide).astype(bf16)
-    raw = dot_nt(grad_all[:, :half], down_m) + dot_nt(grad_all[:, half:], down_o)
-    dots = jnp.sum((raw * act).reshape(length, stacks, hidden_here), -1)
-    dact = raw * coef_wide
-    dg = (dact * u_vals * (sig_g * (1.0 + g_vals * (1.0 - sig_g)))).astype(bf16)
-    du = (dact * silu_g).astype(bf16)
-    dup = jnp.concatenate([dg, du], 1)
-    branch_part = jnp.concatenate([dot_nn(act_c, down_m), dot_nn(act_c, down_o)], 1)
-    dxn2_part = jnp.concatenate([dot_nt(dup, up_m), dot_nt(dup, up_o)], 1)
-    dots_wide = jnp.concatenate(
-        [
-            lax.dynamic_update_slice_in_dim(
-                jnp.zeros((length, expert_count), jnp.float32),
-                dots[:, 1:],
-                group * local_experts,
-                1,
-            ),
-            dots[:, :1],
-        ],
-        1,
-    )
-    dxn2_sum = sum_rows(dxn2_part.astype(bf16)).astype(jnp.float32)
-    dots_own = sum_rows(dots_wide)
-    branch = sum_rows(branch_part.astype(bf16)).astype(jnp.float32)
-    block_own = own_half_first((hidden + branch).astype(bf16))
-    block_out = lax.all_gather(block_own, "experts", axis=0, tiled=True)
+    coefs = jnp.pad(coefs, ((0, 0), (0, 128 - stacks)))
+    send4, branch_part, dup, act_c = hidden_units(both, up_w, down_w, coefs, shared_w_gate.shape[1])
+    up_g = dot_tn(xn2, dup).astype(bf16)
+    down_g = dot_tn(act_c, grad_all).astype(bf16)
+    send4, up_g, down_g = lax.optimization_barrier((send4, up_g, down_g))
+    up_grads, down_grads = [None] * (2 * stacks), [None] * stacks
+    sums, up_grads[0], up_grads[1] = sum_and_return(send4, up_g, 0, 4)
+    dxn2_sum, dots_own = sums[:, :width], sums[:, width:]
 
     row_first = place * rows + first
     prob = lax.dynamic_slice_in_dim(prob_all, row_first, own_rows, 0)
@@ -747,12 +1735,10 @@
     dhidden = grad_own + inverse2 * (
         dscaled2 - normed2 * jnp.mean(dscaled2 * normed2, -1, keepdims=True)
     )
-    dhidden_all = share_rows(dhidden.astype(bf16))
-
-    out_grad_part = dot_tn(attended, dhidden_all)
-    dattended = (
-        dot_nt(dhidden_all[:, :half], out_m) + dot_nt(dhidden_all[:, half:], out_o)
-    ).astype(bf16)
+    dhidden_all, down_grads[0] = share_and_return(dhidden.astype(bf16), down_g, 0, 5)
+
+    out_g = dot_tn(attended, dhidden_all).astype(bf16)
+    dattended = dot_nt(dhidden_all, out_w).astype(bf16)
     delta = jnp.sum(
         dattended.astype(jnp.float32) * attended.astype(jnp.float32), -1, keepdims=True
     )
@@ -772,16 +1758,13 @@
     )
     bias_part = jnp.sum(dqkv, 0)
     dqkv_b = dqkv.astype(bf16)
-    qkv_grad = dot_tn(xn1, dqkv_b)
-    dxn1_part = jnp.concatenate([dot_nt(dqkv_b, qkv_m), dot_nt(dqkv_b, qkv_o)], 1)
-    dxn1 = sum_rows(dxn1_part.astype(bf16)).astype(jnp.float32)
+    qkv_g = dot_tn(xn1, dqkv_b).astype(bf16)
+    dxn1_part = dot_nt(dqkv_b, qkv_w).astype(bf16)
+    dxn1, up_grads[2], up_grads[3] = sum_and_return(dxn1_part, up_g, 1, 6)
     norm1_grad = jnp.sum(dxn1 * normed1, 0)
     dscaled1 = dxn1 * gain1
     tokens_grad_own = dhidden + inverse1 * (
         dscaled1 - normed1 * jnp.mean(dscaled1 * normed1, -1, keepdims=True)
-    )
-    tokens_grad = lax.all_gather(
-        own_half_first(tokens_grad_own), "experts", axis=0, tiled=True
     )
 
     bias_wide = jnp.zeros((group_size, parts, 3 * HEAD_DIM), jnp.float32)
@@ -795,60 +1778,57 @@
             bias_wide.reshape(-1),
         ]
     )
-    small = lax.psum(small, ("dp", "context", "experts"))
+    out_w_grad, qkv_grad, *others, block_out, tokens_grad, small = last_exchange(
+        up_g,
+        down_g,
+        out_g,
+        qkv_g,
+        branch_part,
+        hidden,
+        own_half_first(tokens_grad_own),
+        small.reshape(-1, 128),
+        list(range(2, stacks)),
+        list(range(1, stacks)),
+        7,
+    )
+    small = small.reshape(-1)
+    up_grads[4:] = others[: 2 * (stacks - 2)]
+    down_grads[1:] = others[2 * (stacks - 2) :]
     router_size = width * expert_count
     bias_sum = small[3 * width + router_size :].reshape(group_size, parts, 3, HEAD_DIM)
     bias_grad = jnp.transpose(
         lax.dynamic_slice_in_dim(bias_sum, group, 1, 0)[0], (1, 0, 2)
     ).reshape(3, parts * HEAD_DIM)
 
-    def halves(first_half, second_half):
-        return (first_half + swap_halves(second_half.astype(bf16)).astype(jnp.float32)).astype(bf16)
-
-    down_grad = halves(
-        dot_tn(act_c, grad_all[:, :half]), dot_tn(act_c, grad_all[:, half:])
-    )
-    down_grad = exchange(jnp.transpose(down_grad.reshape(span, parts, block), (1, 0, 2)))
-    down_grad = jnp.transpose(
-        down_grad.reshape(parts, stacks, hidden_here, block), (1, 0, 2, 3)
-    ).reshape(stacks, parts * hidden_here, block).astype(jnp.float32)
-    up_grad = halves(dot_tn(xn2[:, :half], dup), dot_tn(xn2[:, half:], dup))
-    up_grad = exchange(up_grad.reshape(parts, block, 2 * span))
-    up_grad = jnp.transpose(
-        up_grad.reshape(parts, block, 2 * stacks, hidden_here), (2, 1, 0, 3)
-    ).reshape(2 * stacks, block, parts * hidden_here).astype(jnp.float32)
-    out_w_grad = halves(out_grad_part[:, :half], out_grad_part[:, half:])
-    out_w_grad = exchange(
-        jnp.transpose(out_w_grad.reshape(HEAD_DIM, parts, block), (1, 0, 2))
-    ).reshape(parts * HEAD_DIM, block).astype(jnp.float32)
-    qkv_grad = halves(qkv_grad[:half], qkv_grad[half:])
-    qkv_grad = exchange(qkv_grad.reshape(parts, block, 3 * HEAD_DIM))
     qkv_grad = jnp.transpose(
         qkv_grad.reshape(parts, block, 3, HEAD_DIM), (1, 2, 0, 3)
-    ).reshape(block, 3, parts * HEAD_DIM).astype(jnp.float32)
+    ).reshape(block, 3, parts * HEAD_DIM)
+
+    def wide(array):
+        return array.astype(jnp.float32)
 
     return (
         block_out[None],
         tokens_grad[None],
         small[:width],
-        qkv_grad,
+        wide(qkv_grad),
         bias_grad,
-        out_w_grad,
+        wide(out_w_grad),
         small[width : 2 * width],
         small[3 * width : 3 * width + router_size].reshape(width, expert_count),
-        up_grad[1:stacks],
-        up_grad[stacks + 1 :],
-        down_grad[1:],
+        wide(jnp.stack(up_grads[2::2])),
+        wide(jnp.stack(up_grads[3::2])),
+        wide(jnp.stack(down_grads[1:])),
         small[2 * width : 3 * width],
-        up_grad[0],
-        up_grad[stacks],
-        down_grad[0],
+        wide(up_grads[0]),
+        wide(up_grads[1]),
+        wide(down_grads[0]),
     )
 
 
 def plan_of(mesh):
-    one_head_each = mesh.shape["context"] * mesh.shape["experts"] == 16
-    return split_body if one_head_each and mesh.shape["dp"] == 2 else general_body
+    sizes = mesh.shape
+    return split_body if (sizes["dp"], sizes["context"], sizes["experts"]) == (2, 4, 4) else general_body
 
 
 def solution(mesh):

time: 1130 us -> 743 us (0.66)
  Pallas kernels: 0 us -> 613 us
  waiting for transfers between devices: 605 us -> 0 us
  blocking collectives: 154 us -> 0 us
  local copies, waits for them, and re-layouts: 113 us -> 25.1 us
  matrix products: 123 us -> 58.7 us
  starting transfers between devices: 64.3 us -> 0 us
  between operations: 15.7 us -> 1.63 us
    pallas_call x0 -> x8, Pallas kernels: none -> 613 us  [the longest x1 146 us: share_and_move(): comm_call(kernel, number, 'share_and_move', [jax.ShapeDtypeStruct((rows *...]
    reduce_scatter x4 -> x0, waiting for transfers between devices: 176 us -> none  [sum_rows(): lax.psum_scatter(value, ('context', 'experts'), scatter_dimension=0, tile...]
    all_gather x6 -> x0, waiting for transfers between devices: 157 us -> none  [the longest x2 95.3 us: share_rows(): return lax.all_gather(value, ('context', 'experts'), axis=0, tiled=True)]
    ppermute x8 -> x0, waiting for transfers between devices: 121 us -> none  [swap_halves(): return lax.ppermute(value, 'dp', [(0, 1), (1, 0)])]
    all_gather x2 -> x0, blocking collectives: 113 us -> none  [the longest x1 94.8 us: split_body(): route_all = lax.all_gather(routes[0], 'context', axis=0, tiled=True)]
    all_to_all x7 -> x0, waiting for transfers between devices: 62 us -> none  [exchange(): lax.all_to_all(value, 'context', split_axis=0, concat_axis=0, tiled=True)]
    psum x1 -> x0, waiting for transfers between devices: 58.7 us -> none  [split_body(): small = lax.psum(small, ('dp', 'context', 'experts'))]
    all_to_all x7 -> x0, starting transfers between devices: 56.3 us -> none  [exchange(): lax.all_to_all(value, 'context', split_axis=0, concat_axis=0, tiled=True)]
  transfers between devices with their start and end apart: 27 -> 0, of which waited for: 15 -> 0; matrix products, arithmetic and copies ran while one was open for 19% -> 0% of each run, Pallas kernels for 0% -> 0%
where the time goes in v2:
time: 743 us; the launch traced here: 733 us
  Pallas kernels  613 us (83%)
  matrix products  58.7 us (8%)
  other arithmetic  34.4 us (5%)
  local copies, waits for them, and re-layouts  25.1 us (3%)
    pallas_call x1, Pallas kernels, share_and_move(): comm_call(kernel, number, 'share_and_move', [jax.ShapeDtypeStruct((rows *...  146 us
    pallas_call x2, Pallas kernels, sum_and_return(): comm_call(kernel, number, 'sum_and_return', [jax.ShapeDtypeStruct((rows,...  127 us
    pallas_call x1, Pallas kernels, last_exchange(): comm_call(kernel, number, 'last_exchange', out_shape, [IN_PLACE] * (len(o...  120 us
    pallas_call x1, Pallas kernels, sum_and_move(): comm_call(kernel, number, 'sum_and_move', [jax.ShapeDtypeStruct((rows, wi...  88.1 us
    pallas_call x1, Pallas kernels, share_first(): comm_call(kernel, number, 'share_first', [jax.ShapeDtypeStruct((rows * pa...  48.6 us
    pallas_call x1, Pallas kernels, share_and_return(): comm_call(kernel, number, 'share_and_return', [jax.ShapeDtypeStruct((rows...  42.5 us
    pallas_call x1, Pallas kernels, hidden_units(): pl.pallas_call(functools.partial(hidden_kernel, lax.axis_size('context'),...  41.4 us
    dot_general x6, matrix products, dot_tn(): lax.dot_general(left, right, (((0,), (0,)), ((), ())), preferred_element_...  30.7 us

profile of v2, /device:TPU:16, one launch (start us, length us, event | category | flops | bytes accessed | tf_op | source)
XLA Modules:
  0.0 732.9 jit_solution(10446318653669749342)
XLA Ops:
  12.7 48.6 %share_first.1 = (bf16[1024,2176]{1,0:T(8,128)(2,1)}, bf16[2048,384]{1,0:T(8,128)(2,1)}, bf16[128,2048]{1,0:T(8,128)(2,1)}) custom-call(bf16[64,2176]{1,0:T(8,128)(2,1)} %fusion.60.own_ref, bf16[1024,384]{1,0:T(8,128)(2,1)} %copy.103.qkv_ref, bf16[512,256]{1,0:T(8,128)(2,1)} %outw_ref.1), custom_call_target="tpu_custom_call" | custom-call | bytes 180000000 | tf_op jit(solution)/shard_map/share_first/pallas_call | solution.py:1080
  64.4 4.5 fusion.19
  70.6 1.5 copy-done.2
  73.2 3.3 convolution_convert_fusion.3.part_ref
  76.4 88.1 %sum_and_move.1 = (f32[64,2048]{1,0:T(8,128)}, bf16[1152,2048]{1,0:T(8,128)(2,1)}) custom-call(bf16[1024,2048]{1,0:T(8,128)(2,1)} %convolution_convert_fusion.3.part_ref, bf16[1408,256]{1,0:T(8,128)(2,1)} %shared_ref.1, bf16[2,1408,256]{2,1,0:T(8,128)(2,1)} %expert_ref.1), custom_call_target="tpu_custom_call" | custom-call | bytes 180000000 | tf_op jit(solution)/shard_map/sum_and_move/pallas_call | solution.py:1139
  166.8 145.8 %share_and_move.1 = (bf16[1024,4096]{1,0:T(8,128)(2,1)}, bf16[2048,2304]{1,0:T(8,128)(2,1)}) custom-call(bf16[64,4096]{1,0:T(8,128)(2,1)} %pad_maximum_fusion.3.own_ref, bf16[256,1408]{1,0:T(8,128)(2,1)} %sg_ref.1, bf16[256,1408]{1,0:T(8,128)(2,1)} %su_ref.1, bf16[2,256,1408]{2,1,0:T(8,128)(2,1)} %eg_ref.1, bf16[2,256,1408]{2,1,0:T(8,128)(2,1)} %eu_ref.1), custom_call_target="tpu_custom_call" | custom-call | bytes 300000000 | tf_op jit(solution)/shard_map/share_and_move/pallas_call | solution.py:1198
  312.6 3.4 fusion.2
  318.5 41.4 %hidden_units.1 = (bf16[1024,2176]{1,0:T(8,128)(2,1)}, bf16[1024,2048]{1,0:T(8,128)(2,1)}, bf16[1024,2304]{1,0:T(8,128)(2,1)}, bf16[1024,1152]{1,0:T(8,128)(2,1)}) custom-call(bf16[1024,4096]{1,0:T(8,128)(2,1)} %get-tuple-element.50.both_ref, bf16[2048,2304]{1,0:T(8,128)(2,1)} %get-tuple-element.51.wgu_ref, bf16[1152,2048]{1,0:T(8,128)(2,1)} %get-tuple-element.52.wd_ref, ...), custom_call_target="tpu_custom_call" | custom-call | flops 28991029248 | bytes 40000000 | tf_op jit(solution)/shard_map/hidden_units/pallas_call | solution.py:1579
  359.9 9.2 %convolution_convert_fusion.1.grads_ref.downg_ref = bf16[1152,2048]{1,0:T(8,128)(2,1)} fusion(bf16[1024,1152]{1,0:T(8,128)(2,1)} %get-tuple-element.55, bf16[1024,4096]{1,0:T(8,128)(2,1)} %get-tuple-element.50.both_ref), kind=kOutput, calls=%fused_computation.1 | convolution fusion | flops 4834197504 | bytes 11272192 | tf_op jit(solution)/shard_map/dot_general | solution.py:558
  369.1 14.9 %convolution_convert_fusion.grads_ref.upg_ref = bf16[2048,2304]{1,0:T(8,128)(2,1)} fusion(bf16[1024,2304]{1,0:T(8,128)(2,1)S(1)} %copy-done.20, bf16[1024,4096]{1,0:T(8,128)(2,1)} %get-tuple-element.50.both_ref), kind=kOutput, calls=%fused_computation | convolution fusion | flops 9668395008 | bytes 18350080 | tf_op jit(solution)/shard_map/dot_general | solution.py:558
  384.0 57.7 %sum_and_return.2 = (f32[64,2176]{1,0:T(8,128)}, bf16[256,1408]{1,0:T(8,128)(2,1)}, bf16[256,1408]{1,0:T(8,128)(2,1)}) custom-call(bf16[1024,2176]{1,0:T(8,128)(2,1)} %get-tuple-element.58.part_ref, bf16[2048,2304]{1,0:T(8,128)(2,1)} %convolution_convert_fusion.grads_ref.upg_ref), custom_call_target="tpu_custom_call" | custom-call | bytes 250000000 | tf_op jit(solution)/shard_map/sum_and_return/pallas_call | solution.py:1280
  445.0 1.7 multiply_reduce_fusion
  449.7 2.4 convert_element_type.170
  452.1 42.5 %share_and_return.1 = (bf16[1024,2048]{1,0:T(8,128)(2,1)}, bf16[1408,256]{1,0:T(8,128)(2,1)}) custom-call(bf16[64,2048]{1,0:T(8,128)(2,1)} %fusion.90.own_ref, bf16[1152,2048]{1,0:T(8,128)(2,1)} %convolution_convert_fusion.1.grads_ref.downg_ref), custom_call_target="tpu_custom_call" | custom-call | bytes 180000000 | tf_op jit(solution)/shard_map/share_and_return/pallas_call | solution.py:1317
  494.6 3.9 multiply_reduce_fusion.1
  498.5 1.5 convolution_convert_fusion.4.outg_ref
  500.8 2.0 multiply_convert_fusion
  506.3 3.5 fusion.11.qkvg_ref
  510.1 2.3 convert_element_type.171
  512.4 6.0 convolution_convert_fusion.2.part_ref
  518.4 69.4 %sum_and_return.3 = (f32[64,2048]{1,0:T(8,128)}, bf16[256,1408]{1,0:T(8,128)(2,1)}, bf16[256,1408]{1,0:T(8,128)(2,1)}) custom-call(bf16[1024,2048]{1,0:T(8,128)(2,1)} %convolution_convert_fusion.2.part_ref, bf16[2048,2304]{1,0:T(8,128)(2,1)} %convolution_convert_fusion.grads_ref.upg_ref), custom_call_target="tpu_custom_call" | custom-call | bytes 250000000 | tf_op jit(solution)/shard_map/sum_and_return/pallas_call | solution.py:1280
  587.8 1.3 fusion.40
  589.2 1.4 fusion.39
  591.6 119.7 %last_exchange.1 = (bf16[512,256]{1,0:T(8,128)(2,1)}, bf16[1024,384]{1,0:T(8,128)(2,1)}, bf16[256,1408]{1,0:T(8,128)(2,1)}, bf16[256,1408]{1,0:T(8,128)(2,1)}, b...) custom-call(bf16[2048,2304]{1,0:T(8,128)(2,1)} %convolution_convert_, ...), custom_call_target="tpu_custom_call" | custom-call | bytes 300000000 | tf_op jit(solution)/shard_map/last_exchange/pallas_call | solution.py:1515
  712.7 1.3 slice_bitcast_fusion
  714.8 1.8 convert_element_type.165
  718.1 1.4 copy.114
  720.6 1.6 copy.117
  722.2 3.2 maximum_convert_fusion
  725.4 3.2 maximum_convert_fusion.1
  728.6 1.8 maximum_convert_fusion.2
  731.3 1.3 copy.137
  (146 shorter events, 39.7 us)
Async XLA Ops:
  0.6 9.8 %copy-start.11 = (bf16[256,3,512]{2,0,1:T(8,128)(2,1)S(1)}, bf16[256,3,512]{2,0,1:T(8,128)(2,1)}, u32[]{:S(2)}) copy-start(bf16[256,3,512]{2,0,1:T(8,128)(2,1)} %param.22) | copy-start | bytes 2359300
  68.9 1.7 copy-start.4
  69.3 1.3 copy-start.6
  69.3 1.3 copy-start.9
  70.1 2.0 copy-start.2
  72.1 1.0 copy-start.15
  165.8 423.3 %copy-start = (f32[64,2048]{1,0:T(8,128)}, f32[64,2048]{1,0:T(8,128)S(1)}, u32[]{:S(2)}) copy-start(f32[64,2048]{1,0:T(8,128)S(1)} %get-tuple-element.174.hidden_ref) | copy-start | bytes 1572868
  359.9 9.2 %copy-start.20 = (bf16[1024,2304]{1,0:T(8,128)(2,1)S(1)}, bf16[1024,2304]{1,0:T(8,128)(2,1)}, u32[]{:S(2)}) copy-start(bf16[1024,2304]{1,0:T(8,128)(2,1)} %get-tuple-element.54) | copy-start | bytes 14155780
  384.0 61.0 %copy-start.19 = (bf16[2048,8]{0,1:T(8,128)(2,1)S(1)}, bf16[2048,8]{0,1:T(8,128)(2,1)}, u32[]{:S(2)}) copy-start(bf16[2048,8]{0,1:T(8,128)(2,1)} %param.26) | copy-start | bytes 98308
  441.7 5.9 copy-start.12
  449.7 44.9 %copy-start.16 = (bf16[128,2048]{1,0:T(8,128)(2,1)S(1)}, bf16[128,2048]{1,0:T(8,128)(2,1)}, u32[]{:S(2)}) copy-start(bf16[128,2048]{1,0:T(8,128)(2,1)} %get-tuple-element.48) | copy-start | bytes 1572868
  494.6 3.9 copy-start.1
  498.4 2.4 copy-start.3
  502.8 1.0 copy-start.10
  502.8 1.8 copy-start.7
  503.7 6.1 copy-start.17
  503.8 2.4 slice-start
  504.6 1.7 slice-start.1
  590.6 0.9 copy-start.18
  722.2 6.4 copy-start.13
  722.2 6.4 copy-start.14
  725.4 5.0 copy-start.8
  728.6 2.7 copy-start.5

commit v3 on v2

--- a/solution.py
+++ b/solution.py
@@ -897,10 +897,13 @@
         self.on(number, s.place, src(s.place)).start()
         self.local(number).start()
 
+    def send_gap(self, number, gap):
+        s = self.spot
+        s.others(gap, lambda target: self.to(number, target, s.place).start())
+
     def send(self, number):
-        s = self.spot
-        for gap in range(s.parts - 1, 0, -1):
-            s.others(gap, lambda target: self.to(number, target, s.place).start())
+        for gap in range(self.spot.parts - 1, 0, -1):
+            self.send_gap(number, gap)
 
     def forward(self, number, gap):
         s, (_, dst) = self.spot, self.items[number]
@@ -911,16 +914,26 @@
 
         s.others(gap, one)
 
-    def end(self):
+    def ready(self, number):
+        s, (_, dst) = self.spot, self.items[number]
+        self.local(number).wait()
+        for part in range(s.parts):
+            self.on(number, part, dst(0, part)).wait_recv()
+
+    def sent(self):
         s = self.spot
-        for number, (src, dst) in enumerate(self.items):
-            self.local(number).wait()
+        for number, (_, dst) in enumerate(self.items):
             for part in range(s.parts):
-                self.on(number, part, dst(0, part)).wait()
+                self.on(number, part, dst(0, part)).wait_send()
 
                 @pl.when(part != s.place)
                 def _():
                     self.to(number, part, s.place).wait_send()
+
+    def end(self):
+        for number in range(len(self.items)):
+            self.ready(number)
+        self.sent()
 
 
 class Return:
@@ -1038,16 +1051,50 @@
     return jnp.minimum(index * WINDOW, length - WINDOW)
 
 
-def share_first(value, qkv_in, out_weight, number):
+def turn(value, cosine, sine_part):
+    return value * cosine + pltpu.roll(value, HEAD_DIM // 2, 1) * sine_part
+
+
+def turn_tables(facts):
+    both = facts[:, :HEAD_DIM].astype(jnp.float32) + facts[:, HEAD_DIM:].astype(jnp.float32)
+    swapped = pltpu.roll(both, HEAD_DIM // 2, 1)
+    low = lax.broadcasted_iota(jnp.int32, (1, HEAD_DIM), 1) < HEAD_DIM // 2
+    return jnp.where(low, both, swapped), jnp.where(low, -swapped, both)
+
+
+def attention_first(value, qkv_in, out_weight, bias, shared_down, expert_down, number):
     parts = lax.axis_size("context")
-    rows, width = value.shape
+    rows, wide = value.shape
     block, span = qkv_in.shape[0] // parts, qkv_in.shape[1]
     head, lanes = out_weight.shape[0] // parts, out_weight.shape[1]
-    share_sems, move_sems = Share.sems(parts), Move.sems(2, parts)
-
-    def kernel(own_ref, qkv_ref, outw_ref, all_ref, wqkv_ref, wout_ref, *sems):
+    width, length = 2 * parts * lanes, rows * parts * 4
+    units = shared_down.shape[0]
+    count = 1 + expert_down.shape[0]
+    step = 256
+    scale = HEAD_DIM ** (-0.5)
+    f32, bf16 = jnp.float32, jnp.bfloat16
+    sets = [
+        [
+            pltpu.VMEM((length, wide), bf16),
+            pltpu.VMEM((2 * parts * block, span), bf16),
+            pltpu.VMEM((head, width), bf16),
+            pltpu.VMEM((length, width), bf16),
+            DMA((3,)),
+        ],
+        Share.sems(parts),
+        Move.sems(2 + count, parts),
+        Sum.scratch(parts, rows, width),
+    ]
+
+    def kernel(own_ref, qkv_ref, outw_ref, bias_ref, shared_ref, expert_ref,
+               all_hbm, wqkv_hbm, wout_hbm, wd_ref, q_ref, k_ref, v_ref, att_ref, lse_ref, sum_ref, *scratch):
+        scratch, split = list(scratch), []
+        for one in sets:
+            split.append(scratch[: len(one)])
+            scratch = scratch[len(one) :]
+        all_ref, wqkv_ref, wout_ref, part_ref, keep = split[0]
         spot = Spot()
-        share = Share(spot, own_ref, all_ref, sems[: len(share_sems)])
+        share = Share(spot, own_ref, all_ref, split[1])
         items = [
             (
                 lambda target: rows_at(qkv_ref, target * block, block),
@@ -1058,156 +1105,294 @@
                 lambda side, source: lanes_at(wout_ref, (side * parts + source) * lanes, lanes),
             ),
         ]
-        move = Move(spot, items, sems[len(share_sems) :])
-        spot.greet(True, True)
-        share.begin()
-        for item in range(2):
-            move.own(item)
-        move.send(0)
-        share.step(1)
-        move.send(1)
-        move.forward(0, 1)
-        share.step(2)
-        move.forward(0, 2)
-        share.step(3)
-        move.forward(0, 3)
-        for gap in (1, 2, 3):
-            move.forward(1, gap)
-        share.end()
-        move.end()
-
-    bf16 = jnp.bfloat16
-    return comm_call(
-        kernel,
-        number,
-        "share_first",
-        [
-            jax.ShapeDtypeStruct((rows * parts * 4, width), value.dtype),
-            jax.ShapeDtypeStruct((2 * parts * block, span), bf16),
-            jax.ShapeDtypeStruct((head, 2 * parts * lanes), bf16),
-        ],
-        [IN_PLACE] * 3,
-        [IN_VMEM, IN_PLACE, IN_PLACE],
-        share_sems + move_sems,
-        180_000_000,
-    )(value, qkv_in, out_weight)
-
-
-def sum_and_move(value, shared_down, expert_down, number):
-    parts = lax.axis_size("context")
-    total, width = value.shape
-    rows = total // (4 * parts)
-    hidden, lanes = shared_down.shape
-    count = 1 + expert_down.shape[0]
-    sum_scratch, move_sems = Sum.scratch(parts, rows, width), Move.sems(count, parts)
-
-    def kernel(part_ref, shared_ref, expert_ref, out_ref, wd_ref, *scratch):
-        spot = Spot()
-        summed = Sum(spot, part_ref, out_ref, scratch[: len(sum_scratch)])
-
-        def item(k):
+
+        def down(k):
             ref = shared_ref if k == 0 else expert_ref.at[k - 1]
             return (
-                lambda target: rows_at(ref, window_of(target, hidden), WINDOW),
+                lambda target: rows_at(ref, window_of(target, units), WINDOW),
                 lambda side, source: wd_ref.at[
                     pl.ds(k * WINDOW, WINDOW),
                     pl.ds(pl.multiple_of((side * parts + source) * lanes, lanes), lanes),
                 ],
             )
 
-        move = Move(spot, [item(k) for k in range(count)], scratch[len(sum_scratch) :])
+        move = Move(spot, items + [down(k) for k in range(count)], split[2])
+        summed = Sum(spot, part_ref, sum_ref, split[3])
+        copies = [
+            pltpu.make_async_copy(source, target, keep.at[index])
+            for index, (source, target) in enumerate(((all_ref, all_hbm), (wqkv_ref, wqkv_hbm), (wout_ref, wout_hbm)))
+        ]
+
+        def project(index, carry):
+            at = pl.ds(pl.multiple_of(index * step, step), step)
+            qkv = jnp.dot(all_ref[at, :width], wqkv_ref[...], preferred_element_type=f32) + bias_ref[...]
+            cosine, sine_part = turn_tables(all_ref[at, width:])
+            q_ref[at, :] = turn(qkv[:, :HEAD_DIM], cosine, sine_part).astype(bf16)
+            k_ref[at, :] = turn(qkv[:, HEAD_DIM : 2 * HEAD_DIM], cosine, sine_part).astype(bf16)
+            v_ref[at, :] = qkv[:, 2 * HEAD_DIM :].astype(bf16)
+            return carry
+
+        def attend(index, carry):
+            start = pl.multiple_of(index * step, step)
+            at = pl.ds(start, step)
+            scores = dot_nt(q_ref[at, :], k_ref[...]) * scale
+            query_index = start + lax.broadcasted_iota(jnp.int32, scores.shape, 0)
+            allowed = lax.broadcasted_iota(jnp.int32, scores.shape, 1) <= query_index
+            row_max = jnp.max(jnp.where(allowed, scores, MASKED), -1, keepdims=True)
+            weights = jnp.where(allowed, jnp.exp(scores - row_max), 0.0)
+            row_sum = jnp.sum(weights, -1, keepdims=True)
+            attended = (jnp.dot(weights.astype(bf16), v_ref[...], preferred_element_type=f32) / row_sum).astype(bf16)
+            att_ref[at, :] = attended
+            lse_ref[at, :] = jnp.broadcast_to(row_max + jnp.log(row_sum), (step, HEAD_DIM))
+            part_ref[at, :] = jnp.dot(attended, wout_ref[...], preferred_element_type=f32).astype(bf16)
+            return carry
+
         spot.greet(True, True)
+        share.begin()
+        for number in range(len(move.items)):
+            move.own(number)
+        move.send_gap(0, 3)
+        share.step(1)
+        move.send_gap(0, 2)
+        share.step(2)
+        move.send_gap(0, 1)
+        share.step(3)
+        move.send(1)
+        move.send(2)
+        for gap in (1, 2, 3):
+            move.forward(0, gap)
+        for gap in (1, 2, 3):
+            move.forward(1, gap)
+        share.end()
+        copies[0].start()
+        move.ready(0)
+        copies[1].start()
+        lax.fori_loop(0, length // step, project, 0)
+        move.ready(1)
+        copies[2].start()
+        for number in range(3, len(move.items)):
+            move.send(number)
+        lax.fori_loop(0, length // step, attend, 0)
         summed.begin()
-        for k in range(count):
-            move.own(k)
-        move.send(0)
-        move.send(1)
+        for gap in (1, 2, 3):
+            move.forward(2, gap)
         for index in range(parts):
             summed.cross(index)
-        for gap in (1, 2, 3):
-            move.forward(0, gap)
+        for number in range(3, len(move.items)):
+            for gap in (1, 2, 3):
+                move.forward(number, gap)
         for index in range(parts):
             summed.line(index)
-        for k in range(2, count):
-            move.send(k)
-        for k in range(1, count):
-            for gap in (1, 2, 3):
-                move.forward(k, gap)
         summed.end()
-        move.end()
-
+        for number in range(2, len(move.items)):
+            move.ready(number)
+        move.sent()
+        for copy in copies:
+            copy.wait()
+
+    heads = jax.ShapeDtypeStruct((length, HEAD_DIM), bf16)
     return comm_call(
         kernel,
         number,
-        "sum_and_move",
+        "attention_first",
         [
-            jax.ShapeDtypeStruct((rows, width), jnp.float32),
-            jax.ShapeDtypeStruct((count * WINDOW, 2 * parts * lanes), jnp.bfloat16),
+            jax.ShapeDtypeStruct((length, wide), bf16),
+            jax.ShapeDtypeStruct((2 * parts * block, span), bf16),
+            jax.ShapeDtypeStruct((head, width), bf16),
+            jax.ShapeDtypeStruct((count * WINDOW, width), bf16),
+            heads,
+            heads,
+            heads,
+            heads,
+            jax.ShapeDtypeStruct((length, HEAD_DIM), f32),
+            jax.ShapeDtypeStruct((rows, width), f32),
         ],
-        [IN_VMEM, IN_PLACE],
-        [IN_VMEM, IN_PLACE, IN_PLACE],
-        sum_scratch + move_sems,
-        180_000_000,
-    )(value, shared_down, expert_down)
-
-
-def share_and_move(value, shared_gate, shared_up, expert_gate, expert_up, number):
+        [IN_PLACE] * 4 + [IN_VMEM] * 6,
+        [IN_VMEM, IN_PLACE, IN_PLACE, IN_VMEM, IN_PLACE, IN_PLACE],
+        [one for group in sets for one in group],
+        250_000_000,
+    )(value, qkv_in, out_weight, bias, shared_down, expert_down)
+
+
+def share_move_compute(value, shared_gate, shared_up, expert_gate, expert_up, wd, number):
     parts = lax.axis_size("context")
-    rows, width = value.shape
-    block, hidden = shared_gate.shape
+    rows, wide = value.shape
+    width = wd.shape[1]
+    block, units = shared_gate.shape
     stacks = 1 + expert_gate.shape[0]
     count = 2 * stacks
+    length = rows * parts * 4
+    experts = (stacks - 1) * 4
+    step = 256
+    f32, bf16 = jnp.float32, jnp.bfloat16
     share_sems, move_sems = Share.sems(parts), Move.sems(count, parts)
-
-    def kernel(own_ref, sg_ref, su_ref, eg_ref, eu_ref, all_ref, wgu_ref, *sems):
+    scratch = [
+        pltpu.VMEM((length, wide), bf16),
+        pltpu.VMEM((2 * parts * block, count * WINDOW), bf16),
+        pltpu.VMEM(wd.shape, bf16),
+        pltpu.VMEM((length, width), f32),
+        pltpu.VMEM((length, width), f32),
+        pltpu.VMEM((length, 128), f32),
+        pltpu.VMEM((length, stacks * WINDOW), bf16),
+        pltpu.VMEM((length, count * WINDOW), bf16),
+        pltpu.VMEM((2, step, width + 128), bf16),
+        pltpu.VMEM((2, step, width), bf16),
+        DMA((2,)),
+        DMA((stacks,)),
+        DMA((stacks,)),
+        DMA((length // step,)),
+        DMA((length // step,)),
+    ]
+
+    def kernel(own_ref, sg_ref, su_ref, eg_ref, eu_ref, wd_hbm, both_hbm, send_hbm, branch_hbm, dup_hbm, act_hbm, *rest):
+        both, wgu, wd_ref, dx_acc, out_acc, dot_acc, act_ref, dup_ref, send_buf, branch_buf, load, act_s, dup_s, send_s, branch_s = rest[: len(scratch)]
+        sems = rest[len(scratch) :]
         spot = Spot()
-        share = Share(spot, own_ref, all_ref, sems[: len(share_sems)])
+        share = Share(spot, own_ref, both, sems[: len(share_sems)])
 
         def item(number):
             k = number // 2
             shared, expert = (sg_ref, eg_ref) if number % 2 == 0 else (su_ref, eu_ref)
             ref = shared if k == 0 else expert.at[k - 1]
             return (
-                lambda target: lanes_at(ref, window_of(target, hidden), WINDOW),
-                lambda side, source: wgu_ref.at[
+                lambda target: lanes_at(ref, window_of(target, units), WINDOW),
+                lambda side, source: wgu.at[
                     pl.ds(pl.multiple_of((side * parts + source) * block, block), block),
                     pl.ds(number * WINDOW, WINDOW),
                 ],
             )
 
         move = Move(spot, [item(number) for number in range(count)], sems[len(share_sems) :])
+        weights = pltpu.make_async_copy(wd_hbm, wd_ref, load.at[0])
+        keep = pltpu.make_async_copy(both, both_hbm, load.at[1])
+        repeated = jnp.where(spot.place == parts - 1, WINDOW * parts - units, 0)
+        lane = lax.broadcasted_iota(jnp.int32, (1, WINDOW), 1)
+        fresh = jnp.where(lane >= repeated, 1.0, 0.0)
+        column = lax.broadcasted_iota(jnp.int32, (1, 128), 1)
+
+        def send_out(index):
+            at = pl.ds(pl.multiple_of(index * step, step), step)
+            return pltpu.make_async_copy(send_buf.at[lax.rem(index, 2)], send_hbm.at[at, :], send_s.at[index])
+
+        def branch_out(index):
+            at = pl.ds(pl.multiple_of(index * step, step), step)
+            return pltpu.make_async_copy(branch_buf.at[lax.rem(index, 2)], branch_hbm.at[at, :], branch_s.at[index])
+
+        def act_out(k):
+            at = pl.ds(k * WINDOW, WINDOW)
+            return pltpu.make_async_copy(act_ref.at[:, at], act_hbm.at[:, at], act_s.at[k])
+
+        def dup_out(k):
+            at = pl.ds(2 * k * WINDOW, 2 * WINDOW)
+            return pltpu.make_async_copy(dup_ref.at[:, at], dup_hbm.at[:, at], dup_s.at[k])
+
+        def compute(k, first, last):
+            up, down = pl.ds(2 * k * WINDOW, 2 * WINDOW), pl.ds(k * WINDOW, WINDOW)
+            at = experts if k == 0 else spot.group * (stacks - 1) + k - 1
+            here = jnp.where(column == at, 1.0, 0.0)
+            both_parts = jnp.where((column == at) | (column == at + 64), 1.0, 0.0)
+
+            def one(index, carry):
+                rows_here = pl.ds(pl.multiple_of(index * step, step), step)
+                vals = jnp.dot(both[rows_here, :width], wgu[:, up], preferred_element_type=f32)
+                raw = dot_nt(both[rows_here, width : 2 * width], wd_ref[down, :]) * fresh
+                coef = jnp.sum(both[rows_here, 2 * width :].astype(f32) * both_parts, -1, keepdims=True)
+                g_vals, u_vals = vals[:, :WINDOW], vals[:, WINDOW:]
+                sig_g = jax.nn.sigmoid(g_vals)
+                silu_g = g_vals * sig_g
+                act = silu_g * u_vals
+                dots = jnp.sum(raw * act, -1, keepdims=True) * here
+                act_ref[rows_here, down] = (act * (coef * fresh)).astype(bf16)
+                dact = raw * coef
+                dup_ref[rows_here, pl.ds(2 * k * WINDOW, WINDOW)] = (
+                    dact * u_vals * (sig_g * (1.0 + g_vals * (1.0 - sig_g)))
+                ).astype(bf16)
+                dup_ref[rows_here, pl.ds((2 * k + 1) * WINDOW, WINDOW)] = (dact * silu_g).astype(bf16)
+                out_part = jnp.dot(act_ref[rows_here, down], wd_ref[down, :], preferred_element_type=f32)
+                dx_part = dot_nt(dup_ref[rows_here, up], wgu[:, up])
+                if k == 0:
+                    out_acc[rows_here, :] = out_part
+                    dx_acc[rows_here, :] = dx_part
+                    dot_acc[rows_here, :] = dots
+                elif k < stacks - 1:
+                    out_acc[rows_here, :] += out_part
+                    dx_acc[rows_here, :] += dx_part
+                    dot_acc[rows_here, :] += dots
+                else:
+
+                    @pl.when(index >= 2)
+                    def _():
+                        send_out(index - 2).wait()
+                        branch_out(index - 2).wait()
+
+                    slot = lax.rem(index, 2)
+                    branch_buf[slot] = (out_acc[rows_here, :] + out_part).astype(bf16)
+                    send_buf[slot, :, :width] = (dx_acc[rows_here, :] + dx_part).astype(bf16)
+                    send_buf[slot, :, width:] = (dot_acc[rows_here, :] + dots).astype(bf16)
+                    send_out(index).start()
+                    branch_out(index).start()
+                return carry
+
+            lax.fori_loop(first, last, one, 0)
+
+        def forward(number):
+            for gap in (1, 2, 3):
+                move.forward(number, gap)
+
         spot.greet(True, True)
         share.begin()
+        weights.start()
         for number in range(count):
             move.own(number)
         move.send(0)
         share.step(1)
         move.send(1)
         share.step(2)
-        for gap in (1, 2, 3):
-            move.forward(0, gap)
+        forward(0)
         share.step(3)
         for number in range(2, count):
             move.send(number)
-        for number in range(1, count):
-            for gap in (1, 2, 3):
-                move.forward(number, gap)
         share.end()
-        move.end()
+        keep.start()
+        forward(1)
+        weights.wait()
+        pieces = length // step
+        for k in range(stacks):
+            if k < stacks - 1:
+                forward(2 * k + 2)
+            move.ready(2 * k)
+            move.ready(2 * k + 1)
+            compute(k, 0, pieces // 2)
+            if k < stacks - 1:
+                forward(2 * k + 3)
+            compute(k, pieces // 2, pieces)
+            act_out(k).start()
+            dup_out(k).start()
+        for index in (pieces - 2, pieces - 1):
+            send_out(index).wait()
+            branch_out(index).wait()
+        for k in range(stacks):
+            act_out(k).wait()
+            dup_out(k).wait()
+        keep.wait()
+        move.sent()
 
     return comm_call(
         kernel,
         number,
-        "share_and_move",
+        "share_move_compute",
         [
-            jax.ShapeDtypeStruct((rows * parts * 4, width), value.dtype),
-            jax.ShapeDtypeStruct((2 * parts * block, count * WINDOW), jnp.bfloat16),
+            jax.ShapeDtypeStruct((length, wide), bf16),
+            jax.ShapeDtypeStruct((length, width + 128), bf16),
+            jax.ShapeDtypeStruct((length, width), bf16),
+            jax.ShapeDtypeStruct((length, count * WINDOW), bf16),
+            jax.ShapeDtypeStruct((length, stacks * WINDOW), bf16),
         ],
-        [IN_PLACE] * 2,
-        [IN_VMEM] + [IN_PLACE] * 4,
-        share_sems + move_sems,
+        [IN_PLACE] * 5,
+        [IN_VMEM] + [IN_PLACE] * 5,
+        scratch + share_sems + move_sems,
         300_000_000,
-    )(value, shared_gate, shared_up, expert_gate, expert_up)
+    )(value, shared_gate, shared_up, expert_gate, expert_up, wd)
 
 
 def up_item(grads_ref, k, gate_ref, up_ref, block, parts):
@@ -1246,87 +1431,165 @@
     }
 
 
-def sum_and_return(value, up_grads, k, number):
+def attention_last(send4, up_grads, down_grads, hidden, grad, gain, chances, named, router, out_w, qkv_w, heads, lse, turns, number):
     parts = lax.axis_size("context")
-    total, width = value.shape
-    rows = total // (4 * parts)
+    length, width = send4.shape[0], hidden.shape[1]
+    rows, wide = hidden.shape[0], send4.shape[1]
     block = up_grads.shape[0] // (2 * parts)
-    hidden = WINDOW * parts - 128
-    sum_scratch = Sum.scratch(parts, rows, width)
-    back_scratch = Return.scratch([(block, 2 * WINDOW)], [2], parts)
-
-    def kernel(part_ref, grads_ref, out_ref, gate_ref, up_ref, *scratch):
+    lanes = down_grads.shape[1] // (2 * parts)
+    units = WINDOW * parts - 128
+    step = 256
+    experts = 8
+    scale = HEAD_DIM ** (-0.5)
+    f32, bf16 = jnp.float32, jnp.bfloat16
+    shapes, pieces = [(block, 2 * WINDOW), (WINDOW, lanes)], [2, 1]
+    sets = [
+        [
+            pltpu.VMEM((rows, wide), f32),
+            pltpu.VMEM((rows, width), bf16),
+            pltpu.VMEM((length, width), bf16),
+            pltpu.VMEM((length, width), bf16),
+            pltpu.VMEM((length, HEAD_DIM), bf16),
+            pltpu.VMEM((length, HEAD_DIM), f32),
+            pltpu.VMEM((length, HEAD_DIM), f32),
+            pltpu.VMEM((length, HEAD_DIM), f32),
+            DMA,
+        ],
+        Sum.scratch(parts, rows, wide),
+        Share.sems(parts),
+        Sum.scratch(parts, rows, width),
+        Return.scratch(shapes, pieces, parts),
+    ]
+
+    def kernel(send_ref, upg_ref, downg_ref, hidden_ref, grad_ref, gain_ref, chance_ref, named_ref, router_ref, wout_ref, wqkv_ref,
+               q_ref, k_ref, v_ref, att_ref, lse_ref, turn_ref,
+               dh_hbm, gate_out, up_out, down_out, dots_ref, dxn2_ref, dhidden_ref, dqkv_ref, bias_ref, dxn1_ref, *scratch):
+        scratch, split = list(scratch), []
+        for one in sets:
+            split.append(scratch[: len(one)])
+            scratch = scratch[len(one) :]
+        sums, dh_own, dh_all, part_ref, datt_ref, dq_acc, dk_acc, dv_acc, keep_sem = split[0]
         spot = Spot()
-        summed = Sum(spot, part_ref, out_ref, scratch[: len(sum_scratch)])
-        got, mine, *sems = scratch[len(sum_scratch) :]
-        back = Return(spot, [up_item(grads_ref, k, gate_ref, up_ref, block, parts)], [got], [mine], sems)
+        first = Sum(spot, send_ref, sums, split[1])
+        share = Share(spot, dh_own, dh_all, split[2])
+        second = Sum(spot, part_ref, dxn1_ref, split[3])
+        items = [up_item(upg_ref, 0, gate_out, up_out, block, parts), down_item(downg_ref, 0, down_out, parts)]
+        back = Return(spot, items, split[4][:2], split[4][2:4], split[4][4:])
+        keep = pltpu.make_async_copy(dh_all, dh_hbm, keep_sem)
+
+        def owner():
+            lane = lax.broadcasted_iota(jnp.int32, (rows, 128), 1)
+            dots = sums[:, width:]
+            dots_ref[...] = dots
+            chance = chance_ref[...]
+            dprob = dots * named_ref[...]
+            prob = jnp.where(lane < experts, chance, 0.0)
+            dlogit = prob * (dprob - jnp.sum(prob * dprob, -1, keepdims=True))
+            mix = jnp.where(lane < experts, dlogit, jnp.where(lane == experts, chance * (1.0 - chance) * dots, 0.0))
+            dxn2_ref[...] = jnp.dot(mix, router_ref[...], precision=PRECISE, preferred_element_type=f32)
+
+            def one(index, carry):
+                at = pl.ds(pl.multiple_of(index * 16, 16), 16)
+                dxn2 = dxn2_ref[at, :] + sums[at, :width]
+                dxn2_ref[at, :] = dxn2
+                value = hidden_ref[at, :]
+                inverse = lax.rsqrt(jnp.mean(value * value, -1, keepdims=True) + EPSILON)
+                normed = value * inverse
+                scaled = dxn2 * gain_ref[...]
+                dhidden = grad_ref[at, :].astype(f32) + inverse * (scaled - normed * jnp.mean(scaled * normed, -1, keepdims=True))
+                dhidden_ref[at, :] = dhidden
+                dh_own[at, :] = dhidden.astype(bf16)
+                return carry
+
+            lax.fori_loop(0, rows // 16, one, 0)
+
+        def attend(index, carry):
+            start = pl.multiple_of(index * step, step)
+            at = pl.ds(start, step)
+            datt = dot_nt(dh_all[at, :], wout_ref[...]).astype(bf16)
+            delta = jnp.sum(datt.astype(f32) * att_ref[at, :].astype(f32), -1, keepdims=True)
+            scores = dot_nt(q_ref[at, :], k_ref[...]) * scale
+            query_index = start + lax.broadcasted_iota(jnp.int32, scores.shape, 0)
+            allowed = lax.broadcasted_iota(jnp.int32, scores.shape, 1) <= query_index
+            prob = jnp.where(allowed, jnp.exp(scores - lse_ref[at, :1]), 0.0)
+            dscore = (prob * (dot_nt(datt, v_ref[...]) - delta)).astype(bf16)
+            dq_acc[at, :] = jnp.dot(dscore, k_ref[...], preferred_element_type=f32) * scale
+            dk_acc[...] += dot_tn(dscore, q_ref[at, :])
+            dv_acc[...] += dot_tn(prob.astype(bf16), datt)
+            return carry
+
+        def project(index, carry):
+            at = pl.ds(pl.multiple_of(index * step, step), step)
+            cosine, sine_part = turn_tables(turn_ref[at, :])
+            dq, dk, dv = dq_acc[at, :], dk_acc[at, :] * scale, dv_acc[at, :]
+            dq = dq * cosine - pltpu.roll(dq, HEAD_DIM // 2, 1) * sine_part
+            dk = dk * cosine - pltpu.roll(dk, HEAD_DIM // 2, 1) * sine_part
+            for which, value in enumerate((dq, dk, dv)):
+                bias_ref[:, pl.ds(which * HEAD_DIM, HEAD_DIM)] += jnp.sum(value, 0, keepdims=True)
+                dqkv_ref[at, pl.ds(which * HEAD_DIM, HEAD_DIM)] = value.astype(bf16)
+            part_ref[at, :] = dot_nt(dqkv_ref[at, :], wqkv_ref[...]).astype(bf16)
+            return carry
+
         spot.greet(True, True)
-        summed.begin()
+        first.begin()
         back.start(0)
+        back.start(1)
+        dk_acc[...] = jnp.zeros_like(dk_acc)
+        dv_acc[...] = jnp.zeros_like(dv_acc)
+        bias_ref[...] = jnp.zeros_like(bias_ref)
         for index in range(parts):
-            summed.cross(index)
+            first.cross(index)
         back.reduce(0, 0)
         back.reduce(0, 1)
-        summed.line(0)
-        summed.line(1)
+        for index in range(parts):
+            first.line(index)
+        owner()
+        share.begin()
+        share.step(1)
+        share.step(2)
         back.reduce(0, 2)
+        share.step(3)
         back.reduce(0, 3)
-        summed.line(2)
-        summed.line(3)
-        summed.end()
+        share.end()
+        keep.start()
+        back.reduce(1, 0)
+        back.reduce(1, 1)
+        lax.fori_loop(0, length // step, attend, 0)
+        lax.fori_loop(0, length // step, project, 0)
+        second.begin()
+        back.reduce(1, 2)
+        for index in range(parts):
+            second.cross(index)
+        back.reduce(1, 3)
+        for index in range(parts):
+            second.line(index)
+        first.end()
+        second.end()
         back.end()
-
-    piece = jax.ShapeDtypeStruct((block, hidden), jnp.bfloat16)
+        keep.wait()
+
+    piece = jax.ShapeDtypeStruct((block, units), bf16)
     return comm_call(
         kernel,
         number,
-        "sum_and_return",
-        [jax.ShapeDtypeStruct((rows, width), jnp.float32), piece, piece],
-        [IN_VMEM, IN_PLACE, IN_PLACE],
-        [IN_VMEM, IN_PLACE],
-        sum_scratch + back_scratch,
+        "attention_last",
+        [
+            jax.ShapeDtypeStruct((length, width), bf16),
+            piece,
+            piece,
+            jax.ShapeDtypeStruct((units, lanes), bf16),
+            jax.ShapeDtypeStruct((rows, 128), f32),
+            jax.ShapeDtypeStruct((rows, width), f32),
+            jax.ShapeDtypeStruct((rows, width), f32),
+            jax.ShapeDtypeStruct((length, 3 * HEAD_DIM), bf16),
+            jax.ShapeDtypeStruct((1, 3 * HEAD_DIM), f32),
+            jax.ShapeDtypeStruct((rows, width), f32),
+        ],
+        [IN_PLACE] * 4 + [IN_VMEM] * 6,
+        [IN_VMEM, IN_PLACE, IN_PLACE] + [IN_VMEM] * 14,
+        [one for group in sets for one in group],
         250_000_000,
-    )(value, up_grads)
-
-
-def share_and_return(value, down_grads, k, number):
-    parts = lax.axis_size("context")
-    rows, width = value.shape
-    lanes = down_grads.shape[1] // (2 * parts)
-    hidden = WINDOW * parts - 128
-    share_sems = Share.sems(parts)
-    back_scratch = Return.scratch([(WINDOW, lanes)], [1], parts)
-
-    def kernel(own_ref, grads_ref, all_ref, down_ref, *scratch):
-        spot = Spot()
-        share = Share(spot, own_ref, all_ref, scratch[: len(share_sems)])
-        got, mine, *sems = scratch[len(share_sems) :]
-        back = Return(spot, [down_item(grads_ref, k, down_ref, parts)], [got], [mine], sems)
-        spot.greet(True, True)
-        share.begin()
-        back.start(0)
-        share.step(1)
-        share.step(2)
-        back.reduce(0, 0)
-        share.step(3)
-        for index in range(1, parts):
-            back.reduce(0, index)
-        share.end()
-        back.end()
-
-    return comm_call(
-        kernel,
-        number,
-        "share_and_return",
-        [
-            jax.ShapeDtypeStruct((rows * parts * 4, width), value.dtype),
-            jax.ShapeDtypeStruct((hidden, lanes), jnp.bfloat16),
-        ],
-        [IN_PLACE, IN_PLACE],
-        [IN_VMEM, IN_PLACE],
-        share_sems + back_scratch,
-        180_000_000,
-    )(value, down_grads)
+    )(send4, up_grads, down_grads, hidden, grad, gain, chances, named, router, out_w, qkv_w, *heads, lse, turns)
 
 
 class Group:
@@ -1524,81 +1787,6 @@
     )(up_grads, down_grads, out_grads, qkv_grads, branch, hidden, tokens_grad, small)
 
 
-def hidden_kernel(parts, stacks, units, both_ref, wgu_ref, wd_ref, coef_ref, send_ref, branch_ref, dup_ref, act_ref, dx_acc, out_acc, dot_acc):
-    width = branch_ref.shape[1]
-    f32, bf16 = jnp.float32, jnp.bfloat16
-    repeated = jnp.where(lax.axis_index("context") == parts - 1, WINDOW * parts - units, 0)
-    lane = lax.broadcasted_iota(jnp.int32, (1, WINDOW), 1)
-    fresh = jnp.where(lane >= repeated, 1.0, 0.0)
-    group = lax.axis_index("experts")
-    column = lax.broadcasted_iota(jnp.int32, (1, 128), 1)
-    dot_acc[...] = jnp.zeros_like(dot_acc)
-    for k in range(stacks):
-        up = pl.ds(2 * k * WINDOW, 2 * WINDOW)
-        down = pl.ds(k * WINDOW, WINDOW)
-        vals = jnp.dot(both_ref[:, :width], wgu_ref[:, up], preferred_element_type=f32)
-        raw = dot_nt(both_ref[:, width:], wd_ref[down, :]) * fresh
-        g_vals, u_vals = vals[:, :WINDOW], vals[:, WINDOW:]
-        sig_g = jax.nn.sigmoid(g_vals)
-        silu_g = g_vals * sig_g
-        act = silu_g * u_vals
-        coef = coef_ref[:, k : k + 1]
-        at = (stacks - 1) * 4 if k == 0 else group * (stacks - 1) + k - 1
-        dots = jnp.sum(raw * act, -1, keepdims=True)
-        dot_acc[...] += dots * jnp.where(column == at, 1.0, 0.0)
-        act_ref[:, down] = (act * (coef * fresh)).astype(bf16)
-        dact = raw * coef
-        dup_ref[:, pl.ds(2 * k * WINDOW, WINDOW)] = (dact * u_vals * (sig_g * (1.0 + g_vals * (1.0 - sig_g)))).astype(bf16)
-        dup_ref[:, pl.ds((2 * k + 1) * WINDOW, WINDOW)] = (dact * silu_g).astype(bf16)
-        out_part = jnp.dot(act_ref[:, down], wd_ref[down, :], preferred_element_type=f32)
-        dx_part = dot_nt(dup_ref[:, up], wgu_ref[:, up])
-        if k == 0:
-            out_acc[...] = out_part
-            dx_acc[...] = dx_part
-        elif k < stacks - 1:
-            out_acc[...] += out_part
-            dx_acc[...] += dx_part
-        else:
-            branch_ref[...] = (out_acc[...] + out_part).astype(bf16)
-            send_ref[:, :width] = (dx_acc[...] + dx_part).astype(bf16)
-    send_ref[:, width:] = dot_acc[...].astype(bf16)
-
-
-def hidden_units(both, wgu, wd, coefs, units):
-    length, width = both.shape[0], both.shape[1] // 2
-    stacks = wd.shape[0] // WINDOW
-    step = min(256, length)
-    bf16 = jnp.bfloat16
-
-    def rows_block(columns):
-        return pl.BlockSpec((step, columns), lambda i: (i, 0))
-
-    def whole(array):
-        return pl.BlockSpec(array.shape, lambda i: (0, 0), pipeline_mode=pl.Buffered(1))
-
-    return pl.pallas_call(
-        functools.partial(hidden_kernel, lax.axis_size("context"), stacks, units),
-        grid=(length // step,),
-        in_specs=[rows_block(2 * width), whole(wgu), whole(wd), rows_block(coefs.shape[1])],
-        out_specs=[rows_block(width + 128), rows_block(width), rows_block(wgu.shape[1]), rows_block(wd.shape[0])],
-        out_shape=[
-            jax.ShapeDtypeStruct((length, width + 128), bf16),
-            jax.ShapeDtypeStruct((length, width), bf16),
-            jax.ShapeDtypeStruct((length, wgu.shape[1]), bf16),
-            jax.ShapeDtypeStruct((length, wd.shape[0]), bf16),
-        ],
-        scratch_shapes=[
-            pltpu.VMEM((step, width), jnp.float32),
-            pltpu.VMEM((step, width), jnp.float32),
-            pltpu.VMEM((step, 128), jnp.float32),
-        ],
-        cost_estimate=pl.CostEstimate(
-            flops=6 * length * width * wgu.shape[1], bytes_accessed=40_000_000, transcendentals=length * wd.shape[0]
-        ),
-        name="hidden_units",
-    )(both, wgu, wd, coefs)
-
-
 def split_body(
     tokens,
     positions,
@@ -1645,122 +1833,95 @@
     token_own = own_half_first(own_of(tokens[0])).astype(jnp.float32)
     inverse1 = lax.rsqrt(jnp.mean(token_own * token_own, -1, keepdims=True) + EPSILON)
     normed1 = token_own * inverse1
-    places_own = own_of(positions[0])[:, None]
-    facts = jnp.concatenate([places_own // 64, places_own % 64, own_of(routes[0])], 1)
-    facts = jnp.pad(facts, ((0, 0), (0, 128 - facts.shape[1]))).astype(bf16)
-    send1 = jnp.concatenate([(normed1 * gain1).astype(bf16), facts], 1)
+    half_dim = HEAD_DIM // 2
+    frequency = ROPE_BASE ** (-2.0 * jnp.arange(half_dim, dtype=jnp.float32) / HEAD_DIM)
+    angles = own_of(positions[0]).astype(jnp.float32)[:, None] * frequency[None, :]
+    turns = jnp.concatenate([jnp.cos(angles), jnp.sin(angles)], 1)
+    turns_high = turns.astype(bf16)
+    turns_low = (turns - turns_high.astype(jnp.float32)).astype(bf16)
+    send1 = jnp.concatenate([(normed1 * gain1).astype(bf16), turns_high, turns_low], 1)
     qkv_in = jnp.transpose(
         qkv_weight.reshape(block, 3, parts, HEAD_DIM), (2, 0, 1, 3)
     ).reshape(parts * block, 3 * HEAD_DIM)
-    shared1, qkv_w, out_w = share_first(send1, qkv_in, out_weight, 1)
-    xn1, facts = shared1[:, :width], shared1[:, width:].astype(jnp.int32)
-    position_all = facts[:, 0] * 64 + facts[:, 1]
-    route_all = facts[:, 2 : 2 + routes.shape[2]]
-
     bias_here = lax.dynamic_slice_in_dim(
         qkv_bias.reshape(3, parts, HEAD_DIM), place, 1, 1
     ).reshape(1, 3 * HEAD_DIM)
-    qkv = (
-        dot_nn(xn1, qkv_w)
-        + bias_here.astype(jnp.float32)
-    )
-    cosine, sine_part = rope_tables(position_all)
-    cosine, sine_part = cosine[:, 0], sine_part[:, 0]
-    q_raw, k_raw, v_raw = jnp.split(qkv, 3, 1)
-    query = (q_raw * cosine + rotate(q_raw) * sine_part).astype(bf16)
-    key = (k_raw * cosine + rotate(k_raw) * sine_part).astype(bf16)
-    value = v_raw.astype(bf16)
-    index = jnp.arange(length, dtype=jnp.int32)
-    allowed = index[None, :] <= index[:, None]
-    scores = dot_nt(query, key) * scale
-    row_max = jnp.max(jnp.where(allowed, scores, MASKED), -1, keepdims=True)
-    weights = jnp.where(allowed, jnp.exp(scores - row_max), 0.0)
-    row_sum = jnp.sum(weights, -1, keepdims=True)
-    attended = (dot_nn(weights.astype(bf16), value) / row_sum).astype(bf16)
-    lse = row_max + jnp.log(row_sum)
-
-    head_part = dot_nn(attended, out_w).astype(bf16)
-    head_sum, down_w = sum_and_move(head_part, shared_w_down, expert_down, 2)
+    shared1, qkv_w, out_w, down_w, query, key, value, attended, lse, head_sum = attention_first(
+        send1, qkv_in, out_weight, bias_here.astype(jnp.float32), shared_w_down, expert_down, 1
+    )
+    xn1, turns = shared1[:, :width], shared1[:, width:]
     hidden = token_own + head_sum
     inverse2 = lax.rsqrt(jnp.mean(hidden * hidden, -1, keepdims=True) + EPSILON)
     normed2 = hidden * inverse2
     xn2_own = (normed2 * gain2).astype(bf16)
-    both, up_w = share_and_move(
-        jnp.concatenate([xn2_own, grad_own_b], 1), shared_w_gate, shared_w_up, expert_gate, expert_up, 3
-    )
-    xn2, grad_all = both[:, :width], both[:, width:]
-
     router_here = own_half_first(router_weight.T).T
     gate_here = own_half_first(shared_gate)
     heads_w = jnp.concatenate([router_here, gate_here[:, None]], 1)
-    logits_all = dot_nn(xn2, heads_w)
-    prob_all = jax.nn.softmax(logits_all[:, :expert_count], -1)
-    sig_all = jax.nn.sigmoid(logits_all[:, expert_count])
-    named_all = jnp.sum(
+    logits = dot_nn(xn2_own, heads_w)
+    prob = jax.nn.softmax(logits[:, :expert_count], -1)
+    sig_own = jax.nn.sigmoid(logits[:, expert_count])
+    named = jnp.sum(
         (
-            route_all[:, :, None] == jnp.arange(expert_count, dtype=jnp.int32)[None, None, :]
+            own_of(routes[0])[:, :, None] == jnp.arange(expert_count, dtype=jnp.int32)[None, None, :]
         ).astype(jnp.float32),
         1,
     )
-    gates_all = prob_all * named_all
-    gates_here = lax.dynamic_slice_in_dim(gates_all, group * local_experts, local_experts, 1)
-    coefs = jnp.concatenate([sig_all[:, None], gates_here], 1)
-
-    coefs = jnp.pad(coefs, ((0, 0), (0, 128 - stacks)))
-    send4, branch_part, dup, act_c = hidden_units(both, up_w, down_w, coefs, shared_w_gate.shape[1])
-    up_g = dot_tn(xn2, dup).astype(bf16)
-    down_g = dot_tn(act_c, grad_all).astype(bf16)
+    gates = jnp.pad(
+        jnp.concatenate([prob * named, sig_own[:, None]], 1), ((0, 0), (0, 63 - expert_count))
+    )
+    gates_high = gates.astype(bf16)
+    gates_low = (gates - gates_high.astype(jnp.float32)).astype(bf16)
+    send3 = jnp.concatenate([xn2_own, grad_own_b, gates_high, gates_low], 1)
+
+    both, send4, branch_part, dup, act_c = share_move_compute(
+        send3, shared_w_gate, shared_w_up, expert_gate, expert_up, down_w, 3
+    )
+    up_g = dot_tn(both[:, :width], dup).astype(bf16)
+    down_g = dot_tn(act_c, both[:, width : 2 * width]).astype(bf16)
     send4, up_g, down_g = lax.optimization_barrier((send4, up_g, down_g))
     up_grads, down_grads = [None] * (2 * stacks), [None] * stacks
-    sums, up_grads[0], up_grads[1] = sum_and_return(send4, up_g, 0, 4)
-    dxn2_sum, dots_own = sums[:, :width], sums[:, width:]
-
-    row_first = place * rows + first
-    prob = lax.dynamic_slice_in_dim(prob_all, row_first, own_rows, 0)
-    named = lax.dynamic_slice_in_dim(named_all, row_first, own_rows, 0)
-    sig_own = lax.dynamic_slice_in_dim(sig_all, row_first, own_rows, 0)
+    side = 128 - expert_count - 1
+    chances = jnp.pad(jnp.concatenate([prob, sig_own[:, None]], 1), ((0, 0), (0, side)))
+    named_wide = jnp.pad(named, ((0, 0), (0, 128 - expert_count)))
+    router_wide = jnp.pad(heads_w.T.astype(jnp.float32), ((0, side), (0, 0)))
+    (
+        dhidden_all,
+        up_grads[0],
+        up_grads[1],
+        down_grads[0],
+        dots_own,
+        dxn2,
+        dhidden,
+        dqkv_b,
+        bias_part,
+        dxn1,
+    ) = attention_last(
+        send4,
+        up_g,
+        down_g,
+        hidden,
+        grad_own_b,
+        gain2[None, :],
+        chances,
+        named_wide,
+        router_wide,
+        out_w,
+        qkv_w,
+        (query, key, value, attended),
+        lse,
+        turns,
+        4,
+    )
+    out_g = dot_tn(attended, dhidden_all).astype(bf16)
+    qkv_g = dot_tn(xn1, dqkv_b).astype(bf16)
+
     dprob = dots_own[:, :expert_count] * named
     dlogit = prob * (dprob - jnp.sum(prob * dprob, -1, keepdims=True))
     coef = sig_own * (1.0 - sig_own) * dots_own[:, expert_count]
     xn2_float = xn2_own.astype(jnp.float32)
     router_grad = jnp.dot(xn2_float.T, dlogit, precision=PRECISE)
     shared_gate_grad = jnp.dot(coef, xn2_float, precision=PRECISE)
-    dxn2 = (
-        dxn2_sum
-        + jnp.dot(dlogit, router_here.astype(jnp.float32).T, precision=PRECISE)
-        + coef[:, None] * gate_here.astype(jnp.float32)[None, :]
-    )
     norm2_grad = jnp.sum(dxn2 * normed2, 0)
-    dscaled2 = dxn2 * gain2
-    dhidden = grad_own + inverse2 * (
-        dscaled2 - normed2 * jnp.mean(dscaled2 * normed2, -1, keepdims=True)
-    )
-    dhidden_all, down_grads[0] = share_and_return(dhidden.astype(bf16), down_g, 0, 5)
-
-    out_g = dot_tn(attended, dhidden_all).astype(bf16)
-    dattended = dot_nt(dhidden_all, out_w).astype(bf16)
-    delta = jnp.sum(
-        dattended.astype(jnp.float32) * attended.astype(jnp.float32), -1, keepdims=True
-    )
-    scores = dot_nt(query, key) * scale
-    prob_att = jnp.where(allowed, jnp.exp(scores - lse), 0.0)
-    dvalue = dot_tn(prob_att.astype(bf16), dattended)
-    dscore = (prob_att * (dot_nt(dattended, value) - delta)).astype(bf16)
-    dquery = dot_nn(dscore, key) * scale
-    dkey = dot_tn(dscore, query) * scale
-    dqkv = jnp.concatenate(
-        [
-            dquery * cosine + rotate_back(dquery * sine_part),
-            dkey * cosine + rotate_back(dkey * sine_part),
-            dvalue,
-        ],
-        1,
-    )
-    bias_part = jnp.sum(dqkv, 0)
-    dqkv_b = dqkv.astype(bf16)
-    qkv_g = dot_tn(xn1, dqkv_b).astype(bf16)
-    dxn1_part = dot_nt(dqkv_b, qkv_w).astype(bf16)
-    dxn1, up_grads[2], up_grads[3] = sum_and_return(dxn1_part, up_g, 1, 6)
     norm1_grad = jnp.sum(dxn1 * normed1, 0)
     dscaled1 = dxn1 * gain1
     tokens_grad_own = dhidden + inverse1 * (
@@ -1768,7 +1929,7 @@
     )
 
     bias_wide = jnp.zeros((group_size, parts, 3 * HEAD_DIM), jnp.float32)
-    bias_wide = lax.dynamic_update_slice(bias_wide, bias_part[None, None], (group, place, 0))
+    bias_wide = lax.dynamic_update_slice(bias_wide, bias_part[None], (group, place, 0))
     small = jnp.concatenate(
         [
             own_half_first(norm1_grad),
@@ -1787,13 +1948,13 @@
         hidden,
         own_half_first(tokens_grad_own),
         small.reshape(-1, 128),
-        list(range(2, stacks)),
+        list(range(1, stacks)),
         list(range(1, stacks)),
         7,
     )
     small = small.reshape(-1)
-    up_grads[4:] = others[: 2 * (stacks - 2)]
-    down_grads[1:] = others[2 * (stacks - 2) :]
+    up_grads[2:] = others[: 2 * (stacks - 1)]
+    down_grads[1:] = others[2 * (stacks - 1) :]
     router_size = width * expert_count
     bias_sum = small[3 * width + router_size :].reshape(group_size, parts, 3, HEAD_DIM)
     bias_grad = jnp.transpose(

time: 743 us -> 663 us (0.89)
  Pallas kernels: 613 us -> 580 us
  matrix products: 58.7 us -> 35.1 us
  other arithmetic: 34.4 us -> 19.3 us
    pallas_call x7 -> x3, Pallas kernels: 493 us -> 424 us  [the longest x1 169 us: share_move_compute(): comm_call(kernel, number, 'share_move_compute', [jax.ShapeDtypeStruct((le...]
    pallas_call x1, Pallas kernels: 120 us -> 155 us  [last_exchange(): comm_call(kernel, number, 'last_exchange', out_shape, [IN_PLACE] * (len(o...]
    dot_general x5 -> x0, matrix products: 14.3 us -> none  [the longest x4 12.6 us: dot_nt(): lax.dot_general(left, right, (((1,), (1,)), ((), ())), preferred_element_...]
    dot_general x5 -> x1, matrix products: 12.4 us -> 0.2 us  [dot_nn(): return jnp.dot(left, right, preferred_element_type=jnp.float32)]
    dot_general x6 -> x4, matrix products: 30.7 us -> 34.3 us  [dot_tn(): lax.dot_general(left, right, (((0,), (0,)), ((), ())), preferred_element_...]
where the time goes in v3:
time: 663 us; the launch traced here: 657 us
  Pallas kernels  580 us (87%)
  matrix products  35.1 us (5%)
  local copies, waits for them, and re-layouts  21.8 us (3%)
  other arithmetic  19.3 us (3%)
    pallas_call x1, Pallas kernels, share_move_compute(): comm_call(kernel, number, 'share_move_compute', [jax.ShapeDtypeStruct((le...  169 us
    pallas_call x1, Pallas kernels, last_exchange(): comm_call(kernel, number, 'last_exchange', out_shape, [IN_PLACE] * (len(o...  155 us
    pallas_call x1, Pallas kernels, attention_last(): comm_call(kernel, number, 'attention_last', [jax.ShapeDtypeStruct((length...  138 us
    pallas_call x1, Pallas kernels, attention_first(): comm_call(kernel, number, 'attention_first', [jax.ShapeDtypeStruct((lengt...  118 us
    dot_general x4, matrix products, dot_tn(): lax.dot_general(left, right, (((0,), (0,)), ((), ())), preferred_element_...  34.3 us

profile of v3, /device:TPU:16, one launch (start us, length us, event | category | flops | bytes accessed | tf_op | source)
XLA Modules:
  0.0 657.2 jit_solution(8695762912931173005)
XLA Ops:
  0.7 0.8 fusion.39
  1.9 1.1 dynamic-slice_bitcast_fusion
  5.4 0.7 pad_maximum_fusion.own_ref
  6.3 0.7 copy.89
  7.2 1.2 copy.91.qkv_ref
  9.6 117.8 %attention_first.1 = (bf16[1024,2304]{1,0:T(8,128)(2,1)}, bf16[2048,384]{1,0:T(8,128)(2,1)}, bf16[128,2048]{1,0:T(8,128)(2,1)}, bf16[1152,2048]{1,0:T(8,128)(2,1...) custom-call(bf16[64,2304]{1,0:T(8,128)(2,1)} %pad_maximum_fusion.own, ...), custom_call_target="tpu_custom_call" | custom-call | bytes 250000000 | tf_op jit(solution)/shard_map/attention_first/pallas_call | solution.py:1194
  127.5 1.2 multiply_reduce_fusion.1
  130.2 1.2 concatenate.64.own_ref
  131.4 168.6 %share_move_compute.1 = (bf16[1024,4224]{1,0:T(8,128)(2,1)}, bf16[1024,2176]{1,0:T(8,128)(2,1)}, bf16[1024,2048]{1,0:T(8,128)(2,1)}, bf16[1024,2304]{1,0:T(8,128)(2,1)}, bf16[1024,1152]{1,0:T(8,128)(2,1)}) custom-call(bf16[64,4224]{1,0:T(8,128)(2,1)} %concatenate.64.own_ref, bf16[256,1408]{1,0:T(8,128)(2,1)} %sg_ref.1, bf16[256,1408]{1,0:T(8,128)(2,1)} %su_ref.1, ...), custom_call_target="tpu_custom_call" | custom-call | bytes 300000000 | tf_op jit(solution)/shard_map/share_move_compute/pallas_call | solution.py:1380
  300.0 15.7 %convolution_convert_fusion.upg_ref = bf16[2048,2304]{1,0:T(8,128)(2,1)} fusion(bf16[1024,2304]{1,0:T(8,128)(2,1)} %get-tuple-element.58, bf16[1024,4224]{1,0:T(8,128)(2,1)} %get-tuple-element.57), kind=kOutput, calls=%fused_computation | convolution fusion | flops 9668395008 | bytes 18350080 | tf_op jit(solution)/shard_map/dot_general | solution.py:558
  315.7 9.0 %convolution_convert_fusion.1.downg_ref = bf16[1152,2048]{1,0:T(8,128)(2,1)} fusion(bf16[1024,1152]{1,0:T(8,128)(2,1)S(1)} %copy-done.28, bf16[1024,4224]{1,0:T(8,128)(2,1)} %get-tuple-element.57), kind=kOutput, calls=%fused_computation.1 | convolution fusion | flops 4834197504 | bytes 11272192 | tf_op jit(solution)/shard_map/dot_general | solution.py:558
  326.0 1.1 pad_convert_fusion.router_ref
  327.1 1.9 slice.132.turn_ref
  328.9 138.0 %attention_last.1 = (bf16[1024,2048]{1,0:T(8,128)(2,1)}, bf16[256,1408]{1,0:T(8,128)(2,1)}, bf16[256,1408]{1,0:T(8,128)(2,1)}, bf16[1408,256]{1,0:T(8,128)(2,1)}...) custom-call(bf16[1024,2176]{1,0:T(8,128)(2,1)} %get-tuple-element.63, ...), custom_call_target="tpu_custom_call" | custom-call | bytes 250000000 | tf_op jit(solution)/shard_map/attention_last/pallas_call | solution.py:1572
  466.9 3.8 convolution_convert_fusion.2.outg_ref
  470.8 5.8 fusion.4.qkvg_ref
  477.1 0.9 maximum_select_fusion.tokens_ref
  480.9 155.2 %last_exchange.1 = (bf16[512,256]{1,0:T(8,128)(2,1)}, bf16[1024,384]{1,0:T(8,128)(2,1)}, bf16[256,1408]{1,0:T(8,128)(2,1)}, bf16[256,1408]{1,0:T(8,128)(2,1)}, b...) custom-call(bf16[2048,2304]{1,0:T(8,128)(2,1)} %convolution_convert_, ...), custom_call_target="tpu_custom_call" | custom-call | bytes 300000000 | tf_op jit(solution)/shard_map/last_exchange/pallas_call | solution.py:1778
  636.1 1.3 slice_bitcast_fusion
  637.4 1.4 copy.99
  638.9 0.7 reshape.145
  639.9 1.6 copy.102
  642.2 0.8 convert_element_type.134
  643.6 0.9 copy.103
  644.5 2.9 maximum_convert_fusion
  647.4 1.8 maximum_convert_fusion.1
  649.3 1.8 maximum_convert_fusion.2
  651.1 1.2 convert_element_type.138
  652.3 1.2 convert_element_type.139
  653.5 1.2 convert_element_type.140
  654.7 1.0 copy.121
  655.6 1.3 copy.122
  (130 shorter events, 12.0 us)
Async XLA Ops:
  0.6 128.3 %copy-start = (s32[1,256,4]{1,2,0:T(4,128)S(1)}, s32[1,256,4]{1,2,0:T(4,128)}, u32[]{:S(2)}) copy-start(s32[1,256,4]{1,2,0:T(4,128)} %param.19) | copy-start | bytes 12292
  0.7 5.5 copy-start.9
  5.3 123.4 %copy-start.25 = (f32[2048]{0:T(1024)}, f32[2048]{0:T(1024)S(1)}, u32[]{:S(2)}) copy-start(f32[2048]{0:T(1024)S(1)} %get-tuple-element.225) | copy-start | bytes 24580
  9.6 119.5 %copy-start.26 = (bf16[2048]{0:T(1024)(128)(2,1)S(1)}, bf16[2048]{0:T(1024)(128)(2,1)}, u32[]{:S(2)}) copy-start(bf16[2048]{0:T(1024)(128)(2,1)} %param.30) | copy-start | bytes 12292
  9.6 119.6 %copy-start.23 = (bf16[2048,8]{0,1:T(8,128)(2,1)S(1)}, bf16[2048,8]{0,1:T(8,128)(2,1)}, u32[]{:S(2)}) copy-start(bf16[2048,8]{0,1:T(8,128)(2,1)} %param.26) | copy-start | bytes 98308
  128.7 171.3 %copy-start.2 = (f32[64,2048]{1,0:T(8,128)}, f32[64,2048]{1,0:T(8,128)S(1)}, u32[]{:S(2)}) copy-start(f32[64,2048]{1,0:T(8,128)S(1)} %get-tuple-element.190.hidden_ref) | copy-start | bytes 1572868
  129.0 171.0 %copy-start.4 = (bf16[64,2048]{1,0:T(8,128)(2,1)}, bf16[64,2048]{1,0:T(8,128)(2,1)S(1)}, u32[]{:S(2)}) copy-start(bf16[64,2048]{1,0:T(8,128)(2,1)S(1)} %maximum_select_fusion.2.grad_ref) | copy-start | bytes 786436
  300.0 15.7 %copy-start.28 = (bf16[1024,1152]{1,0:T(8,128)(2,1)S(1)}, bf16[1024,1152]{1,0:T(8,128)(2,1)}, u32[]{:S(2)}) copy-start(bf16[1024,1152]{1,0:T(8,128)(2,1)} %get-tuple-element.59) | copy-start | bytes 7077892
  328.9 138.0 %copy-start.7 = (bf16[1024,128]{1,0:T(8,128)(2,1)S(1)}, bf16[1024,128]{1,0:T(8,128)(2,1)}, u32[]{:S(2)}) copy-start(bf16[1024,128]{1,0:T(8,128)(2,1)} %get-tuple-element.62.att_ref) | copy-start | bytes 786436
  466.9 3.8 copy-start.29
  470.7 5.8 copy-start.5
  470.7 6.1 copy-start.18
  476.6 1.4 copy-start.3
  476.6 1.4 copy-start.19
  476.9 1.3 copy-start.20
  477.1 2.8 copy-start.27
  480.3 0.6 copy-start.22
  639.6 1.9 copy-start.24
  639.6 2.6 copy-start.21
  641.5 3.0 copy-start.17
  643.6 3.8 copy-start.15
  643.6 3.8 copy-start.16
  647.4 1.8 copy-start.13
  647.4 1.9 copy-start.14
  649.2 1.9 copy-start.12
  649.3 3.0 copy-start.11
  651.1 2.4 copy-start.10
  651.1 3.6 copy-start.8
  652.3 3.4 copy-start.6
  653.5 3.5 copy-start.1

commit v4 on v3

--- a/solution.py
+++ b/solution.py
@@ -583,6 +583,22 @@
     return ref.at[:, pl.ds(pl.multiple_of(start, 128), size)]
 
 
+def by_width(device, narrow, body):
+    if narrow is None:
+        body(False)
+    elif isinstance(device, int):
+        body(device == narrow)
+    else:
+
+        @pl.when(device == narrow)
+        def _():
+            body(True)
+
+        @pl.when(device != narrow)
+        def _():
+            body(False)
+
+
 class Spot:
     def __init__(self):
         self.parts = lax.axis_size("context")
@@ -879,56 +895,81 @@
     def sems(count, parts):
         return [DMA((count * parts,))] * 4 + [DMA((count,))]
 
-    def to(self, number, target, source):
-        s, (src, dst) = self.spot, self.items[number]
-        return remote(src(target), dst(0, source), self.line_s.at[number * s.parts + target], self.line_r.at[number * s.parts + source], {"context": target})
-
-    def on(self, number, source, view):
-        s, (_, dst) = self.spot, self.items[number]
+    def fit(self, number, device, body):
+        by_width(device, self.items[number]["short"], body)
+
+    def to(self, number, target, source, short):
+        s, item = self.spot, self.items[number]
+        sems = self.line_s.at[number * s.parts + target], self.line_r.at[number * s.parts + source]
+        return remote(item["src"](target, short), item["dst"](0, source, short), *sems, {"context": target})
+
+    def on(self, number, source, short, view=None):
+        s, item = self.spot, self.items[number]
         slot = number * s.parts + source
-        return remote(view, dst(1, source), self.twin_s.at[slot], self.twin_r.at[slot], s.twin)
-
-    def local(self, number):
-        s, (src, dst) = self.spot, self.items[number]
-        return pltpu.make_async_copy(src(s.place), dst(0, s.place), self.local_sem.at[number])
+        view = item["dst"](0, source, short) if view is None else view
+        return remote(view, item["dst"](1, source, short), self.twin_s.at[slot], self.twin_r.at[slot], s.twin)
+
+    def local(self, number, short):
+        s, item = self.spot, self.items[number]
+        return pltpu.make_async_copy(item["src"](s.place, short), item["dst"](0, s.place, short), self.local_sem.at[number])
 
     def own(self, number):
-        s, (src, _) = self.spot, self.items[number]
-        self.on(number, s.place, src(s.place)).start()
-        self.local(number).start()
+        s, item = self.spot, self.items[number]
+
+        def one(short):
+            self.on(number, s.place, short, item["src"](s.place, short)).start()
+            self.local(number, short).start()
+
+        self.fit(number, s.place, one)
 
     def send_gap(self, number, gap):
         s = self.spot
-        s.others(gap, lambda target: self.to(number, target, s.place).start())
+
+        def one(target):
+            self.fit(number, target, lambda short: self.to(number, target, s.place, short).start())
+
+        s.others(gap, one)
 
     def send(self, number):
         for gap in range(self.spot.parts - 1, 0, -1):
             self.send_gap(number, gap)
 
     def forward(self, number, gap):
-        s, (_, dst) = self.spot, self.items[number]
+        s = self.spot
 
         def one(source):
-            self.to(number, s.place, source).wait_recv()
-            self.on(number, source, dst(0, source)).start()
+            def step(short):
+                self.to(number, s.place, source, short).wait_recv()
+                self.on(number, source, short).start()
+
+            self.fit(number, s.place, step)
 
         s.others(gap, one)
 
     def ready(self, number):
-        s, (_, dst) = self.spot, self.items[number]
-        self.local(number).wait()
-        for part in range(s.parts):
-            self.on(number, part, dst(0, part)).wait_recv()
+        s = self.spot
+
+        def one(short):
+            self.local(number, short).wait()
+            for part in range(s.parts):
+                self.on(number, part, short).wait_recv()
+
+        self.fit(number, s.place, one)
 
     def sent(self):
         s = self.spot
-        for number, (_, dst) in enumerate(self.items):
+        for number in range(len(self.items)):
+
+            def one(short):
+                for part in range(s.parts):
+                    self.on(number, part, short).wait_send()
+
+            self.fit(number, s.place, one)
             for part in range(s.parts):
-                self.on(number, part, dst(0, part)).wait_send()
 
                 @pl.when(part != s.place)
                 def _():
-                    self.to(number, part, s.place).wait_send()
+                    self.fit(number, part, lambda short: self.to(number, part, s.place, short).wait_send())
 
     def end(self):
         for number in range(len(self.items)):
@@ -978,19 +1019,8 @@
         slot = self.bases[number][0] // s.parts + which
         return pltpu.make_async_copy(cut(self.mine_buf[number].at[s.place], short), out(s.place, short), self.local_sem.at[slot])
 
-    def by_width(self, source, body):
-        last = source == self.spot.parts - 1
-        if not isinstance(source, int):
-
-            @pl.when(last)
-            def _():
-                body(True)
-
-            @pl.when(jnp.logical_not(last))
-            def _():
-                body(False)
-        else:
-            body(last)
+    def fit(self, number, source, body):
+        by_width(source, self.items[number].get("short"), body)
 
     def reduce(self, number, index):
         s, part = self.spot, self.order[index]
@@ -1009,9 +1039,9 @@
         lax.fori_loop(0, rows // step, one, 0)
         for which in range(len(item["pieces"])):
             if index < s.parts - 1:
-                self.by_width(s.place, lambda short: self.piece(number, which, part, s.place, short).start())
+                self.fit(number, s.place, lambda short: self.piece(number, which, part, s.place, short).start())
             else:
-                self.by_width(s.place, lambda short: self.keep(number, which, short).start())
+                self.fit(number, s.place, lambda short: self.keep(number, which, short).start())
 
     def end(self):
         s = self.spot
@@ -1022,11 +1052,58 @@
 
                     @pl.when(part != s.place)
                     def _():
-                        self.by_width(s.place, lambda short: self.piece(number, which, part, s.place, short).wait_send())
-                        self.by_width(part, lambda short: self.piece(number, which, s.place, part, short).wait_recv())
+                        self.fit(number, s.place, lambda short: self.piece(number, which, part, s.place, short).wait_send())
+                        self.fit(number, part, lambda short: self.piece(number, which, s.place, part, short).wait_recv())
 
             for which in range(len(item["pieces"])):
-                self.by_width(s.place, lambda short: self.keep(number, which, short).wait())
+                self.fit(number, s.place, lambda short: self.keep(number, which, short).wait())
+
+
+class Grads:
+    def __init__(self, both, width, dup, act, up_out, down_out, up_buf, down_buf, up_s, down_s):
+        self.both, self.width, self.dup, self.act = both, width, dup, act
+        self.up_out, self.down_out, self.up_buf, self.down_buf = up_out, down_out, up_buf, down_buf
+        self.up_s, self.down_s = up_s, down_s
+        self.step = 256
+
+    @staticmethod
+    def scratch():
+        up, down = pltpu.VMEM((2, 256, 2 * WINDOW), jnp.bfloat16), pltpu.VMEM((2, WINDOW, 256), jnp.bfloat16)
+        return [up, down, DMA((2,)), DMA((2,))]
+
+    def copies(self, index):
+        at = pl.ds(pl.multiple_of(index * self.step, self.step), self.step)
+        slot = lax.rem(index, 2)
+        return (
+            lambda: pltpu.make_async_copy(self.up_buf.at[slot], self.up_out.at[at, :], self.up_s.at[slot]),
+            lambda: pltpu.make_async_copy(self.down_buf.at[slot], self.down_out.at[:, at], self.down_s.at[slot]),
+        )
+
+    def run(self):
+        count = self.width // self.step
+
+        def one(index, carry):
+            up_copy, down_copy = self.copies(index)
+
+            @pl.when(index >= 2)
+            def _():
+                up_copy().wait()
+                down_copy().wait()
+
+            slot = lax.rem(index, 2)
+            at = pl.multiple_of(index * self.step, self.step)
+            up = dot_tn(self.both[:, pl.ds(at, self.step)], self.dup[...])
+            self.up_buf[slot] = up.astype(jnp.bfloat16)
+            down = dot_tn(self.act[...], self.both[:, pl.ds(self.width + at, self.step)])
+            self.down_buf[slot] = down.astype(jnp.bfloat16)
+            up_copy().start()
+            down_copy().start()
+            return carry
+
+        lax.fori_loop(0, count, one, 0)
+        for index in (count - 2, count - 1):
+            for copy in self.copies(index):
+                copy().wait()
 
 
 def comm_call(kernel, number, name, out_shape, out_specs, in_specs, scratch, bytes_moved):
@@ -1047,8 +1124,27 @@
 WINDOW = 384
 
 
-def window_of(index, length):
-    return jnp.minimum(index * WINDOW, length - WINDOW)
+SPARE = 128
+
+
+def narrow_of(k):
+    return 0 if k % 2 else 3
+
+
+def window_of(k, index, narrow):
+    if narrow_of(k) == 0:
+        return (0, WINDOW - SPARE, 0) if narrow else (index * WINDOW - SPARE, WINDOW, 0)
+    return (index * WINDOW, WINDOW - SPARE, SPARE) if narrow else (index * WINDOW, WINDOW, 0)
+
+
+def first_unit(value):
+    return value if isinstance(value, int) else pl.multiple_of(value, SPARE)
+
+
+def units_at(ref, k, index, narrow, axis, base=0):
+    start, size, inside = window_of(k, index, narrow)
+    start = first_unit(start) if base is None else base + inside
+    return ref.at[pl.ds(start, size), :] if axis == 0 else ref.at[:, pl.ds(start, size)]
 
 
 def turn(value, cosine, sine_part):
@@ -1068,7 +1164,6 @@
     block, span = qkv_in.shape[0] // parts, qkv_in.shape[1]
     head, lanes = out_weight.shape[0] // parts, out_weight.shape[1]
     width, length = 2 * parts * lanes, rows * parts * 4
-    units = shared_down.shape[0]
     count = 1 + expert_down.shape[0]
     step = 256
     scale = HEAD_DIM ** (-0.5)
@@ -1096,25 +1191,27 @@
         spot = Spot()
         share = Share(spot, own_ref, all_ref, split[1])
         items = [
-            (
-                lambda target: rows_at(qkv_ref, target * block, block),
-                lambda side, source: rows_at(wqkv_ref, (side * parts + source) * block, block),
-            ),
-            (
-                lambda target: rows_at(outw_ref, target * head, head),
-                lambda side, source: lanes_at(wout_ref, (side * parts + source) * lanes, lanes),
-            ),
+            {
+                "src": lambda target, short: rows_at(qkv_ref, target * block, block),
+                "dst": lambda side, source, short: rows_at(wqkv_ref, (side * parts + source) * block, block),
+                "short": None,
+            },
+            {
+                "src": lambda target, short: rows_at(outw_ref, target * head, head),
+                "dst": lambda side, source, short: lanes_at(wout_ref, (side * parts + source) * lanes, lanes),
+                "short": None,
+            },
         ]
 
         def down(k):
             ref = shared_ref if k == 0 else expert_ref.at[k - 1]
-            return (
-                lambda target: rows_at(ref, window_of(target, units), WINDOW),
-                lambda side, source: wd_ref.at[
-                    pl.ds(k * WINDOW, WINDOW),
-                    pl.ds(pl.multiple_of((side * parts + source) * lanes, lanes), lanes),
-                ],
-            )
+            return {
+                "src": lambda target, short: units_at(ref, k, target, short, 0, None),
+                "dst": lambda side, source, short: lanes_at(
+                    units_at(wd_ref, k, 0, short, 0, k * WINDOW), (side * parts + source) * lanes, lanes
+                ),
+                "short": narrow_of(k),
+            }
 
         move = Move(spot, items + [down(k) for k in range(count)], split[2])
         summed = Sum(spot, part_ref, sum_ref, split[3])
@@ -1218,14 +1315,14 @@
     parts = lax.axis_size("context")
     rows, wide = value.shape
     width = wd.shape[1]
-    block, units = shared_gate.shape
+    block = shared_gate.shape[0]
     stacks = 1 + expert_gate.shape[0]
     count = 2 * stacks
     length = rows * parts * 4
     experts = (stacks - 1) * 4
     step = 256
     f32, bf16 = jnp.float32, jnp.bfloat16
-    share_sems, move_sems = Share.sems(parts), Move.sems(count, parts)
+    share_sems, move_sems, grad_scratch = Share.sems(parts), Move.sems(count, parts), Grads.scratch()
     scratch = [
         pltpu.VMEM((length, wide), bf16),
         pltpu.VMEM((2 * parts * block, count * WINDOW), bf16),
@@ -1244,9 +1341,9 @@
         DMA((length // step,)),
     ]
 
-    def kernel(own_ref, sg_ref, su_ref, eg_ref, eu_ref, wd_hbm, both_hbm, send_hbm, branch_hbm, dup_hbm, act_hbm, *rest):
+    def kernel(own_ref, sg_ref, su_ref, eg_ref, eu_ref, wd_hbm, both_hbm, send_hbm, branch_hbm, dup_hbm, act_hbm, upg_hbm, downg_hbm, *rest):
         both, wgu, wd_ref, dx_acc, out_acc, dot_acc, act_ref, dup_ref, send_buf, branch_buf, load, act_s, dup_s, send_s, branch_s = rest[: len(scratch)]
-        sems = rest[len(scratch) :]
+        grad_refs, sems = rest[len(scratch) : len(scratch) + 4], rest[len(scratch) + 4 :]
         spot = Spot()
         share = Share(spot, own_ref, both, sems[: len(share_sems)])
 
@@ -1254,20 +1351,17 @@
             k = number // 2
             shared, expert = (sg_ref, eg_ref) if number % 2 == 0 else (su_ref, eu_ref)
             ref = shared if k == 0 else expert.at[k - 1]
-            return (
-                lambda target: lanes_at(ref, window_of(target, units), WINDOW),
-                lambda side, source: wgu.at[
-                    pl.ds(pl.multiple_of((side * parts + source) * block, block), block),
-                    pl.ds(number * WINDOW, WINDOW),
-                ],
-            )
+            return {
+                "src": lambda target, short: units_at(ref, k, target, short, 1, None),
+                "dst": lambda side, source, short: rows_at(
+                    units_at(wgu, k, 0, short, 1, number * WINDOW), (side * parts + source) * block, block
+                ),
+                "short": narrow_of(k),
+            }
 
         move = Move(spot, [item(number) for number in range(count)], sems[len(share_sems) :])
         weights = pltpu.make_async_copy(wd_hbm, wd_ref, load.at[0])
         keep = pltpu.make_async_copy(both, both_hbm, load.at[1])
-        repeated = jnp.where(spot.place == parts - 1, WINDOW * parts - units, 0)
-        lane = lax.broadcasted_iota(jnp.int32, (1, WINDOW), 1)
-        fresh = jnp.where(lane >= repeated, 1.0, 0.0)
         column = lax.broadcasted_iota(jnp.int32, (1, 128), 1)
 
         def send_out(index):
@@ -1278,13 +1372,15 @@
             at = pl.ds(pl.multiple_of(index * step, step), step)
             return pltpu.make_async_copy(branch_buf.at[lax.rem(index, 2)], branch_hbm.at[at, :], branch_s.at[index])
 
-        def act_out(k):
-            at = pl.ds(k * WINDOW, WINDOW)
-            return pltpu.make_async_copy(act_ref.at[:, at], act_hbm.at[:, at], act_s.at[k])
-
-        def dup_out(k):
-            at = pl.ds(2 * k * WINDOW, 2 * WINDOW)
-            return pltpu.make_async_copy(dup_ref.at[:, at], dup_hbm.at[:, at], dup_s.at[k])
+        def act_out():
+            return pltpu.make_async_copy(act_ref.at[:, pl.ds((stacks - 1) * WINDOW, WINDOW)], act_hbm, act_s.at[0])
+
+        def dup_out():
+            return pltpu.make_async_copy(dup_ref.at[:, pl.ds(2 * (stacks - 1) * WINDOW, 2 * WINDOW)], dup_hbm, dup_s.at[0])
+
+        def gradients(k):
+            up, down = pl.ds(2 * k * WINDOW, 2 * WINDOW), pl.ds(k * WINDOW, WINDOW)
+            Grads(both, width, dup_ref.at[:, up], act_ref.at[:, down], upg_hbm.at[:, up], downg_hbm.at[down, :], *grad_refs).run()
 
         def compute(k, first, last):
             up, down = pl.ds(2 * k * WINDOW, 2 * WINDOW), pl.ds(k * WINDOW, WINDOW)
@@ -1295,14 +1391,14 @@
             def one(index, carry):
                 rows_here = pl.ds(pl.multiple_of(index * step, step), step)
                 vals = jnp.dot(both[rows_here, :width], wgu[:, up], preferred_element_type=f32)
-                raw = dot_nt(both[rows_here, width : 2 * width], wd_ref[down, :]) * fresh
+                raw = dot_nt(both[rows_here, width : 2 * width], wd_ref[down, :])
                 coef = jnp.sum(both[rows_here, 2 * width :].astype(f32) * both_parts, -1, keepdims=True)
                 g_vals, u_vals = vals[:, :WINDOW], vals[:, WINDOW:]
                 sig_g = jax.nn.sigmoid(g_vals)
                 silu_g = g_vals * sig_g
                 act = silu_g * u_vals
                 dots = jnp.sum(raw * act, -1, keepdims=True) * here
-                act_ref[rows_here, down] = (act * (coef * fresh)).astype(bf16)
+                act_ref[rows_here, down] = (act * coef).astype(bf16)
                 dact = raw * coef
                 dup_ref[rows_here, pl.ds(2 * k * WINDOW, WINDOW)] = (
                     dact * u_vals * (sig_g * (1.0 + g_vals * (1.0 - sig_g)))
@@ -1356,6 +1452,15 @@
         keep.start()
         forward(1)
         weights.wait()
+        for k in range(stacks):
+
+            @pl.when(spot.place == narrow_of(k))
+            def _():
+                spare = 0 if narrow_of(k) else WINDOW - SPARE
+                wd_ref[pl.ds(k * WINDOW + spare, SPARE), :] = jnp.zeros((SPARE, width), bf16)
+                for which in (2 * k, 2 * k + 1):
+                    wgu[:, pl.ds(which * WINDOW + spare, SPARE)] = jnp.zeros((2 * parts * block, SPARE), bf16)
+
         pieces = length // step
         for k in range(stacks):
             if k < stacks - 1:
@@ -1366,14 +1471,15 @@
             if k < stacks - 1:
                 forward(2 * k + 3)
             compute(k, pieces // 2, pieces)
-            act_out(k).start()
-            dup_out(k).start()
+            if k < stacks - 1:
+                gradients(k)
+        act_out().start()
+        dup_out().start()
         for index in (pieces - 2, pieces - 1):
             send_out(index).wait()
             branch_out(index).wait()
-        for k in range(stacks):
-            act_out(k).wait()
-            dup_out(k).wait()
+        act_out().wait()
+        dup_out().wait()
         keep.wait()
         move.sent()
 
@@ -1385,53 +1491,51 @@
             jax.ShapeDtypeStruct((length, wide), bf16),
             jax.ShapeDtypeStruct((length, width + 128), bf16),
             jax.ShapeDtypeStruct((length, width), bf16),
-            jax.ShapeDtypeStruct((length, count * WINDOW), bf16),
-            jax.ShapeDtypeStruct((length, stacks * WINDOW), bf16),
+            jax.ShapeDtypeStruct((length, 2 * WINDOW), bf16),
+            jax.ShapeDtypeStruct((length, WINDOW), bf16),
+            jax.ShapeDtypeStruct((width, 2 * (stacks - 1) * WINDOW), bf16),
+            jax.ShapeDtypeStruct(((stacks - 1) * WINDOW, width), bf16),
         ],
-        [IN_PLACE] * 5,
+        [IN_PLACE] * 7,
         [IN_VMEM] + [IN_PLACE] * 5,
-        scratch + share_sems + move_sems,
+        scratch + grad_scratch + share_sems + move_sems,
         300_000_000,
     )(value, shared_gate, shared_up, expert_gate, expert_up, wd)
 
 
-def up_item(grads_ref, k, gate_ref, up_ref, block, parts):
-    hidden = gate_ref.shape[1]
-    tail = hidden - (parts - 1) * WINDOW
-
-    def cut(offset):
-        return lambda buf, short: buf.at[:, pl.ds(offset + (WINDOW - tail if short else 0), tail if short else WINDOW)]
-
-    def out(ref):
-        return lambda source, short: ref.at[:, pl.ds(hidden - tail, tail)] if short else lanes_at(ref, source * WINDOW, WINDOW)
+def up_item(grads_ref, at, k, gate_ref, up_ref, block, parts):
+    def piece(offset, ref):
+        return (
+            lambda buf, short: units_at(buf, k, 0, short, 1, offset),
+            lambda source, short: units_at(ref, k, source, short, 1, None),
+        )
 
     return {
         "block": lambda side, part: grads_ref.at[
-            pl.ds(pl.multiple_of((side * parts + part) * block, block), block), pl.ds(2 * k * WINDOW, 2 * WINDOW)
+            pl.ds(pl.multiple_of((side * parts + part) * block, block), block), pl.ds(2 * at * WINDOW, 2 * WINDOW)
         ],
-        "pieces": [(cut(0), out(gate_ref)), (cut(WINDOW), out(up_ref))],
-        "shape": (block, 2 * WINDOW),
+        "pieces": [piece(0, gate_ref), piece(WINDOW, up_ref)],
+        "short": narrow_of(k),
     }
 
 
-def down_item(grads_ref, k, down_ref, parts):
-    hidden, lanes = down_ref.shape
-    tail = hidden - (parts - 1) * WINDOW
+def down_item(grads_ref, at, k, down_ref, parts):
+    lanes = down_ref.shape[1]
     return {
         "block": lambda side, part: grads_ref.at[
-            pl.ds(k * WINDOW, WINDOW), pl.ds(pl.multiple_of((side * parts + part) * lanes, lanes), lanes)
+            pl.ds(at * WINDOW, WINDOW), pl.ds(pl.multiple_of((side * parts + part) * lanes, lanes), lanes)
         ],
         "pieces": [
             (
-                lambda buf, short: buf.at[pl.ds(WINDOW - tail if short else 0, tail if short else WINDOW), :],
-                lambda source, short: down_ref.at[pl.ds(hidden - tail, tail), :] if short else rows_at(down_ref, source * WINDOW, WINDOW),
+                lambda buf, short: units_at(buf, k, 0, short, 0),
+                lambda source, short: units_at(down_ref, k, source, short, 0, None),
             )
         ],
-        "shape": (WINDOW, lanes),
+        "short": narrow_of(k),
     }
 
 
-def attention_last(send4, up_grads, down_grads, hidden, grad, gain, chances, named, router, out_w, qkv_w, heads, lse, turns, number):
+def attention_last(send4, up_grads, down_grads, hidden, grad, gain, chances, named, router, out_w, qkv_w, heads, lse, shared, number):
     parts = lax.axis_size("context")
     length, width = send4.shape[0], hidden.shape[1]
     rows, wide = hidden.shape[0], send4.shape[1]
@@ -1442,18 +1546,19 @@
     experts = 8
     scale = HEAD_DIM ** (-0.5)
     f32, bf16 = jnp.float32, jnp.bfloat16
-    shapes, pieces = [(block, 2 * WINDOW), (WINDOW, lanes)], [2, 1]
+    shapes, pieces = [(block, 2 * WINDOW), (WINDOW, lanes), (block, 2 * WINDOW)], [2, 1, 2]
     sets = [
         [
             pltpu.VMEM((rows, wide), f32),
             pltpu.VMEM((rows, width), bf16),
             pltpu.VMEM((length, width), bf16),
             pltpu.VMEM((length, width), bf16),
-            pltpu.VMEM((length, HEAD_DIM), bf16),
+            pltpu.VMEM((length, 3 * HEAD_DIM), bf16),
             pltpu.VMEM((length, HEAD_DIM), f32),
             pltpu.VMEM((length, HEAD_DIM), f32),
             pltpu.VMEM((length, HEAD_DIM), f32),
-            DMA,
+            pltpu.VMEM(shared.shape, bf16),
+            DMA((2,)),
         ],
         Sum.scratch(parts, rows, wide),
         Share.sems(parts),
@@ -1462,20 +1567,25 @@
     ]
 
     def kernel(send_ref, upg_ref, downg_ref, hidden_ref, grad_ref, gain_ref, chance_ref, named_ref, router_ref, wout_ref, wqkv_ref,
-               q_ref, k_ref, v_ref, att_ref, lse_ref, turn_ref,
-               dh_hbm, gate_out, up_out, down_out, dots_ref, dxn2_ref, dhidden_ref, dqkv_ref, bias_ref, dxn1_ref, *scratch):
+               q_ref, k_ref, v_ref, att_ref, lse_ref, shared_hbm,
+               dh_hbm, gate_out, up_out, down_out, gate_out1, up_out1, dots_ref, dxn2_ref, dhidden_ref, outg_ref, qkvg_ref, bias_ref, dxn1_ref, *scratch):
         scratch, split = list(scratch), []
         for one in sets:
             split.append(scratch[: len(one)])
             scratch = scratch[len(one) :]
-        sums, dh_own, dh_all, part_ref, datt_ref, dq_acc, dk_acc, dv_acc, keep_sem = split[0]
+        sums, dh_own, dh_all, part_ref, dqkv_ref, dq_acc, dk_acc, dv_acc, shared_ref, keep_sem = split[0]
         spot = Spot()
         first = Sum(spot, send_ref, sums, split[1])
         share = Share(spot, dh_own, dh_all, split[2])
         second = Sum(spot, part_ref, dxn1_ref, split[3])
-        items = [up_item(upg_ref, 0, gate_out, up_out, block, parts), down_item(downg_ref, 0, down_out, parts)]
-        back = Return(spot, items, split[4][:2], split[4][2:4], split[4][4:])
-        keep = pltpu.make_async_copy(dh_all, dh_hbm, keep_sem)
+        items = [
+            up_item(upg_ref, 0, 0, gate_out, up_out, block, parts),
+            down_item(downg_ref, 0, 0, down_out, parts),
+            up_item(upg_ref, 1, 1, gate_out1, up_out1, block, parts),
+        ]
+        back = Return(spot, items, split[4][:3], split[4][3:6], split[4][6:])
+        keep = pltpu.make_async_copy(dh_all, dh_hbm, keep_sem.at[0])
+        fetch = pltpu.make_async_copy(shared_hbm, shared_ref, keep_sem.at[1])
 
         def owner():
             lane = lax.broadcasted_iota(jnp.int32, (rows, 128), 1)
@@ -1520,7 +1630,7 @@
 
         def project(index, carry):
             at = pl.ds(pl.multiple_of(index * step, step), step)
-            cosine, sine_part = turn_tables(turn_ref[at, :])
+            cosine, sine_part = turn_tables(shared_ref[at, width:])
             dq, dk, dv = dq_acc[at, :], dk_acc[at, :] * scale, dv_acc[at, :]
             dq = dq * cosine - pltpu.roll(dq, HEAD_DIM // 2, 1) * sine_part
             dk = dk * cosine - pltpu.roll(dk, HEAD_DIM // 2, 1) * sine_part
@@ -1530,10 +1640,17 @@
             part_ref[at, :] = dot_nt(dqkv_ref[at, :], wqkv_ref[...]).astype(bf16)
             return carry
 
+        def features(index, carry):
+            at = pl.ds(pl.multiple_of(index * step, step), step)
+            qkvg_ref[at, :] = dot_tn(shared_ref[:, at], dqkv_ref[...]).astype(bf16)
+            outg_ref[:, at] = dot_tn(att_ref[...], dh_all[:, at]).astype(bf16)
+            return carry
+
         spot.greet(True, True)
         first.begin()
-        back.start(0)
-        back.start(1)
+        for number in range(3):
+            back.start(number)
+        fetch.start()
         dk_acc[...] = jnp.zeros_like(dk_acc)
         dv_acc[...] = jnp.zeros_like(dv_acc)
         bias_ref[...] = jnp.zeros_like(bias_ref)
@@ -1552,17 +1669,21 @@
         back.reduce(0, 3)
         share.end()
         keep.start()
-        back.reduce(1, 0)
-        back.reduce(1, 1)
+        for index in range(parts):
+            back.reduce(1, index)
         lax.fori_loop(0, length // step, attend, 0)
+        fetch.wait()
         lax.fori_loop(0, length // step, project, 0)
         second.begin()
-        back.reduce(1, 2)
+        back.reduce(2, 0)
         for index in range(parts):
             second.cross(index)
-        back.reduce(1, 3)
+        back.reduce(2, 1)
+        lax.fori_loop(0, width // step, features, 0)
         for index in range(parts):
             second.line(index)
+        back.reduce(2, 2)
+        back.reduce(2, 3)
         first.end()
         second.end()
         back.end()
@@ -1578,18 +1699,21 @@
             piece,
             piece,
             jax.ShapeDtypeStruct((units, lanes), bf16),
+            piece,
+            piece,
             jax.ShapeDtypeStruct((rows, 128), f32),
             jax.ShapeDtypeStruct((rows, width), f32),
             jax.ShapeDtypeStruct((rows, width), f32),
-            jax.ShapeDtypeStruct((length, 3 * HEAD_DIM), bf16),
+            jax.ShapeDtypeStruct((HEAD_DIM, width), bf16),
+            jax.ShapeDtypeStruct((width, 3 * HEAD_DIM), bf16),
             jax.ShapeDtypeStruct((1, 3 * HEAD_DIM), f32),
             jax.ShapeDtypeStruct((rows, width), f32),
         ],
-        [IN_PLACE] * 4 + [IN_VMEM] * 6,
-        [IN_VMEM, IN_PLACE, IN_PLACE] + [IN_VMEM] * 14,
+        [IN_PLACE] * 6 + [IN_VMEM] * 7,
+        [IN_VMEM, IN_PLACE, IN_PLACE] + [IN_VMEM] * 13 + [IN_PLACE],
         [one for group in sets for one in group],
         250_000_000,
-    )(send4, up_grads, down_grads, hidden, grad, gain, chances, named, router, out_w, qkv_w, *heads, lse, turns)
+    )(send4, up_grads, down_grads, hidden, grad, gain, chances, named, router, out_w, qkv_w, *heads, lse, shared)
 
 
 class Group:
@@ -1667,15 +1791,14 @@
         self.out[...] = self.out[...] + self.got[index]
 
 
-def last_exchange(up_grads, down_grads, out_grads, qkv_grads, branch, hidden, tokens_grad, small, ups, downs, number):
+def last_exchange(down_grads, out_grads, qkv_grads, both, dup, act, branch, hidden, tokens_grad, small, number):
     parts = lax.axis_size("context")
-    block = up_grads.shape[0] // (2 * parts)
-    lanes = down_grads.shape[1] // (2 * parts)
+    rows, width = hidden.shape
+    block = lanes = width // (2 * parts)
     units = WINDOW * parts - 128
     head, span = out_grads.shape[0], qkv_grads.shape[1]
-    rows, width = hidden.shape
-    shapes = [(head, lanes), (block, span)] + [(block, 2 * WINDOW)] * len(ups) + [(WINDOW, lanes)] * len(downs)
-    pieces = [1, 1] + [2] * len(ups) + [1] * len(downs)
+    shapes = [(head, lanes), (block, span), (WINDOW, lanes), (block, 2 * WINDOW), (WINDOW, lanes)]
+    pieces = [1, 1, 1, 2, 1]
     count, bf16 = len(shapes), jnp.bfloat16
     groups = [
         Return.scratch(shapes, pieces, parts),
@@ -1683,23 +1806,31 @@
         Total.scratch(small.shape),
         Group.sems(),
         Group.sems(),
+        Grads.scratch() + [pltpu.VMEM(both.shape, bf16), pltpu.VMEM(dup.shape, bf16), pltpu.VMEM(act.shape, bf16), DMA((3,))],
     ]
     piece, column = jax.ShapeDtypeStruct((block, units), bf16), jax.ShapeDtypeStruct((units, lanes), bf16)
     out_shape = [jax.ShapeDtypeStruct((parts * head, lanes), bf16), jax.ShapeDtypeStruct((parts * block, span), bf16)]
-    out_shape += [piece] * (2 * len(ups)) + [column] * len(downs)
+    out_shape += [column, piece, piece, column]
     out_shape += [
+        jax.ShapeDtypeStruct((width, 2 * WINDOW), bf16),
+        jax.ShapeDtypeStruct((WINDOW, width), bf16),
         jax.ShapeDtypeStruct((4 * rows, width), bf16),
         jax.ShapeDtypeStruct((4 * rows, width), jnp.float32),
         jax.ShapeDtypeStruct(small.shape, jnp.float32),
     ]
 
-    def kernel(upg_ref, downg_ref, outg_ref, qkvg_ref, branch_ref, hidden_ref, tokens_ref, small_ref, *rest):
+    def kernel(downg_ref, outg_ref, qkvg_ref, both_hbm, dup_hbm, act_hbm, branch_ref, hidden_ref, tokens_ref, small_ref, *rest):
         outs, scratch = rest[: len(out_shape)], list(rest[len(out_shape) :])
         sets = []
         for one in groups:
             sets.append(scratch[: len(one)])
             scratch = scratch[len(one) :]
-        grads, (block_all, tokens_all, small_out) = outs[:-3], outs[-3:]
+        grads, (upg2_hbm, downg2_hbm, block_all, tokens_all, small_out) = outs[:-5], outs[-5:]
+        *grad_refs, both_ref, dup_ref, act_ref, load = sets[5]
+        loads = [
+            pltpu.make_async_copy(source, target, load.at[index])
+            for index, (source, target) in enumerate(((both_hbm, both_ref), (dup_hbm, dup_ref), (act_hbm, act_ref)))
+        ]
         items = [
             {
                 "block": lambda side, part: lanes_at(outg_ref, (side * parts + part) * lanes, lanes),
@@ -1710,8 +1841,11 @@
                 "pieces": [(lambda buf, short: buf, lambda source, short: rows_at(grads[1], source * block, block))],
             },
         ]
-        items += [up_item(upg_ref, k, grads[2 + 2 * i], grads[3 + 2 * i], block, parts) for i, k in enumerate(ups)]
-        items += [down_item(downg_ref, k, grads[2 + 2 * len(ups) + i], parts) for i, k in enumerate(downs)]
+        items += [
+            down_item(downg_ref, 1, 1, grads[2], parts),
+            up_item(upg2_hbm, 0, 2, grads[3], grads[4], block, parts),
+            down_item(downg2_hbm, 0, 2, grads[5], parts),
+        ]
         spot = Spot()
         back = Return(spot, items, sets[0][:count], sets[0][count : 2 * count], sets[0][2 * count :])
         total_branch, own_block = sets[1][-2:]
@@ -1722,16 +1856,16 @@
         spot.greet(True, True)
         total.begin()
         summed.begin()
-        back.start(0)
-        back.start(1)
+        for item in range(3):
+            back.start(item)
+        for copy in loads:
+            copy.start()
         total.take(0)
         total.send(1)
         for index in range(parts):
             summed.cross(index)
         total.take(1)
         total.send(2)
-        for item in range(2, count):
-            back.start(item)
         for index in range(parts):
             back.reduce(0, index)
         total.take(2)
@@ -1740,14 +1874,17 @@
             back.reduce(1, index)
         total.take(3)
         total.send(4)
-        summed.line(0)
-        summed.line(1)
+        for copy in loads:
+            copy.wait()
+        Grads(both_ref, width, dup_ref, act_ref, upg2_hbm, downg2_hbm, *grad_refs).run()
+        back.start(3)
+        back.start(4)
+        for index in range(parts):
+            back.reduce(2, index)
         total.take(4)
         tokens_group.begin()
-        back.reduce(2, 0)
-        summed.line(2)
-        back.reduce(2, 1)
-        summed.line(3)
+        for index in range(parts):
+            summed.line(index)
         half = width // 2
 
         def finish(at, start, step):
@@ -1765,8 +1902,6 @@
 
         summed.chunks(finish)
         block_group.begin()
-        for index in range(2, parts):
-            back.reduce(2, index)
         for item in range(3, count):
             for index in range(parts):
                 back.reduce(item, index)
@@ -1781,10 +1916,42 @@
         "last_exchange",
         out_shape,
         [IN_PLACE] * (len(out_shape) - 1) + [IN_VMEM],
-        [IN_PLACE] * 4 + [IN_VMEM] * 4,
+        [IN_PLACE] * 6 + [IN_VMEM] * 4,
         [one for group in groups for one in group],
         300_000_000,
-    )(up_grads, down_grads, out_grads, qkv_grads, branch, hidden, tokens_grad, small)
+    )(down_grads, out_grads, qkv_grads, both, dup, act, branch, hidden, tokens_grad, small)
+
+
+def widen(singles, pairs):
+    steps = 8
+
+    def spec(shape):
+        if len(shape) == 3:
+            return pl.BlockSpec((shape[0], shape[1] // steps, shape[2]), lambda i: (0, i, 0))
+        return pl.BlockSpec((shape[0] // steps, shape[1]), lambda i: (i, 0))
+
+    kinds = [jnp.bfloat16 if keep else jnp.float32 for _, keep in singles]
+    arrays = [array for array, _ in singles] + [one for pair in pairs for one in pair]
+    out_shape = [jax.ShapeDtypeStruct(array.shape, kind) for (array, _), kind in zip(singles, kinds)]
+    out_shape += [jax.ShapeDtypeStruct((2,) + pair[0].shape, jnp.float32) for pair in pairs]
+    count = len(singles)
+
+    def kernel(*refs):
+        sources, targets = refs[: len(arrays)], refs[len(arrays) :]
+        for source, target in zip(sources[:count], targets[:count]):
+            target[...] = source[...].astype(target.dtype)
+        for index, target in enumerate(targets[count:]):
+            for which in range(2):
+                target[which] = sources[count + 2 * index + which][...].astype(jnp.float32)
+
+    return pl.pallas_call(
+        kernel,
+        grid=(steps,),
+        in_specs=[spec(array.shape) for array in arrays],
+        out_specs=[spec(one.shape) for one in out_shape],
+        out_shape=out_shape,
+        name="widen",
+    )(*arrays)
 
 
 def split_body(
@@ -1849,7 +2016,6 @@
     shared1, qkv_w, out_w, down_w, query, key, value, attended, lse, head_sum = attention_first(
         send1, qkv_in, out_weight, bias_here.astype(jnp.float32), shared_w_down, expert_down, 1
     )
-    xn1, turns = shared1[:, :width], shared1[:, width:]
     hidden = token_own + head_sum
     inverse2 = lax.rsqrt(jnp.mean(hidden * hidden, -1, keepdims=True) + EPSILON)
     normed2 = hidden * inverse2
@@ -1873,26 +2039,26 @@
     gates_low = (gates - gates_high.astype(jnp.float32)).astype(bf16)
     send3 = jnp.concatenate([xn2_own, grad_own_b, gates_high, gates_low], 1)
 
-    both, send4, branch_part, dup, act_c = share_move_compute(
+    both, send4, branch_part, dup, act_c, up_g, down_g = share_move_compute(
         send3, shared_w_gate, shared_w_up, expert_gate, expert_up, down_w, 3
     )
-    up_g = dot_tn(both[:, :width], dup).astype(bf16)
-    down_g = dot_tn(act_c, both[:, width : 2 * width]).astype(bf16)
-    send4, up_g, down_g = lax.optimization_barrier((send4, up_g, down_g))
     up_grads, down_grads = [None] * (2 * stacks), [None] * stacks
     side = 128 - expert_count - 1
     chances = jnp.pad(jnp.concatenate([prob, sig_own[:, None]], 1), ((0, 0), (0, side)))
     named_wide = jnp.pad(named, ((0, 0), (0, 128 - expert_count)))
     router_wide = jnp.pad(heads_w.T.astype(jnp.float32), ((0, side), (0, 0)))
     (
-        dhidden_all,
+        _,
         up_grads[0],
         up_grads[1],
         down_grads[0],
+        up_grads[2],
+        up_grads[3],
         dots_own,
         dxn2,
         dhidden,
-        dqkv_b,
+        out_g,
+        qkv_g,
         bias_part,
         dxn1,
     ) = attention_last(
@@ -1909,11 +2075,9 @@
         qkv_w,
         (query, key, value, attended),
         lse,
-        turns,
+        shared1,
         4,
     )
-    out_g = dot_tn(attended, dhidden_all).astype(bf16)
-    qkv_g = dot_tn(xn1, dqkv_b).astype(bf16)
 
     dprob = dots_own[:, :expert_count] * named
     dlogit = prob * (dprob - jnp.sum(prob * dprob, -1, keepdims=True))
@@ -1939,22 +2103,32 @@
             bias_wide.reshape(-1),
         ]
     )
-    out_w_grad, qkv_grad, *others, block_out, tokens_grad, small = last_exchange(
-        up_g,
+    (
+        out_w_grad,
+        qkv_grad,
+        down_grads[1],
+        up_grads[4],
+        up_grads[5],
+        down_grads[2],
+        _,
+        _,
+        block_out,
+        tokens_grad,
+        small,
+    ) = last_exchange(
         down_g,
         out_g,
         qkv_g,
+        both,
+        dup,
+        act_c,
         branch_part,
         hidden,
         own_half_first(tokens_grad_own),
         small.reshape(-1, 128),
-        list(range(1, stacks)),
-        list(range(1, stacks)),
         7,
     )
     small = small.reshape(-1)
-    up_grads[2:] = others[: 2 * (stacks - 1)]
-    down_grads[1:] = others[2 * (stacks - 1) :]
     router_size = width * expert_count
     bias_sum = small[3 * width + router_size :].reshape(group_size, parts, 3, HEAD_DIM)
     bias_grad = jnp.transpose(
@@ -1963,27 +2137,26 @@
 
     qkv_grad = jnp.transpose(
         qkv_grad.reshape(parts, block, 3, HEAD_DIM), (1, 2, 0, 3)
-    ).reshape(block, 3, parts * HEAD_DIM)
-
-    def wide(array):
-        return array.astype(jnp.float32)
+    ).reshape(block, 3, parts * HEAD_DIM).astype(jnp.float32)
+    singles = [(block_out, True), (tokens_grad, False), (out_w_grad, False)]
+    singles += [(up_grads[0], False), (up_grads[1], False), (down_grads[0], False)]
+    pairs = [up_grads[2::2], up_grads[3::2], down_grads[1:]]
+    block_out, tokens_grad, out_w_grad, *shared_grads, gate_grads, up_grads, down_grads = widen(singles, pairs)
 
     return (
         block_out[None],
         tokens_grad[None],
         small[:width],
-        wide(qkv_grad),
+        qkv_grad,
         bias_grad,
-        wide(out_w_grad),
+        out_w_grad,
         small[width : 2 * width],
         small[3 * width : 3 * width + router_size].reshape(width, expert_count),
-        wide(jnp.stack(up_grads[2::2])),
-        wide(jnp.stack(up_grads[3::2])),
-        wide(jnp.stack(down_grads[1:])),
+        gate_grads,
+        up_grads,
+        down_grads,
         small[2 * width : 3 * width],
-        wide(up_grads[0]),
-        wide(up_grads[1]),
-        wide(down_grads[0]),
+        *shared_grads,
     )
 
 

time: 663 us -> 616 us (0.929)
  matrix products: 35.1 us -> 1.58 us
  other arithmetic: 19.3 us -> 8.88 us
  local copies, waits for them, and re-layouts: 21.8 us -> 13.2 us
    dot_general x4 -> x0, matrix products: 34.3 us -> none  [dot_tn(): lax.dot_general(left, right, (((0,), (0,)), ((), ())), preferred_element_...]
    pallas_call x1, Pallas kernels: 138 us -> 170 us  [attention_last(): comm_call(kernel, number, 'attention_last', [jax.ShapeDtypeStruct((length...]
    pallas_call x1, Pallas kernels: 155 us -> 125 us  [last_exchange(): comm_call(kernel, number, 'last_exchange', out_shape, [IN_PLACE] * (len(o...]
    pallas_call x1, Pallas kernels: 169 us -> 156 us  [share_move_compute(): comm_call(kernel, number, 'share_move_compute', [jax.ShapeDtypeStruct((le...]
    convert_element_type x7 -> x0, other arithmetic: 10.8 us -> none  [wide(): return array.astype(jnp.float32)]
    pallas_call x0 -> x1, Pallas kernels: none -> 10.8 us  [widen(): pl.pallas_call(kernel, grid=(steps,), in_specs=[spec(array.shape) for arr...]
where the time goes in v4:
time: 616 us; the launch traced here: 604 us
  Pallas kernels  579 us (94%)
  local copies, waits for them, and re-layouts  13.2 us (2%)
  other arithmetic  8.88 us (1%)
    pallas_call x1, Pallas kernels, attention_last(): comm_call(kernel, number, 'attention_last', [jax.ShapeDtypeStruct((length...  170 us
    pallas_call x1, Pallas kernels, share_move_compute(): comm_call(kernel, number, 'share_move_compute', [jax.ShapeDtypeStruct((le...  156 us
    pallas_call x1, Pallas kernels, last_exchange(): comm_call(kernel, number, 'last_exchange', out_shape, [IN_PLACE] * (len(o...  125 us
    pallas_call x1, Pallas kernels, attention_first(): comm_call(kernel, number, 'attention_first', [jax.ShapeDtypeStruct((lengt...  117 us

profile of v4, /device:TPU:16, one launch (start us, length us, event | category | flops | bytes accessed | tf_op | source)
XLA Modules:
  0.0 604.2 jit_solution(16050733638308652501)
XLA Ops:
  0.7 1.1 dynamic-slice_bitcast_fusion
  2.8 0.7 pad_maximum_fusion.own_ref
  3.5 0.7 convert_bitcast_fusion
  4.2 0.6 copy.113
  4.9 0.7 copy.89
  5.8 1.2 copy.91.qkv_ref
  7.0 117.2 %attention_first.1 = (bf16[1024,2304]{1,0:T(8,128)(2,1)}, bf16[2048,384]{1,0:T(8,128)(2,1)}, bf16[128,2048]{1,0:T(8,128)(2,1)}, bf16[1152,2048]{1,0:T(8,128)(2,1...) custom-call(bf16[64,2304]{1,0:T(8,128)(2,1)} %pad_maximum_fusion.own, ...), custom_call_target="tpu_custom_call" | custom-call | bytes 250000000 | tf_op jit(solution)/shard_map/attention_first/pallas_call | solution.py:1291
  124.2 1.2 multiply_reduce_fusion.1
  126.8 0.9 concatenate.64.own_ref
  127.8 155.9 %share_move_compute.1 = (bf16[1024,4224]{1,0:T(8,128)(2,1)}, bf16[1024,2176]{1,0:T(8,128)(2,1)}, bf16[1024,2048]{1,0:T(8,128)(2,1)}, bf16[1024,768]{1,0:T(8,128)...) custom-call(bf16[64,4224]{1,0:T(8,128)(2,1)} %concatenate.64.own_ref, ...), custom_call_target="tpu_custom_call" | custom-call | bytes 300000000 | tf_op jit(solution)/shard_map/share_move_compute/pallas_call | solution.py:1486
  283.7 0.6 pad.19.chance_ref
  284.3 1.1 pad_convert_fusion.router_ref
  285.4 0.6 pad.20.named_ref
  286.0 169.7 %attention_last.1 = (bf16[1024,2048]{1,0:T(8,128)(2,1)}, bf16[256,1408]{1,0:T(8,128)(2,1)}, bf16[256,1408]{1,0:T(8,128)(2,1)}, bf16[1408,256]{1,0:T(8,128)(2,1)}...) custom-call(bf16[1024,2176]{1,0:T(8,128)(2,1)} %get-tuple-element.65, ...), custom_call_target="tpu_custom_call" | custom-call | bytes 250000000 | tf_op jit(solution)/shard_map/attention_last/pallas_call | solution.py:1693
  455.7 0.9 multiply_reduce_fusion.2
  456.7 1.2 fusion.18
  457.9 0.3 copy.98
  458.2 0.5 reshape.137
  458.9 0.2 fusion.33
  459.1 1.2 multiply_reduce_fusion
  460.4 0.3 fusion.9
  461.1 0.9 maximum_select_fusion.tokens_ref
  461.9 125.1 %last_exchange.1 = (bf16[512,256]{1,0:T(8,128)(2,1)}, bf16[1024,384]{1,0:T(8,128)(2,1)}, bf16[1408,256]{1,0:T(8,128)(2,1)}, bf16[256,1408]{1,0:T(8,128)(2,1)}, b...) custom-call(bf16[768,2048]{1,0:T(8,128)(2,1)} %get-tuple-element.64., ...), custom_call_target="tpu_custom_call" | custom-call | bytes 300000000 | tf_op jit(solution)/shard_map/last_exchange/pallas_call | solution.py:1913
  587.1 10.8 %widen.1 = (bf16[256,2048]{1,0:T(8,128)(2,1)}, f32[256,2048]{1,0:T(8,128)}, f32[512,256]{1,0:T(8,128)}, f32[256,1408]{1,0:T(8,128)}, f32[256,1408]{1,0:T(8,128)}...) custom-call(bf16[256,2048]{1,0:T(8,128)(2,1)} %get-tuple-element.86.refs_0_,, ...), custom_call_target="tpu_custom_call" | custom-call | tf_op jit(solution)/shard_map/widen/pallas_call | solution.py:1947
  597.9 0.3 copy.99
  598.2 0.7 reshape.145
  599.0 0.3 copy.100
  599.3 1.6 copy.102
  600.9 0.6 reshape.142
  601.5 0.9 copy.103
  602.5 0.6 copy.111
  603.1 0.6 slice_bitcast_fusion
  (95 shorter events, 3.1 us)
Async XLA Ops:
  0.6 125.5 %copy-start = (s32[1,256,4]{1,2,0:T(4,128)S(1)}, s32[1,256,4]{1,2,0:T(4,128)}, u32[]{:S(2)}) copy-start(s32[1,256,4]{1,2,0:T(4,128)} %param.19) | copy-start | bytes 12292
  0.7 1.4 copy-start.16
  0.7 1.4 copy-start.15
  0.7 1.6 copy-start.18
  0.7 4.1 copy-start.6
  2.2 123.3 %copy-start.13 = (f32[2048]{0:T(1024)}, f32[2048]{0:T(1024)S(1)}, u32[]{:S(2)}) copy-start(f32[2048]{0:T(1024)S(1)} %get-tuple-element.241) | copy-start | bytes 24580
  7.0 118.5 %copy-start.11 = (bf16[2048,8]{0,1:T(8,128)(2,1)S(1)}, bf16[2048,8]{0,1:T(8,128)(2,1)}, u32[]{:S(2)}) copy-start(bf16[2048,8]{0,1:T(8,128)(2,1)} %param.26) | copy-start | bytes 98308
  7.0 118.6 %copy-start.14 = (bf16[2048]{0:T(1024)(128)(2,1)S(1)}, bf16[2048]{0:T(1024)(128)(2,1)}, u32[]{:S(2)}) copy-start(bf16[2048]{0:T(1024)(128)(2,1)} %param.30) | copy-start | bytes 12292
  125.4 2.4 copy-start.2
  126.8 156.8 %copy-start.4 = (bf16[64,2048]{1,0:T(8,128)(2,1)}, bf16[64,2048]{1,0:T(8,128)(2,1)S(1)}, u32[]{:S(2)}) copy-start(bf16[64,2048]{1,0:T(8,128)(2,1)S(1)} %maximum_select_fusion.2.grad_ref) | copy-start | bytes 786436
  455.7 3.0 copy-start.9
  455.7 3.4 copy-start.3
  456.7 3.7 copy-start.5
  457.9 2.8 copy-start.17
  458.2 2.6 copy-start.8
  460.8 1.1 copy-start.10
  587.1 10.8 %copy-start.7 = (bf16[1024,384]{1,0:T(8,128)(2,1)S(1)}, bf16[1024,384]{1,0:T(8,128)(2,1)}, u32[]{:S(2)}) copy-start(bf16[1024,384]{1,0:T(8,128)(2,1)} %get-tuple-element.101) | copy-start | bytes 2359300
  599.3 1.6 copy-start.12
  599.3 4.4 copy-start.1

commit v5 on v4

--- a/solution.py
+++ b/solution.py
@@ -1002,10 +1002,13 @@
         item, slot = self.items[number], number * self.spot.parts + part
         return pltpu.make_async_copy(item["block"](0, part), self.mine_buf[number].at[part], self.load.at[slot])
 
+    def start_one(self, number, index):
+        self.swap(number, self.order[index]).start()
+        self.fetch(number, self.order[index]).start()
+
     def start(self, number):
-        for part in self.order:
-            self.swap(number, part).start()
-            self.fetch(number, part).start()
+        for index in range(self.spot.parts):
+            self.start_one(number, index)
 
     def piece(self, number, which, target, source, short):
         s = self.spot
@@ -1060,8 +1063,8 @@
 
 
 class Grads:
-    def __init__(self, both, width, dup, act, up_out, down_out, up_buf, down_buf, up_s, down_s):
-        self.both, self.width, self.dup, self.act = both, width, dup, act
+    def __init__(self, rows, cotangents, dup, act, up_out, down_out, up_buf, down_buf, up_s, down_s):
+        self.rows, self.cotangents, self.dup, self.act = rows, cotangents, dup, act
         self.up_out, self.down_out, self.up_buf, self.down_buf = up_out, down_out, up_buf, down_buf
         self.up_s, self.down_s = up_s, down_s
         self.step = 256
@@ -1080,7 +1083,7 @@
         )
 
     def run(self):
-        count = self.width // self.step
+        count = self.cotangents.shape[1] // self.step
 
         def one(index, carry):
             up_copy, down_copy = self.copies(index)
@@ -1092,9 +1095,9 @@
 
             slot = lax.rem(index, 2)
             at = pl.multiple_of(index * self.step, self.step)
-            up = dot_tn(self.both[:, pl.ds(at, self.step)], self.dup[...])
+            up = dot_tn(self.rows[:, pl.ds(at, self.step)], self.dup[...])
             self.up_buf[slot] = up.astype(jnp.bfloat16)
-            down = dot_tn(self.act[...], self.both[:, pl.ds(self.width + at, self.step)])
+            down = dot_tn(self.act[...], self.cotangents[:, pl.ds(at, self.step)])
             self.down_buf[slot] = down.astype(jnp.bfloat16)
             up_copy().start()
             down_copy().start()
@@ -1158,7 +1161,7 @@
     return jnp.where(low, both, swapped), jnp.where(low, -swapped, both)
 
 
-def attention_first(value, qkv_in, out_weight, bias, shared_down, expert_down, number):
+def attention_first(value, grad, qkv_in, out_weight, bias, shared_down, expert_down, number):
     parts = lax.axis_size("context")
     rows, wide = value.shape
     block, span = qkv_in.shape[0] // parts, qkv_in.shape[1]
@@ -1179,10 +1182,11 @@
         Share.sems(parts),
         Move.sems(2 + count, parts),
         Sum.scratch(parts, rows, width),
+        Share.sems(parts),
     ]
 
-    def kernel(own_ref, qkv_ref, outw_ref, bias_ref, shared_ref, expert_ref,
-               all_hbm, wqkv_hbm, wout_hbm, wd_ref, q_ref, k_ref, v_ref, att_ref, lse_ref, sum_ref, *scratch):
+    def kernel(own_ref, grad_ref, qkv_ref, outw_ref, bias_ref, shared_ref, expert_ref,
+               all_hbm, grad_all, wqkv_hbm, wout_hbm, wd_ref, q_ref, k_ref, v_ref, att_ref, lse_ref, sum_ref, *scratch):
         scratch, split = list(scratch), []
         for one in sets:
             split.append(scratch[: len(one)])
@@ -1190,6 +1194,7 @@
         all_ref, wqkv_ref, wout_ref, part_ref, keep = split[0]
         spot = Spot()
         share = Share(spot, own_ref, all_ref, split[1])
+        grads = Share(spot, grad_ref, grad_all, split[4])
         items = [
             {
                 "src": lambda target, short: rows_at(qkv_ref, target * block, block),
@@ -1261,25 +1266,30 @@
         for gap in (1, 2, 3):
             move.forward(1, gap)
         share.end()
+        grads.begin()
         copies[0].start()
         move.ready(0)
         copies[1].start()
         lax.fori_loop(0, length // step, project, 0)
         move.ready(1)
         copies[2].start()
+        grads.step(1)
         for number in range(3, len(move.items)):
             move.send(number)
         lax.fori_loop(0, length // step, attend, 0)
         summed.begin()
         for gap in (1, 2, 3):
             move.forward(2, gap)
+        grads.step(2)
         for index in range(parts):
             summed.cross(index)
         for number in range(3, len(move.items)):
             for gap in (1, 2, 3):
                 move.forward(number, gap)
+        grads.step(3)
         for index in range(parts):
             summed.line(index)
+        grads.end()
         summed.end()
         for number in range(2, len(move.items)):
             move.ready(number)
@@ -1294,6 +1304,7 @@
         "attention_first",
         [
             jax.ShapeDtypeStruct((length, wide), bf16),
+            jax.ShapeDtypeStruct((length, width), bf16),
             jax.ShapeDtypeStruct((2 * parts * block, span), bf16),
             jax.ShapeDtypeStruct((head, width), bf16),
             jax.ShapeDtypeStruct((count * WINDOW, width), bf16),
@@ -1304,14 +1315,14 @@
             jax.ShapeDtypeStruct((length, HEAD_DIM), f32),
             jax.ShapeDtypeStruct((rows, width), f32),
         ],
-        [IN_PLACE] * 4 + [IN_VMEM] * 6,
-        [IN_VMEM, IN_PLACE, IN_PLACE, IN_VMEM, IN_PLACE, IN_PLACE],
+        [IN_PLACE] * 5 + [IN_VMEM] * 6,
+        [IN_VMEM, IN_VMEM, IN_PLACE, IN_PLACE, IN_VMEM, IN_PLACE, IN_PLACE],
         [one for group in sets for one in group],
         250_000_000,
-    )(value, qkv_in, out_weight, bias, shared_down, expert_down)
-
-
-def share_move_compute(value, shared_gate, shared_up, expert_gate, expert_up, wd, number):
+    )(value, grad, qkv_in, out_weight, bias, shared_down, expert_down)
+
+
+def share_move_compute(value, grad_all, shared_gate, shared_up, expert_gate, expert_up, wd, number):
     parts = lax.axis_size("context")
     rows, wide = value.shape
     width = wd.shape[1]
@@ -1323,27 +1334,30 @@
     step = 256
     f32, bf16 = jnp.float32, jnp.bfloat16
     share_sems, move_sems, grad_scratch = Share.sems(parts), Move.sems(count, parts), Grads.scratch()
+    back_scratch = Return.scratch([(block, 2 * WINDOW)], [2], parts)
     scratch = [
         pltpu.VMEM((length, wide), bf16),
+        pltpu.VMEM((length, width), bf16),
         pltpu.VMEM((2 * parts * block, count * WINDOW), bf16),
         pltpu.VMEM(wd.shape, bf16),
         pltpu.VMEM((length, width), f32),
         pltpu.VMEM((length, width), f32),
         pltpu.VMEM((length, 128), f32),
-        pltpu.VMEM((length, stacks * WINDOW), bf16),
-        pltpu.VMEM((length, count * WINDOW), bf16),
+        pltpu.VMEM((length, 2 * WINDOW), bf16),
+        pltpu.VMEM((length, 4 * WINDOW), bf16),
         pltpu.VMEM((2, step, width + 128), bf16),
         pltpu.VMEM((2, step, width), bf16),
-        DMA((2,)),
+        DMA((3,)),
         DMA((stacks,)),
         DMA((stacks,)),
         DMA((length // step,)),
         DMA((length // step,)),
     ]
 
-    def kernel(own_ref, sg_ref, su_ref, eg_ref, eu_ref, wd_hbm, both_hbm, send_hbm, branch_hbm, dup_hbm, act_hbm, upg_hbm, downg_hbm, *rest):
-        both, wgu, wd_ref, dx_acc, out_acc, dot_acc, act_ref, dup_ref, send_buf, branch_buf, load, act_s, dup_s, send_s, branch_s = rest[: len(scratch)]
+    def kernel(own_ref, grad_hbm, sg_ref, su_ref, eg_ref, eu_ref, wd_hbm, both_hbm, send_hbm, branch_hbm, dup_hbm, act_hbm, upg_hbm, downg_hbm, gate_out, up_out, *rest):
+        both, grads_ref, wgu, wd_ref, dx_acc, out_acc, dot_acc, act_ref, dup_ref, send_buf, branch_buf, load, act_s, dup_s, send_s, branch_s = rest[: len(scratch)]
         grad_refs, sems = rest[len(scratch) : len(scratch) + 4], rest[len(scratch) + 4 :]
+        back_refs, sems = sems[: len(back_scratch)], sems[len(back_scratch) :]
         spot = Spot()
         share = Share(spot, own_ref, both, sems[: len(share_sems)])
 
@@ -1362,7 +1376,9 @@
         move = Move(spot, [item(number) for number in range(count)], sems[len(share_sems) :])
         weights = pltpu.make_async_copy(wd_hbm, wd_ref, load.at[0])
         keep = pltpu.make_async_copy(both, both_hbm, load.at[1])
+        cotangents = pltpu.make_async_copy(grad_hbm, grads_ref, load.at[2])
         column = lax.broadcasted_iota(jnp.int32, (1, 128), 1)
+        pieces = length // step
 
         def send_out(index):
             at = pl.ds(pl.multiple_of(index * step, step), step)
@@ -1372,40 +1388,50 @@
             at = pl.ds(pl.multiple_of(index * step, step), step)
             return pltpu.make_async_copy(branch_buf.at[lax.rem(index, 2)], branch_hbm.at[at, :], branch_s.at[index])
 
+        back = Return(
+            spot, [up_item(upg_hbm, 0, 0, gate_out, up_out, block, parts)], back_refs[:1], back_refs[1:2], back_refs[2:]
+        )
+
+        def slots(k):
+            return pl.ds(2 * (k % 2) * WINDOW, 2 * WINDOW), pl.ds((k % 2) * WINDOW, WINDOW)
+
         def act_out():
-            return pltpu.make_async_copy(act_ref.at[:, pl.ds((stacks - 1) * WINDOW, WINDOW)], act_hbm, act_s.at[0])
+            return pltpu.make_async_copy(act_ref.at[:, slots(stacks - 1)[1]], act_hbm, act_s.at[0])
 
         def dup_out():
-            return pltpu.make_async_copy(dup_ref.at[:, pl.ds(2 * (stacks - 1) * WINDOW, 2 * WINDOW)], dup_hbm, dup_s.at[0])
+            return pltpu.make_async_copy(dup_ref.at[:, slots(stacks - 1)[0]], dup_hbm, dup_s.at[0])
 
         def gradients(k):
             up, down = pl.ds(2 * k * WINDOW, 2 * WINDOW), pl.ds(k * WINDOW, WINDOW)
-            Grads(both, width, dup_ref.at[:, up], act_ref.at[:, down], upg_hbm.at[:, up], downg_hbm.at[down, :], *grad_refs).run()
-
-        def compute(k, first, last):
+            dup_slot, act_slot = slots(k)
+            Grads(both, grads_ref, dup_ref.at[:, dup_slot], act_ref.at[:, act_slot], upg_hbm.at[:, up], downg_hbm.at[down, :], *grad_refs).run()
+
+        def compute(k, halfway):
             up, down = pl.ds(2 * k * WINDOW, 2 * WINDOW), pl.ds(k * WINDOW, WINDOW)
+            dup_slot, act_slot = slots(k)
             at = experts if k == 0 else spot.group * (stacks - 1) + k - 1
             here = jnp.where(column == at, 1.0, 0.0)
             both_parts = jnp.where((column == at) | (column == at + 64), 1.0, 0.0)
 
             def one(index, carry):
+                pl.when(index == pieces // 2)(halfway)
                 rows_here = pl.ds(pl.multiple_of(index * step, step), step)
                 vals = jnp.dot(both[rows_here, :width], wgu[:, up], preferred_element_type=f32)
-                raw = dot_nt(both[rows_here, width : 2 * width], wd_ref[down, :])
-                coef = jnp.sum(both[rows_here, 2 * width :].astype(f32) * both_parts, -1, keepdims=True)
+                raw = dot_nt(grads_ref[rows_here, :], wd_ref[down, :])
+                coef = jnp.sum(both[rows_here, width:].astype(f32) * both_parts, -1, keepdims=True)
                 g_vals, u_vals = vals[:, :WINDOW], vals[:, WINDOW:]
                 sig_g = jax.nn.sigmoid(g_vals)
                 silu_g = g_vals * sig_g
                 act = silu_g * u_vals
                 dots = jnp.sum(raw * act, -1, keepdims=True) * here
-                act_ref[rows_here, down] = (act * coef).astype(bf16)
+                act_ref[rows_here, act_slot] = (act * coef).astype(bf16)
                 dact = raw * coef
-                dup_ref[rows_here, pl.ds(2 * k * WINDOW, WINDOW)] = (
+                dup_ref[rows_here, pl.ds(2 * (k % 2) * WINDOW, WINDOW)] = (
                     dact * u_vals * (sig_g * (1.0 + g_vals * (1.0 - sig_g)))
                 ).astype(bf16)
-                dup_ref[rows_here, pl.ds((2 * k + 1) * WINDOW, WINDOW)] = (dact * silu_g).astype(bf16)
-                out_part = jnp.dot(act_ref[rows_here, down], wd_ref[down, :], preferred_element_type=f32)
-                dx_part = dot_nt(dup_ref[rows_here, up], wgu[:, up])
+                dup_ref[rows_here, pl.ds((2 * (k % 2) + 1) * WINDOW, WINDOW)] = (dact * silu_g).astype(bf16)
+                out_part = jnp.dot(act_ref[rows_here, act_slot], wd_ref[down, :], preferred_element_type=f32)
+                dx_part = dot_nt(dup_ref[rows_here, dup_slot], wgu[:, up])
                 if k == 0:
                     out_acc[rows_here, :] = out_part
                     dx_acc[rows_here, :] = dx_part
@@ -1429,7 +1455,7 @@
                     branch_out(index).start()
                 return carry
 
-            lax.fori_loop(first, last, one, 0)
+            lax.fori_loop(0, pieces, one, 0)
 
         def forward(number):
             for gap in (1, 2, 3):
@@ -1438,6 +1464,7 @@
         spot.greet(True, True)
         share.begin()
         weights.start()
+        cotangents.start()
         for number in range(count):
             move.own(number)
         move.send(0)
@@ -1452,6 +1479,7 @@
         keep.start()
         forward(1)
         weights.wait()
+        cotangents.wait()
         for k in range(stacks):
 
             @pl.when(spot.place == narrow_of(k))
@@ -1461,18 +1489,33 @@
                 for which in (2 * k, 2 * k + 1):
                     wgu[:, pl.ds(which * WINDOW + spare, SPARE)] = jnp.zeros((2 * parts * block, SPARE), bf16)
 
-        pieces = length // step
         for k in range(stacks):
-            if k < stacks - 1:
+            last = k == stacks - 1
+            if not last:
                 forward(2 * k + 2)
+                if k == stacks - 2:
+                    back.start_one(0, 1)
+            else:
+                back.reduce(0, 0)
+                back.reduce(0, 1)
             move.ready(2 * k)
             move.ready(2 * k + 1)
-            compute(k, 0, pieces // 2)
-            if k < stacks - 1:
-                forward(2 * k + 3)
-            compute(k, pieces // 2, pieces)
-            if k < stacks - 1:
+
+            def halfway():
+                if last:
+                    back.reduce(0, 2)
+                else:
+                    forward(2 * k + 3)
+                if k == stacks - 2:
+                    back.start_one(0, 2)
+                    back.start_one(0, 3)
+
+            compute(k, halfway)
+            if not last:
                 gradients(k)
+            if k == 0:
+                back.start_one(0, 0)
+        back.reduce(0, 3)
         act_out().start()
         dup_out().start()
         for index in (pieces - 2, pieces - 1):
@@ -1482,6 +1525,7 @@
         dup_out().wait()
         keep.wait()
         move.sent()
+        back.end()
 
     return comm_call(
         kernel,
@@ -1495,12 +1539,14 @@
             jax.ShapeDtypeStruct((length, WINDOW), bf16),
             jax.ShapeDtypeStruct((width, 2 * (stacks - 1) * WINDOW), bf16),
             jax.ShapeDtypeStruct(((stacks - 1) * WINDOW, width), bf16),
+            jax.ShapeDtypeStruct(shared_gate.shape, bf16),
+            jax.ShapeDtypeStruct(shared_gate.shape, bf16),
         ],
-        [IN_PLACE] * 7,
-        [IN_VMEM] + [IN_PLACE] * 5,
-        scratch + grad_scratch + share_sems + move_sems,
+        [IN_PLACE] * 9,
+        [IN_VMEM] + [IN_PLACE] * 6,
+        scratch + grad_scratch + back_scratch + share_sems + move_sems,
         300_000_000,
-    )(value, shared_gate, shared_up, expert_gate, expert_up, wd)
+    )(value, grad_all, shared_gate, shared_up, expert_gate, expert_up, wd)
 
 
 def up_item(grads_ref, at, k, gate_ref, up_ref, block, parts):
@@ -1546,7 +1592,7 @@
     experts = 8
     scale = HEAD_DIM ** (-0.5)
     f32, bf16 = jnp.float32, jnp.bfloat16
-    shapes, pieces = [(block, 2 * WINDOW), (WINDOW, lanes), (block, 2 * WINDOW)], [2, 1, 2]
+    shapes, pieces = [(WINDOW, lanes), (block, 2 * WINDOW)], [1, 2]
     sets = [
         [
             pltpu.VMEM((rows, wide), f32),
@@ -1568,7 +1614,7 @@
 
     def kernel(send_ref, upg_ref, downg_ref, hidden_ref, grad_ref, gain_ref, chance_ref, named_ref, router_ref, wout_ref, wqkv_ref,
                q_ref, k_ref, v_ref, att_ref, lse_ref, shared_hbm,
-               dh_hbm, gate_out, up_out, down_out, gate_out1, up_out1, dots_ref, dxn2_ref, dhidden_ref, outg_ref, qkvg_ref, bias_ref, dxn1_ref, *scratch):
+               dh_hbm, down_out, gate_out1, up_out1, dots_ref, dxn2_ref, dhidden_ref, outg_ref, qkvg_ref, bias_ref, dxn1_ref, *scratch):
         scratch, split = list(scratch), []
         for one in sets:
             split.append(scratch[: len(one)])
@@ -1579,11 +1625,10 @@
         share = Share(spot, dh_own, dh_all, split[2])
         second = Sum(spot, part_ref, dxn1_ref, split[3])
         items = [
-            up_item(upg_ref, 0, 0, gate_out, up_out, block, parts),
             down_item(downg_ref, 0, 0, down_out, parts),
             up_item(upg_ref, 1, 1, gate_out1, up_out1, block, parts),
         ]
-        back = Return(spot, items, split[4][:3], split[4][3:6], split[4][6:])
+        back = Return(spot, items, split[4][:2], split[4][2:4], split[4][4:])
         keep = pltpu.make_async_copy(dh_all, dh_hbm, keep_sem.at[0])
         fetch = pltpu.make_async_copy(shared_hbm, shared_ref, keep_sem.at[1])
 
@@ -1648,7 +1693,7 @@
 
         spot.greet(True, True)
         first.begin()
-        for number in range(3):
+        for number in range(2):
             back.start(number)
         fetch.start()
         dk_acc[...] = jnp.zeros_like(dk_acc)
@@ -1667,23 +1712,21 @@
         back.reduce(0, 2)
         share.step(3)
         back.reduce(0, 3)
+        back.reduce(1, 0)
         share.end()
         keep.start()
-        for index in range(parts):
-            back.reduce(1, index)
+        back.reduce(1, 1)
+        back.reduce(1, 2)
         lax.fori_loop(0, length // step, attend, 0)
         fetch.wait()
         lax.fori_loop(0, length // step, project, 0)
         second.begin()
-        back.reduce(2, 0)
+        back.reduce(1, 3)
         for index in range(parts):
             second.cross(index)
-        back.reduce(2, 1)
         lax.fori_loop(0, width // step, features, 0)
         for index in range(parts):
             second.line(index)
-        back.reduce(2, 2)
-        back.reduce(2, 3)
         first.end()
         second.end()
         back.end()
@@ -1696,8 +1739,6 @@
         "attention_last",
         [
             jax.ShapeDtypeStruct((length, width), bf16),
-            piece,
-            piece,
             jax.ShapeDtypeStruct((units, lanes), bf16),
             piece,
             piece,
@@ -1709,7 +1750,7 @@
             jax.ShapeDtypeStruct((1, 3 * HEAD_DIM), f32),
             jax.ShapeDtypeStruct((rows, width), f32),
         ],
-        [IN_PLACE] * 6 + [IN_VMEM] * 7,
+        [IN_PLACE] * 4 + [IN_VMEM] * 7,
         [IN_VMEM, IN_PLACE, IN_PLACE] + [IN_VMEM] * 13 + [IN_PLACE],
         [one for group in sets for one in group],
         250_000_000,
@@ -1791,7 +1832,7 @@
         self.out[...] = self.out[...] + self.got[index]
 
 
-def last_exchange(down_grads, out_grads, qkv_grads, both, dup, act, branch, hidden, tokens_grad, small, number):
+def last_exchange(down_grads, out_grads, qkv_grads, both, cotangents, dup, act, branch, hidden, tokens_grad, small, number):
     parts = lax.axis_size("context")
     rows, width = hidden.shape
     block = lanes = width // (2 * parts)
@@ -1806,7 +1847,7 @@
         Total.scratch(small.shape),
         Group.sems(),
         Group.sems(),
-        Grads.scratch() + [pltpu.VMEM(both.shape, bf16), pltpu.VMEM(dup.shape, bf16), pltpu.VMEM(act.shape, bf16), DMA((3,))],
+        Grads.scratch() + [pltpu.VMEM(one.shape, bf16) for one in (both, cotangents, dup, act)] + [DMA((4,))],
     ]
     piece, column = jax.ShapeDtypeStruct((block, units), bf16), jax.ShapeDtypeStruct((units, lanes), bf16)
     out_shape = [jax.ShapeDtypeStruct((parts * head, lanes), bf16), jax.ShapeDtypeStruct((parts * block, span), bf16)]
@@ -1819,17 +1860,19 @@
         jax.ShapeDtypeStruct(small.shape, jnp.float32),
     ]
 
-    def kernel(downg_ref, outg_ref, qkvg_ref, both_hbm, dup_hbm, act_hbm, branch_ref, hidden_ref, tokens_ref, small_ref, *rest):
+    def kernel(downg_ref, outg_ref, qkvg_ref, both_hbm, cots_hbm, dup_hbm, act_hbm, branch_ref, hidden_ref, tokens_ref, small_ref, *rest):
         outs, scratch = rest[: len(out_shape)], list(rest[len(out_shape) :])
         sets = []
         for one in groups:
             sets.append(scratch[: len(one)])
             scratch = scratch[len(one) :]
         grads, (upg2_hbm, downg2_hbm, block_all, tokens_all, small_out) = outs[:-5], outs[-5:]
-        *grad_refs, both_ref, dup_ref, act_ref, load = sets[5]
+        *grad_refs, both_ref, cots_ref, dup_ref, act_ref, load = sets[5]
         loads = [
             pltpu.make_async_copy(source, target, load.at[index])
-            for index, (source, target) in enumerate(((both_hbm, both_ref), (dup_hbm, dup_ref), (act_hbm, act_ref)))
+            for index, (source, target) in enumerate(
+                ((both_hbm, both_ref), (cots_hbm, cots_ref), (dup_hbm, dup_ref), (act_hbm, act_ref))
+            )
         ]
         items = [
             {
@@ -1876,7 +1919,7 @@
         total.send(4)
         for copy in loads:
             copy.wait()
-        Grads(both_ref, width, dup_ref, act_ref, upg2_hbm, downg2_hbm, *grad_refs).run()
+        Grads(both_ref, cots_ref, dup_ref, act_ref, upg2_hbm, downg2_hbm, *grad_refs).run()
         back.start(3)
         back.start(4)
         for index in range(parts):
@@ -1916,10 +1959,10 @@
         "last_exchange",
         out_shape,
         [IN_PLACE] * (len(out_shape) - 1) + [IN_VMEM],
-        [IN_PLACE] * 6 + [IN_VMEM] * 4,
+        [IN_PLACE] * 7 + [IN_VMEM] * 4,
         [one for group in groups for one in group],
         300_000_000,
-    )(down_grads, out_grads, qkv_grads, both, dup, act, branch, hidden, tokens_grad, small)
+    )(down_grads, out_grads, qkv_grads, both, cotangents, dup, act, branch, hidden, tokens_grad, small)
 
 
 def widen(singles, pairs):
@@ -2013,8 +2056,8 @@
     bias_here = lax.dynamic_slice_in_dim(
         qkv_bias.reshape(3, parts, HEAD_DIM), place, 1, 1
     ).reshape(1, 3 * HEAD_DIM)
-    shared1, qkv_w, out_w, down_w, query, key, value, attended, lse, head_sum = attention_first(
-        send1, qkv_in, out_weight, bias_here.astype(jnp.float32), shared_w_down, expert_down, 1
+    shared1, grad_all, qkv_w, out_w, down_w, query, key, value, attended, lse, head_sum = attention_first(
+        send1, grad_own_b, qkv_in, out_weight, bias_here.astype(jnp.float32), shared_w_down, expert_down, 1
     )
     hidden = token_own + head_sum
     inverse2 = lax.rsqrt(jnp.mean(hidden * hidden, -1, keepdims=True) + EPSILON)
@@ -2037,20 +2080,19 @@
     )
     gates_high = gates.astype(bf16)
     gates_low = (gates - gates_high.astype(jnp.float32)).astype(bf16)
-    send3 = jnp.concatenate([xn2_own, grad_own_b, gates_high, gates_low], 1)
-
-    both, send4, branch_part, dup, act_c, up_g, down_g = share_move_compute(
-        send3, shared_w_gate, shared_w_up, expert_gate, expert_up, down_w, 3
+    send3 = jnp.concatenate([xn2_own, gates_high, gates_low], 1)
+
+    both, send4, branch_part, dup, act_c, up_g, down_g, *first_grads = share_move_compute(
+        send3, grad_all, shared_w_gate, shared_w_up, expert_gate, expert_up, down_w, 3
     )
     up_grads, down_grads = [None] * (2 * stacks), [None] * stacks
+    up_grads[:2] = first_grads
     side = 128 - expert_count - 1
     chances = jnp.pad(jnp.concatenate([prob, sig_own[:, None]], 1), ((0, 0), (0, side)))
     named_wide = jnp.pad(named, ((0, 0), (0, 128 - expert_count)))
     router_wide = jnp.pad(heads_w.T.astype(jnp.float32), ((0, side), (0, 0)))
     (
         _,
-        up_grads[0],
-        up_grads[1],
         down_grads[0],
         up_grads[2],
         up_grads[3],
@@ -2120,6 +2162,7 @@
         out_g,
         qkv_g,
         both,
+        grad_all,
         dup,
         act_c,
         branch_part,

time: 616 us -> 585 us (0.950); the launches traced: 604 us -> 584 us
  Pallas kernels: 579 us -> 559 us
    pallas_call x1, Pallas kernels: 170 us -> 127 us  [attention_last(): comm_call(kernel, number, 'attention_last', [jax.ShapeDtypeStruct((length...]
    pallas_call x1, Pallas kernels: 156 us -> 176 us  [share_move_compute(): comm_call(kernel, number, 'share_move_compute', [jax.ShapeDtypeStruct((le...]
    pallas_call x1, Pallas kernels: 117 us -> 124 us  [attention_first(): comm_call(kernel, number, 'attention_first', [jax.ShapeDtypeStruct((lengt...]
where the time goes in v5:
time: 585 us; the launch traced here: 584 us
  Pallas kernels  559 us (96%)
  local copies, waits for them, and re-layouts  13 us (2%)
  other arithmetic  9.58 us (2%)
    pallas_call x1, Pallas kernels, share_move_compute(): comm_call(kernel, number, 'share_move_compute', [jax.ShapeDtypeStruct((le...  176 us
    pallas_call x1, Pallas kernels, attention_last(): comm_call(kernel, number, 'attention_last', [jax.ShapeDtypeStruct((length...  127 us
    pallas_call x1, Pallas kernels, attention_first(): comm_call(kernel, number, 'attention_first', [jax.ShapeDtypeStruct((lengt...  124 us
    pallas_call x1, Pallas kernels, last_exchange(): comm_call(kernel, number, 'last_exchange', out_shape, [IN_PLACE] * (len(o...  121 us

profile of v5, /device:TPU:16, one launch (start us, length us, event | category | flops | bytes accessed | tf_op | source)
XLA Modules:
  0.0 584.1 jit_solution(7695797387483624977)
XLA Ops:
  0.7 1.1 dynamic-slice_bitcast_fusion
  2.7 0.7 pad_maximum_fusion.own_ref
  3.5 0.8 maximum_select_fusion.2.grad_ref
  4.2 0.7 convert_bitcast_fusion
  4.9 0.6 copy.113
  5.7 0.7 copy.89
  6.6 1.2 copy.91.qkv_ref
  7.7 123.7 %attention_first.1 = (bf16[1024,2304]{1,0:T(8,128)(2,1)}, bf16[1024,2048]{1,0:T(8,128)(2,1)}, bf16[2048,384]{1,0:T(8,128)(2,1)}, bf16[128,2048]{1,0:T(8,128)(2,1...) custom-call(bf16[64,2304]{1,0:T(8,128)(2,1)} %pad_maximum_fusion.own, ...), custom_call_target="tpu_custom_call" | custom-call | bytes 250000000 | tf_op jit(solution)/shard_map/attention_first/pallas_call | solution.py:1301
  131.4 1.2 multiply_reduce_fusion.1
  134.0 0.8 concatenate.64.own_ref
  134.8 176.1 %share_move_compute.1 = (bf16[1024,2176]{1,0:T(8,128)(2,1)}, bf16[1024,2176]{1,0:T(8,128)(2,1)}, bf16[1024,2048]{1,0:T(8,128)(2,1)}, bf16[1024,768]{1,0:T(8,128)...) custom-call(bf16[64,2176]{1,0:T(8,128)(2,1)} %concatenate.64.own_ref, ...), custom_call_target="tpu_custom_call" | custom-call | bytes 300000000 | tf_op jit(solution)/shard_map/share_move_compute/pallas_call | solution.py:1530
  310.9 0.6 pad.19.chance_ref
  311.5 1.1 pad_convert_fusion.router_ref
  312.6 0.6 pad.20.named_ref
  313.2 127.2 %attention_last.1 = (bf16[1024,2048]{1,0:T(8,128)(2,1)}, bf16[1408,256]{1,0:T(8,128)(2,1)}, bf16[256,1408]{1,0:T(8,128)(2,1)}, bf16[256,1408]{1,0:T(8,128)(2,1)}...) custom-call(bf16[1024,2176]{1,0:T(8,128)(2,1)} %get-tuple-element.67, ...), custom_call_target="tpu_custom_call" | custom-call | bytes 250000000 | tf_op jit(solution)/shard_map/attention_last/pallas_call | solution.py:1736
  440.4 0.9 multiply_reduce_fusion.2
  441.4 1.2 fusion.18
  442.6 0.3 copy.98
  442.9 0.5 reshape.137
  443.8 1.2 multiply_reduce_fusion
  445.0 0.3 fusion.9
  445.8 0.9 maximum_select_fusion.tokens_ref
  446.6 120.8 %last_exchange.1 = (bf16[512,256]{1,0:T(8,128)(2,1)}, bf16[1024,384]{1,0:T(8,128)(2,1)}, bf16[1408,256]{1,0:T(8,128)(2,1)}, bf16[256,1408]{1,0:T(8,128)(2,1)}, b...) custom-call(bf16[768,2048]{1,0:T(8,128)(2,1)} %get-tuple-element.66., ...), custom_call_target="tpu_custom_call" | custom-call | bytes 300000000 | tf_op jit(solution)/shard_map/last_exchange/pallas_call | solution.py:1956
  567.5 10.8 %widen.1 = (bf16[256,2048]{1,0:T(8,128)(2,1)}, f32[256,2048]{1,0:T(8,128)}, f32[512,256]{1,0:T(8,128)}, f32[256,1408]{1,0:T(8,128)}, f32[256,1408]{1,0:T(8,128)}...) custom-call(bf16[256,2048]{1,0:T(8,128)(2,1)} %get-tuple-element.88.refs_0_,, ...), custom_call_target="tpu_custom_call" | custom-call | tf_op jit(solution)/shard_map/widen/pallas_call | solution.py:1990
  578.3 0.3 copy.99
  578.6 0.7 reshape.145
  579.4 0.3 copy.100
  579.7 1.6 copy.102
  581.3 0.6 reshape.142
  581.9 0.9 copy.103
  582.9 0.6 copy.111
  583.5 0.6 slice_bitcast_fusion
  (93 shorter events, 3.3 us)
Async XLA Ops:
  0.6 132.8 %copy-start = (s32[1,256,4]{1,2,0:T(4,128)S(1)}, s32[1,256,4]{1,2,0:T(4,128)}, u32[]{:S(2)}) copy-start(s32[1,256,4]{1,2,0:T(4,128)} %param.19) | copy-start | bytes 12292
  0.7 1.4 copy-start.15
  0.7 1.4 copy-start.14
  0.7 1.6 copy-start.17
  1.8 3.7 copy-start.5
  2.1 130.6 %copy-start.12 = (f32[2048]{0:T(1024)}, f32[2048]{0:T(1024)S(1)}, u32[]{:S(2)}) copy-start(f32[2048]{0:T(1024)S(1)} %get-tuple-element.243) | copy-start | bytes 24580
  7.7 125.1 %copy-start.10 = (bf16[2048,8]{0,1:T(8,128)(2,1)S(1)}, bf16[2048,8]{0,1:T(8,128)(2,1)}, u32[]{:S(2)}) copy-start(bf16[2048,8]{0,1:T(8,128)(2,1)} %param.26) | copy-start | bytes 98308
  7.7 125.1 %copy-start.13 = (bf16[2048]{0:T(1024)(128)(2,1)S(1)}, bf16[2048]{0:T(1024)(128)(2,1)}, u32[]{:S(2)}) copy-start(bf16[2048]{0:T(1024)(128)(2,1)} %param.30) | copy-start | bytes 12292
  132.7 178.2 %copy-start.2 = (f32[64,2048]{1,0:T(8,128)}, f32[64,2048]{1,0:T(8,128)S(1)}, u32[]{:S(2)}) copy-start(f32[64,2048]{1,0:T(8,128)S(1)} %get-tuple-element.208.hidden_ref) | copy-start | bytes 1572868
  440.4 3.0 copy-start.8
  440.4 3.4 copy-start.3
  441.3 3.7 copy-start.4
  442.5 2.8 copy-start.16
  442.9 2.6 copy-start.7
  445.5 1.1 copy-start.9
  567.5 10.8 %copy-start.6 = (bf16[1024,384]{1,0:T(8,128)(2,1)S(1)}, bf16[1024,384]{1,0:T(8,128)(2,1)}, u32[]{:S(2)}) copy-start(bf16[1024,384]{1,0:T(8,128)(2,1)} %get-tuple-element.103) | copy-start | bytes 2359300
  579.6 1.6 copy-start.11
  579.6 4.4 copy-start.1

commit v6 on v5

--- a/solution.py
+++ b/solution.py
@@ -1164,7 +1164,7 @@
 def attention_first(value, grad, qkv_in, out_weight, bias, shared_down, expert_down, number):
     parts = lax.axis_size("context")
     rows, wide = value.shape
-    block, span = qkv_in.shape[0] // parts, qkv_in.shape[1]
+    block, span = qkv_in.shape[1], 3 * HEAD_DIM
     head, lanes = out_weight.shape[0] // parts, out_weight.shape[1]
     width, length = 2 * parts * lanes, rows * parts * 4
     count = 1 + expert_down.shape[0]
@@ -1180,7 +1180,7 @@
             DMA((3,)),
         ],
         Share.sems(parts),
-        Move.sems(2 + count, parts),
+        Move.sems(4 + count, parts),
         Sum.scratch(parts, rows, width),
         Share.sems(parts),
     ]
@@ -1197,10 +1197,15 @@
         grads = Share(spot, grad_ref, grad_all, split[4])
         items = [
             {
-                "src": lambda target, short: rows_at(qkv_ref, target * block, block),
-                "dst": lambda side, source, short: rows_at(wqkv_ref, (side * parts + source) * block, block),
+                "src": lambda target, short, which=which: lanes_at(qkv_ref.at[which], target * HEAD_DIM, HEAD_DIM),
+                "dst": lambda side, source, short, which=which: rows_at(
+                    wqkv_ref.at[:, pl.ds(which * HEAD_DIM, HEAD_DIM)], (side * parts + source) * block, block
+                ),
                 "short": None,
-            },
+            }
+            for which in range(3)
+        ]
+        items += [
             {
                 "src": lambda target, short: rows_at(outw_ref, target * head, head),
                 "dst": lambda side, source, short: lanes_at(wout_ref, (side * parts + source) * lanes, lanes),
@@ -1253,37 +1258,37 @@
         share.begin()
         for number in range(len(move.items)):
             move.own(number)
-        move.send_gap(0, 3)
+        move.send(0)
         share.step(1)
-        move.send_gap(0, 2)
+        move.send(1)
         share.step(2)
-        move.send_gap(0, 1)
+        move.send(2)
         share.step(3)
-        move.send(1)
-        move.send(2)
-        for gap in (1, 2, 3):
-            move.forward(0, gap)
-        for gap in (1, 2, 3):
-            move.forward(1, gap)
+        move.send(3)
+        move.send(4)
+        for number in range(4):
+            for gap in (1, 2, 3):
+                move.forward(number, gap)
         share.end()
         grads.begin()
         copies[0].start()
-        move.ready(0)
+        for number in range(3):
+            move.ready(number)
         copies[1].start()
         lax.fori_loop(0, length // step, project, 0)
-        move.ready(1)
+        move.ready(3)
         copies[2].start()
         grads.step(1)
-        for number in range(3, len(move.items)):
+        for number in range(5, len(move.items)):
             move.send(number)
         lax.fori_loop(0, length // step, attend, 0)
         summed.begin()
         for gap in (1, 2, 3):
-            move.forward(2, gap)
+            move.forward(4, gap)
         grads.step(2)
         for index in range(parts):
             summed.cross(index)
-        for number in range(3, len(move.items)):
+        for number in range(5, len(move.items)):
             for gap in (1, 2, 3):
                 move.forward(number, gap)
         grads.step(3)
@@ -1291,7 +1296,7 @@
             summed.line(index)
         grads.end()
         summed.end()
-        for number in range(2, len(move.items)):
+        for number in range(4, len(move.items)):
             move.ready(number)
         move.sent()
         for copy in copies:
@@ -1345,6 +1350,8 @@
         pltpu.VMEM((length, 128), f32),
         pltpu.VMEM((length, 2 * WINDOW), bf16),
         pltpu.VMEM((length, 4 * WINDOW), bf16),
+        pltpu.VMEM((length, WINDOW), f32),
+        pltpu.VMEM((length, WINDOW), f32),
         pltpu.VMEM((2, step, width + 128), bf16),
         pltpu.VMEM((2, step, width), bf16),
         DMA((3,)),
@@ -1355,7 +1362,7 @@
     ]
 
     def kernel(own_ref, grad_hbm, sg_ref, su_ref, eg_ref, eu_ref, wd_hbm, both_hbm, send_hbm, branch_hbm, dup_hbm, act_hbm, upg_hbm, downg_hbm, gate_out, up_out, *rest):
-        both, grads_ref, wgu, wd_ref, dx_acc, out_acc, dot_acc, act_ref, dup_ref, send_buf, branch_buf, load, act_s, dup_s, send_s, branch_s = rest[: len(scratch)]
+        both, grads_ref, wgu, wd_ref, dx_acc, out_acc, dot_acc, act_ref, dup_ref, raw_ref, gate_ref, send_buf, branch_buf, load, act_s, dup_s, send_s, branch_s = rest[: len(scratch)]
         grad_refs, sems = rest[len(scratch) : len(scratch) + 4], rest[len(scratch) + 4 :]
         back_refs, sems = sems[: len(back_scratch)], sems[len(back_scratch) :]
         spot = Spot()
@@ -1416,10 +1423,16 @@
             def one(index, carry):
                 pl.when(index == pieces // 2)(halfway)
                 rows_here = pl.ds(pl.multiple_of(index * step, step), step)
-                vals = jnp.dot(both[rows_here, :width], wgu[:, up], preferred_element_type=f32)
-                raw = dot_nt(grads_ref[rows_here, :], wd_ref[down, :])
+                if k == stacks - 1:
+                    raw, g_vals = raw_ref[rows_here, :], gate_ref[rows_here, :]
+                    u_vals = jnp.dot(
+                        both[rows_here, :width], wgu[:, pl.ds((2 * k + 1) * WINDOW, WINDOW)], preferred_element_type=f32
+                    )
+                else:
+                    vals = jnp.dot(both[rows_here, :width], wgu[:, up], preferred_element_type=f32)
+                    raw = dot_nt(grads_ref[rows_here, :], wd_ref[down, :])
+                    g_vals, u_vals = vals[:, :WINDOW], vals[:, WINDOW:]
                 coef = jnp.sum(both[rows_here, width:].astype(f32) * both_parts, -1, keepdims=True)
-                g_vals, u_vals = vals[:, :WINDOW], vals[:, WINDOW:]
                 sig_g = jax.nn.sigmoid(g_vals)
                 silu_g = g_vals * sig_g
                 act = silu_g * u_vals
@@ -1457,6 +1470,15 @@
 
             lax.fori_loop(0, pieces, one, 0)
 
+        def prepare(index, carry):
+            rows_here = pl.ds(pl.multiple_of(index * step, step), step)
+            last = stacks - 1
+            raw_ref[rows_here, :] = dot_nt(grads_ref[rows_here, :], wd_ref[pl.ds(last * WINDOW, WINDOW), :])
+            gate_ref[rows_here, :] = jnp.dot(
+                both[rows_here, :width], wgu[:, pl.ds(2 * last * WINDOW, WINDOW)], preferred_element_type=f32
+            )
+            return carry
+
         def forward(number):
             for gap in (1, 2, 3):
                 move.forward(number, gap)
@@ -1499,6 +1521,8 @@
                 back.reduce(0, 0)
                 back.reduce(0, 1)
             move.ready(2 * k)
+            if last:
+                lax.fori_loop(0, pieces, prepare, 0)
             move.ready(2 * k + 1)
 
             def halfway():
@@ -1582,6 +1606,7 @@
 
 
 def attention_last(send4, up_grads, down_grads, hidden, grad, gain, chances, named, router, out_w, qkv_w, heads, lse, shared, number):
+    lazy = [send4, router, out_w, qkv_w, *heads, lse, shared]
     parts = lax.axis_size("context")
     length, width = send4.shape[0], hidden.shape[1]
     rows, wide = hidden.shape[0], send4.shape[1]
@@ -1592,7 +1617,7 @@
     experts = 8
     scale = HEAD_DIM ** (-0.5)
     f32, bf16 = jnp.float32, jnp.bfloat16
-    shapes, pieces = [(WINDOW, lanes), (block, 2 * WINDOW)], [1, 2]
+    shapes, pieces = [(WINDOW, lanes), (block, 2 * WINDOW), (WINDOW, lanes)], [1, 2, 1]
     sets = [
         [
             pltpu.VMEM((rows, wide), f32),
@@ -1603,34 +1628,40 @@
             pltpu.VMEM((length, HEAD_DIM), f32),
             pltpu.VMEM((length, HEAD_DIM), f32),
             pltpu.VMEM((length, HEAD_DIM), f32),
-            pltpu.VMEM(shared.shape, bf16),
-            DMA((2,)),
+            DMA,
         ],
+        [pltpu.VMEM(one.shape, one.dtype) for one in lazy] + [DMA((len(lazy),))],
         Sum.scratch(parts, rows, wide),
         Share.sems(parts),
         Sum.scratch(parts, rows, width),
         Return.scratch(shapes, pieces, parts),
     ]
 
-    def kernel(send_ref, upg_ref, downg_ref, hidden_ref, grad_ref, gain_ref, chance_ref, named_ref, router_ref, wout_ref, wqkv_ref,
-               q_ref, k_ref, v_ref, att_ref, lse_ref, shared_hbm,
-               dh_hbm, down_out, gate_out1, up_out1, dots_ref, dxn2_ref, dhidden_ref, outg_ref, qkvg_ref, bias_ref, dxn1_ref, *scratch):
+    def kernel(upg_ref, downg_ref, hidden_ref, grad_ref, gain_ref, chance_ref, named_ref, *rest):
+        sources, rest = rest[: len(lazy)], rest[len(lazy) :]
+        (dh_hbm, down_out, gate_out1, up_out1, down_out1, dots_ref, dxn2_ref, dhidden_ref, outg_ref, qkvg_ref, bias_ref, dxn1_ref), scratch = rest[:12], rest[12:]
         scratch, split = list(scratch), []
         for one in sets:
             split.append(scratch[: len(one)])
             scratch = scratch[len(one) :]
-        sums, dh_own, dh_all, part_ref, dqkv_ref, dq_acc, dk_acc, dv_acc, shared_ref, keep_sem = split[0]
+        sums, dh_own, dh_all, part_ref, dqkv_ref, dq_acc, dk_acc, dv_acc, keep_sem = split[0]
+        *targets, load = split[1]
+        send_ref, router_ref, wout_ref, wqkv_ref, q_ref, k_ref, v_ref, att_ref, lse_ref, shared_ref = targets
+        loads = [
+            pltpu.make_async_copy(source, target, load.at[index])
+            for index, (source, target) in enumerate(zip(sources, targets))
+        ]
         spot = Spot()
-        first = Sum(spot, send_ref, sums, split[1])
-        share = Share(spot, dh_own, dh_all, split[2])
-        second = Sum(spot, part_ref, dxn1_ref, split[3])
+        first = Sum(spot, send_ref, sums, split[2])
+        share = Share(spot, dh_own, dh_all, split[3])
+        second = Sum(spot, part_ref, dxn1_ref, split[4])
         items = [
             down_item(downg_ref, 0, 0, down_out, parts),
             up_item(upg_ref, 1, 1, gate_out1, up_out1, block, parts),
+            down_item(downg_ref, 1, 1, down_out1, parts),
         ]
-        back = Return(spot, items, split[4][:2], split[4][2:4], split[4][4:])
-        keep = pltpu.make_async_copy(dh_all, dh_hbm, keep_sem.at[0])
-        fetch = pltpu.make_async_copy(shared_hbm, shared_ref, keep_sem.at[1])
+        back = Return(spot, items, split[5][:3], split[5][3:6], split[5][6:])
+        keep = pltpu.make_async_copy(dh_all, dh_hbm, keep_sem)
 
         def owner():
             lane = lax.broadcasted_iota(jnp.int32, (rows, 128), 1)
@@ -1691,11 +1722,13 @@
             outg_ref[:, at] = dot_tn(att_ref[...], dh_all[:, at]).astype(bf16)
             return carry
 
+        for copy in loads:
+            copy.start()
         spot.greet(True, True)
+        loads[0].wait()
         first.begin()
-        for number in range(2):
+        for number in range(3):
             back.start(number)
-        fetch.start()
         dk_acc[...] = jnp.zeros_like(dk_acc)
         dv_acc[...] = jnp.zeros_like(dv_acc)
         bias_ref[...] = jnp.zeros_like(bias_ref)
@@ -1705,6 +1738,8 @@
         back.reduce(0, 1)
         for index in range(parts):
             first.line(index)
+        for copy in loads[1:]:
+            copy.wait()
         owner()
         share.begin()
         share.step(1)
@@ -1717,8 +1752,10 @@
         keep.start()
         back.reduce(1, 1)
         back.reduce(1, 2)
+        back.reduce(2, 0)
+        back.reduce(2, 1)
+        back.reduce(2, 2)
         lax.fori_loop(0, length // step, attend, 0)
-        fetch.wait()
         lax.fori_loop(0, length // step, project, 0)
         second.begin()
         back.reduce(1, 3)
@@ -1727,6 +1764,7 @@
         lax.fori_loop(0, width // step, features, 0)
         for index in range(parts):
             second.line(index)
+        back.reduce(2, 3)
         first.end()
         second.end()
         back.end()
@@ -1742,6 +1780,7 @@
             jax.ShapeDtypeStruct((units, lanes), bf16),
             piece,
             piece,
+            jax.ShapeDtypeStruct((units, lanes), bf16),
             jax.ShapeDtypeStruct((rows, 128), f32),
             jax.ShapeDtypeStruct((rows, width), f32),
             jax.ShapeDtypeStruct((rows, width), f32),
@@ -1750,11 +1789,11 @@
             jax.ShapeDtypeStruct((1, 3 * HEAD_DIM), f32),
             jax.ShapeDtypeStruct((rows, width), f32),
         ],
-        [IN_PLACE] * 4 + [IN_VMEM] * 7,
-        [IN_VMEM, IN_PLACE, IN_PLACE] + [IN_VMEM] * 13 + [IN_PLACE],
+        [IN_PLACE] * 5 + [IN_VMEM] * 7,
+        [IN_PLACE] * 2 + [IN_VMEM] * 5 + [IN_PLACE] * len(lazy),
         [one for group in sets for one in group],
         250_000_000,
-    )(send4, up_grads, down_grads, hidden, grad, gain, chances, named, router, out_w, qkv_w, *heads, lse, shared)
+    )(up_grads, down_grads, hidden, grad, gain, chances, named, *lazy)
 
 
 class Group:
@@ -1832,14 +1871,14 @@
         self.out[...] = self.out[...] + self.got[index]
 
 
-def last_exchange(down_grads, out_grads, qkv_grads, both, cotangents, dup, act, branch, hidden, tokens_grad, small, number):
+def last_exchange(out_grads, qkv_grads, both, cotangents, dup, act, branch, hidden, tokens_grad, small, number):
     parts = lax.axis_size("context")
     rows, width = hidden.shape
     block = lanes = width // (2 * parts)
     units = WINDOW * parts - 128
     head, span = out_grads.shape[0], qkv_grads.shape[1]
-    shapes = [(head, lanes), (block, span), (WINDOW, lanes), (block, 2 * WINDOW), (WINDOW, lanes)]
-    pieces = [1, 1, 1, 2, 1]
+    shapes = [(head, lanes), (block, span), (block, 2 * WINDOW), (WINDOW, lanes)]
+    pieces = [1, 3, 2, 1]
     count, bf16 = len(shapes), jnp.bfloat16
     groups = [
         Return.scratch(shapes, pieces, parts),
@@ -1850,8 +1889,8 @@
         Grads.scratch() + [pltpu.VMEM(one.shape, bf16) for one in (both, cotangents, dup, act)] + [DMA((4,))],
     ]
     piece, column = jax.ShapeDtypeStruct((block, units), bf16), jax.ShapeDtypeStruct((units, lanes), bf16)
-    out_shape = [jax.ShapeDtypeStruct((parts * head, lanes), bf16), jax.ShapeDtypeStruct((parts * block, span), bf16)]
-    out_shape += [column, piece, piece, column]
+    out_shape = [jax.ShapeDtypeStruct((parts * head, lanes), bf16), jax.ShapeDtypeStruct((3, block, parts * HEAD_DIM), bf16)]
+    out_shape += [piece, piece, column]
     out_shape += [
         jax.ShapeDtypeStruct((width, 2 * WINDOW), bf16),
         jax.ShapeDtypeStruct((WINDOW, width), bf16),
@@ -1860,7 +1899,7 @@
         jax.ShapeDtypeStruct(small.shape, jnp.float32),
     ]
 
-    def kernel(downg_ref, outg_ref, qkvg_ref, both_hbm, cots_hbm, dup_hbm, act_hbm, branch_ref, hidden_ref, tokens_ref, small_ref, *rest):
+    def kernel(outg_ref, qkvg_ref, both_hbm, cots_hbm, dup_hbm, act_hbm, branch_ref, hidden_ref, tokens_ref, small_ref, *rest):
         outs, scratch = rest[: len(out_shape)], list(rest[len(out_shape) :])
         sets = []
         for one in groups:
@@ -1881,13 +1920,18 @@
             },
             {
                 "block": lambda side, part: rows_at(qkvg_ref, (side * parts + part) * block, block),
-                "pieces": [(lambda buf, short: buf, lambda source, short: rows_at(grads[1], source * block, block))],
+                "pieces": [
+                    (
+                        lambda buf, short, which=which: buf.at[:, pl.ds(which * HEAD_DIM, HEAD_DIM)],
+                        lambda source, short, which=which: lanes_at(grads[1].at[which], source * HEAD_DIM, HEAD_DIM),
+                    )
+                    for which in range(3)
+                ],
             },
         ]
         items += [
-            down_item(downg_ref, 1, 1, grads[2], parts),
-            up_item(upg2_hbm, 0, 2, grads[3], grads[4], block, parts),
-            down_item(downg2_hbm, 0, 2, grads[5], parts),
+            up_item(upg2_hbm, 0, 2, grads[2], grads[3], block, parts),
+            down_item(downg2_hbm, 0, 2, grads[4], parts),
         ]
         spot = Spot()
         back = Return(spot, items, sets[0][:count], sets[0][count : 2 * count], sets[0][2 * count :])
@@ -1899,7 +1943,7 @@
         spot.greet(True, True)
         total.begin()
         summed.begin()
-        for item in range(3):
+        for item in range(2):
             back.start(item)
         for copy in loads:
             copy.start()
@@ -1920,10 +1964,8 @@
         for copy in loads:
             copy.wait()
         Grads(both_ref, cots_ref, dup_ref, act_ref, upg2_hbm, downg2_hbm, *grad_refs).run()
+        back.start(2)
         back.start(3)
-        back.start(4)
-        for index in range(parts):
-            back.reduce(2, index)
         total.take(4)
         tokens_group.begin()
         for index in range(parts):
@@ -1945,7 +1987,7 @@
 
         summed.chunks(finish)
         block_group.begin()
-        for item in range(3, count):
+        for item in range(2, count):
             for index in range(parts):
                 back.reduce(item, index)
         summed.end()
@@ -1959,10 +2001,10 @@
         "last_exchange",
         out_shape,
         [IN_PLACE] * (len(out_shape) - 1) + [IN_VMEM],
-        [IN_PLACE] * 7 + [IN_VMEM] * 4,
+        [IN_PLACE] * 6 + [IN_VMEM] * 4,
         [one for group in groups for one in group],
         300_000_000,
-    )(down_grads, out_grads, qkv_grads, both, cotangents, dup, act, branch, hidden, tokens_grad, small)
+    )(out_grads, qkv_grads, both, cotangents, dup, act, branch, hidden, tokens_grad, small)
 
 
 def widen(singles, pairs):
@@ -2050,9 +2092,7 @@
     turns_high = turns.astype(bf16)
     turns_low = (turns - turns_high.astype(jnp.float32)).astype(bf16)
     send1 = jnp.concatenate([(normed1 * gain1).astype(bf16), turns_high, turns_low], 1)
-    qkv_in = jnp.transpose(
-        qkv_weight.reshape(block, 3, parts, HEAD_DIM), (2, 0, 1, 3)
-    ).reshape(parts * block, 3 * HEAD_DIM)
+    qkv_in = jnp.transpose(qkv_weight, (1, 0, 2))
     bias_here = lax.dynamic_slice_in_dim(
         qkv_bias.reshape(3, parts, HEAD_DIM), place, 1, 1
     ).reshape(1, 3 * HEAD_DIM)
@@ -2096,6 +2136,7 @@
         down_grads[0],
         up_grads[2],
         up_grads[3],
+        down_grads[1],
         dots_own,
         dxn2,
         dhidden,
@@ -2148,7 +2189,6 @@
     (
         out_w_grad,
         qkv_grad,
-        down_grads[1],
         up_grads[4],
         up_grads[5],
         down_grads[2],
@@ -2158,7 +2198,6 @@
         tokens_grad,
         small,
     ) = last_exchange(
-        down_g,
         out_g,
         qkv_g,
         both,
@@ -2178,19 +2217,16 @@
         lax.dynamic_slice_in_dim(bias_sum, group, 1, 0)[0], (1, 0, 2)
     ).reshape(3, parts * HEAD_DIM)
 
-    qkv_grad = jnp.transpose(
-        qkv_grad.reshape(parts, block, 3, HEAD_DIM), (1, 2, 0, 3)
-    ).reshape(block, 3, parts * HEAD_DIM).astype(jnp.float32)
-    singles = [(block_out, True), (tokens_grad, False), (out_w_grad, False)]
+    singles = [(block_out, True), (tokens_grad, False), (out_w_grad, False), (qkv_grad, False)]
     singles += [(up_grads[0], False), (up_grads[1], False), (down_grads[0], False)]
     pairs = [up_grads[2::2], up_grads[3::2], down_grads[1:]]
-    block_out, tokens_grad, out_w_grad, *shared_grads, gate_grads, up_grads, down_grads = widen(singles, pairs)
+    block_out, tokens_grad, out_w_grad, qkv_grad, *shared_grads, gate_grads, up_grads, down_grads = widen(singles, pairs)
 
     return (
         block_out[None],
         tokens_grad[None],
         small[:width],
-        qkv_grad,
+        jnp.transpose(qkv_grad, (1, 0, 2)),
         bias_grad,
         out_w_grad,
         small[width : 2 * width],

time: 585 us -> 577 us (0.986)
    pallas_call x1, Pallas kernels: 127 us -> 138 us  [attention_last(): comm_call(kernel, number, 'attention_last', [jax.ShapeDtypeStruct((length...]
    pallas_call x1, Pallas kernels: 176 us -> 168 us  [share_move_compute(): comm_call(kernel, number, 'share_move_compute', [jax.ShapeDtypeStruct((le...]
    pallas_call x1, Pallas kernels: 121 us -> 114 us  [last_exchange(): comm_call(kernel, number, 'last_exchange', out_shape, [IN_PLACE] * (len(o...]
where the time goes in v6:
time: 577 us; the launch traced here: 576 us
  Pallas kernels  554 us (96%)
  other arithmetic  10.3 us (2%)
  local copies, waits for them, and re-layouts  9.27 us (2%)
    pallas_call x1, Pallas kernels, share_move_compute(): comm_call(kernel, number, 'share_move_compute', [jax.ShapeDtypeStruct((le...  168 us
    pallas_call x1, Pallas kernels, attention_last(): comm_call(kernel, number, 'attention_last', [jax.ShapeDtypeStruct((length...  138 us
    pallas_call x1, Pallas kernels, attention_first(): comm_call(kernel, number, 'attention_first', [jax.ShapeDtypeStruct((lengt...  123 us
    pallas_call x1, Pallas kernels, last_exchange(): comm_call(kernel, number, 'last_exchange', out_shape, [IN_PLACE] * (len(o...  114 us

profile of v6, /device:TPU:16, one launch (start us, length us, event | category | flops | bytes accessed | tf_op | source)
XLA Modules:
  0.0 576.0 jit_solution(12891413746566041097)
XLA Ops:
  0.7 1.1 dynamic-slice_bitcast_fusion
  2.0 0.7 fusion.52
  2.7 0.7 fusion.53
  3.4 0.7 fusion.28
  4.3 0.2 multiply_cosine_fusion
  4.7 0.7 pad_maximum_fusion.own_ref
  5.5 0.8 maximum_select_fusion.2.grad_ref
  6.2 0.7 convert_bitcast_fusion
  6.9 0.6 copy.80
  7.5 122.9 %attention_first.1 = (bf16[1024,2304]{1,0:T(8,128)(2,1)}, bf16[1024,2048]{1,0:T(8,128)(2,1)}, bf16[2048,384]{1,0:T(8,128)(2,1)}, bf16[128,2048]{1,0:T(8,128)(2,1...) custom-call(bf16[64,2304]{1,0:T(8,128)(2,1)} %pad_maximum_fusion.own, ...), custom_call_target="tpu_custom_call" | custom-call | bytes 250000000 | tf_op jit(solution)/shard_map/attention_first/pallas_call | solution.py:1306
  130.5 1.2 multiply_reduce_fusion.1
  131.9 0.2 fusion.13
  133.0 0.8 concatenate.64.own_ref
  133.8 167.8 %share_move_compute.1 = (bf16[1024,2176]{1,0:T(8,128)(2,1)}, bf16[1024,2176]{1,0:T(8,128)(2,1)}, bf16[1024,2048]{1,0:T(8,128)(2,1)}, bf16[1024,768]{1,0:T(8,128)...) custom-call(bf16[64,2176]{1,0:T(8,128)(2,1)} %concatenate.64.own_ref, ...), custom_call_target="tpu_custom_call" | custom-call | bytes 300000000 | tf_op jit(solution)/shard_map/share_move_compute/pallas_call | solution.py:1554
  301.6 0.6 pad.19.chance_ref
  302.3 1.1 pad_convert_fusion.rest_1_
  303.3 0.6 pad.20.named_ref
  304.0 137.7 %attention_last.1 = (bf16[1024,2048]{1,0:T(8,128)(2,1)}, bf16[1408,256]{1,0:T(8,128)(2,1)}, bf16[256,1408]{1,0:T(8,128)(2,1)}, bf16[256,1408]{1,0:T(8,128)(2,1)}...) custom-call(bf16[2048,1536]{1,0:T(8,128)(2,1)} %get-tuple-element.67, ...), custom_call_target="tpu_custom_call" | custom-call | bytes 250000000 | tf_op jit(solution)/shard_map/attention_last/pallas_call | solution.py:1774
  441.7 1.0 multiply_reduce_fusion.2
  442.7 1.1 fusion.18
  443.8 0.3 copy.69
  444.2 0.5 reshape.123
  444.9 0.2 fusion.33
  445.1 1.2 multiply_reduce_fusion
  446.3 0.3 fusion.9
  447.0 0.9 maximum_select_fusion.tokens_ref
  447.9 114.0 %last_exchange.1 = (bf16[512,256]{1,0:T(8,128)(2,1)}, bf16[3,256,512]{2,1,0:T(8,128)(2,1)}, bf16[256,1408]{1,0:T(8,128)(2,1)}, bf16[256,1408]{1,0:T(8,128)(2,1)}...) custom-call(bf16[128,2048]{1,0:T(8,128)(2,1)} %get-tuple-element.78., ...), custom_call_target="tpu_custom_call" | custom-call | bytes 300000000 | tf_op jit(solution)/shard_map/last_exchange/pallas_call | solution.py:1998
  561.9 11.3 %widen.1 = (bf16[256,2048]{1,0:T(8,128)(2,1)}, f32[256,2048]{1,0:T(8,128)}, f32[512,256]{1,0:T(8,128)}, f32[3,256,512]{2,1,0:T(8,128)}, f32[256,1408]{1,0:T(8,12...) custom-call(bf16[256,2048]{1,0:T(8,128)(2,1)} %get-tuple-element.89., ...), custom_call_target="tpu_custom_call" | custom-call | tf_op jit(solution)/shard_map/widen/pallas_call | solution.py:2032
  573.2 0.6 reshape.128
  573.8 0.9 copy.71
  574.8 0.6 copy.78
  575.4 0.6 slice_bitcast_fusion
  (77 shorter events, 2.3 us)
Async XLA Ops:
  0.6 131.8 %copy-start = (s32[1,256,4]{1,2,0:T(4,128)S(1)}, s32[1,256,4]{1,2,0:T(4,128)}, u32[]{:S(2)}) copy-start(s32[1,256,4]{1,2,0:T(4,128)} %param.19) | copy-start | bytes 12292
  0.7 3.6 copy-start.13
  4.1 127.6 %copy-start.10 = (f32[2048]{0:T(1024)}, f32[2048]{0:T(1024)S(1)}, u32[]{:S(2)}) copy-start(f32[2048]{0:T(1024)S(1)} %get-tuple-element.230) | copy-start | bytes 24580
  7.5 124.3 %copy-start.8 = (bf16[2048,8]{0,1:T(8,128)(2,1)S(1)}, bf16[2048,8]{0,1:T(8,128)(2,1)}, u32[]{:S(2)}) copy-start(bf16[2048,8]{0,1:T(8,128)(2,1)} %param.26) | copy-start | bytes 98308
  7.5 124.4 %copy-start.11 = (bf16[2048]{0:T(1024)(128)(2,1)S(1)}, bf16[2048]{0:T(1024)(128)(2,1)}, u32[]{:S(2)}) copy-start(bf16[2048]{0:T(1024)(128)(2,1)} %param.30) | copy-start | bytes 12292
  131.7 170.0 %copy-start.2 = (f32[64,2048]{1,0:T(8,128)}, f32[64,2048]{1,0:T(8,128)S(1)}, u32[]{:S(2)}) copy-start(f32[64,2048]{1,0:T(8,128)S(1)} %get-tuple-element.195.hidden_ref) | copy-start | bytes 1572868
  441.7 3.0 copy-start.6
  441.7 3.4 copy-start.3
  441.7 4.6 copy-start.4
  441.7 5.0 copy-start.12
  441.7 5.1 copy-start.5
  446.8 1.1 copy-start.7
  561.9 11.3 %copy-start.9 = (f32[224,128]{1,0:T(8,128)S(1)}, f32[224,128]{1,0:T(8,128)}, u32[]{:S(2)}) copy-start(f32[224,128]{1,0:T(8,128)} %get-tuple-element.104) | copy-start | bytes 344068
  561.9 14.1 %copy-start.1 = (s32[1,256,4]{1,2,0:T(4,128)S(1)}, s32[1,256,4]{1,2,0:T(4,128)}, u32[]{:S(2)}) copy-start(s32[1,256,4]{1,2,0:T(4,128)} %param.19) | copy-start | bytes 12292

commit v7 on v6

--- a/solution.py
+++ b/solution.py
@@ -1605,7 +1605,7 @@
     }
 
 
-def attention_last(send4, up_grads, down_grads, hidden, grad, gain, chances, named, router, out_w, qkv_w, heads, lse, shared, number):
+def attention_last(send4, up_grads, down_grads, hidden, grad, gain, chances, router, out_w, qkv_w, heads, lse, shared, number):
     lazy = [send4, router, out_w, qkv_w, *heads, lse, shared]
     parts = lax.axis_size("context")
     length, width = send4.shape[0], hidden.shape[1]
@@ -1637,7 +1637,7 @@
         Return.scratch(shapes, pieces, parts),
     ]
 
-    def kernel(upg_ref, downg_ref, hidden_ref, grad_ref, gain_ref, chance_ref, named_ref, *rest):
+    def kernel(upg_ref, downg_ref, hidden_ref, grad_ref, gain_ref, chance_ref, *rest):
         sources, rest = rest[: len(lazy)], rest[len(lazy) :]
         (dh_hbm, down_out, gate_out1, up_out1, down_out1, dots_ref, dxn2_ref, dhidden_ref, outg_ref, qkvg_ref, bias_ref, dxn1_ref), scratch = rest[:12], rest[12:]
         scratch, split = list(scratch), []
@@ -1667,8 +1667,8 @@
             lane = lax.broadcasted_iota(jnp.int32, (rows, 128), 1)
             dots = sums[:, width:]
             dots_ref[...] = dots
-            chance = chance_ref[...]
-            dprob = dots * named_ref[...]
+            chance = chance_ref[:, :128]
+            dprob = dots * chance_ref[:, 128:]
             prob = jnp.where(lane < experts, chance, 0.0)
             dlogit = prob * (dprob - jnp.sum(prob * dprob, -1, keepdims=True))
             mix = jnp.where(lane < experts, dlogit, jnp.where(lane == experts, chance * (1.0 - chance) * dots, 0.0))
@@ -1790,10 +1790,10 @@
             jax.ShapeDtypeStruct((rows, width), f32),
         ],
         [IN_PLACE] * 5 + [IN_VMEM] * 7,
-        [IN_PLACE] * 2 + [IN_VMEM] * 5 + [IN_PLACE] * len(lazy),
+        [IN_PLACE] * 2 + [IN_VMEM] * 4 + [IN_PLACE] * len(lazy),
         [one for group in sets for one in group],
         250_000_000,
-    )(up_grads, down_grads, hidden, grad, gain, chances, named, *lazy)
+    )(up_grads, down_grads, hidden, grad, gain, chances, *lazy)
 
 
 class Group:
@@ -1886,7 +1886,7 @@
         Total.scratch(small.shape),
         Group.sems(),
         Group.sems(),
-        Grads.scratch() + [pltpu.VMEM(one.shape, bf16) for one in (both, cotangents, dup, act)] + [DMA((4,))],
+        Grads.scratch() + [pltpu.VMEM(one.shape, bf16) for one in (both, cotangents, dup, act, branch)] + [DMA((5,))],
     ]
     piece, column = jax.ShapeDtypeStruct((block, units), bf16), jax.ShapeDtypeStruct((units, lanes), bf16)
     out_shape = [jax.ShapeDtypeStruct((parts * head, lanes), bf16), jax.ShapeDtypeStruct((3, block, parts * HEAD_DIM), bf16)]
@@ -1899,18 +1899,18 @@
         jax.ShapeDtypeStruct(small.shape, jnp.float32),
     ]
 
-    def kernel(outg_ref, qkvg_ref, both_hbm, cots_hbm, dup_hbm, act_hbm, branch_ref, hidden_ref, tokens_ref, small_ref, *rest):
+    def kernel(outg_ref, qkvg_ref, both_hbm, cots_hbm, dup_hbm, act_hbm, branch_hbm, hidden_ref, tokens_ref, small_ref, *rest):
         outs, scratch = rest[: len(out_shape)], list(rest[len(out_shape) :])
         sets = []
         for one in groups:
             sets.append(scratch[: len(one)])
             scratch = scratch[len(one) :]
         grads, (upg2_hbm, downg2_hbm, block_all, tokens_all, small_out) = outs[:-5], outs[-5:]
-        *grad_refs, both_ref, cots_ref, dup_ref, act_ref, load = sets[5]
+        *grad_refs, both_ref, cots_ref, dup_ref, act_ref, branch_ref, load = sets[5]
         loads = [
             pltpu.make_async_copy(source, target, load.at[index])
             for index, (source, target) in enumerate(
-                ((both_hbm, both_ref), (cots_hbm, cots_ref), (dup_hbm, dup_ref), (act_hbm, act_ref))
+                ((both_hbm, both_ref), (cots_hbm, cots_ref), (dup_hbm, dup_ref), (act_hbm, act_ref), (branch_hbm, branch_ref))
             )
         ]
         items = [
@@ -1940,12 +1940,14 @@
         total = Total(spot, small_ref, small_out, sets[2])
         tokens_group = Group(spot, tokens_ref, tokens_all, sets[3])
         block_group = Group(spot, own_block, block_all, sets[4])
+        loads[4].start()
         spot.greet(True, True)
         total.begin()
-        summed.begin()
         for item in range(2):
             back.start(item)
-        for copy in loads:
+        loads[4].wait()
+        summed.begin()
+        for copy in loads[:4]:
             copy.start()
         total.take(0)
         total.send(1)
@@ -1961,7 +1963,7 @@
             back.reduce(1, index)
         total.take(3)
         total.send(4)
-        for copy in loads:
+        for copy in loads[:4]:
             copy.wait()
         Grads(both_ref, cots_ref, dup_ref, act_ref, upg2_hbm, downg2_hbm, *grad_refs).run()
         back.start(2)
@@ -2001,7 +2003,7 @@
         "last_exchange",
         out_shape,
         [IN_PLACE] * (len(out_shape) - 1) + [IN_VMEM],
-        [IN_PLACE] * 6 + [IN_VMEM] * 4,
+        [IN_PLACE] * 7 + [IN_VMEM] * 3,
         [one for group in groups for one in group],
         300_000_000,
     )(out_grads, qkv_grads, both, cotangents, dup, act, branch, hidden, tokens_grad, small)
@@ -2128,8 +2130,8 @@
     up_grads, down_grads = [None] * (2 * stacks), [None] * stacks
     up_grads[:2] = first_grads
     side = 128 - expert_count - 1
-    chances = jnp.pad(jnp.concatenate([prob, sig_own[:, None]], 1), ((0, 0), (0, side)))
-    named_wide = jnp.pad(named, ((0, 0), (0, 128 - expert_count)))
+    blank = jnp.zeros((own_rows, side), jnp.float32)
+    chances = jnp.concatenate([prob, sig_own[:, None], blank, named, blank, blank[:, :1]], 1)
     router_wide = jnp.pad(heads_w.T.astype(jnp.float32), ((0, side), (0, 0)))
     (
         _,
@@ -2152,7 +2154,6 @@
         grad_own_b,
         gain2[None, :],
         chances,
-        named_wide,
         router_wide,
         out_w,
         qkv_w,

time: 577 us -> 576 us (level)
  no operation moved by 1% of the time
where the time goes in v7:
time: 576 us
  Pallas kernels  554 us (96%)
  other arithmetic  10.4 us (2%)
  local copies, waits for them, and re-layouts  8.77 us (2%)
    pallas_call x1, Pallas kernels, share_move_compute(): comm_call(kernel, number, 'share_move_compute', [jax.ShapeDtypeStruct((le...  168 us
    pallas_call x1, Pallas kernels, attention_last(): comm_call(kernel, number, 'attention_last', [jax.ShapeDtypeStruct((length...  137 us
    pallas_call x1, Pallas kernels, attention_first(): comm_call(kernel, number, 'attention_first', [jax.ShapeDtypeStruct((lengt...  123 us
    pallas_call x1, Pallas kernels, last_exchange(): comm_call(kernel, number, 'last_exchange', out_shape, [IN_PLACE] * (len(o...  114 us

profile of v7, /device:TPU:16, one launch (start us, length us, event | category | flops | bytes accessed | tf_op | source)
XLA Modules:
  0.0 575.6 jit_solution(7019566408593342017)
XLA Ops:
  0.7 1.1 dynamic-slice_bitcast_fusion
  1.8 0.2 fusion.10
  2.0 0.7 fusion.53
  2.7 0.7 fusion.54
  3.4 0.7 fusion.29
  4.3 0.2 multiply_cosine_fusion
  4.7 0.7 pad_maximum_fusion.own_ref
  5.5 0.8 maximum_select_fusion.2.grad_ref
  6.2 0.7 convert_bitcast_fusion
  6.9 0.6 copy.80
  7.5 122.9 %attention_first.1 = (bf16[1024,2304]{1,0:T(8,128)(2,1)}, bf16[1024,2048]{1,0:T(8,128)(2,1)}, bf16[2048,384]{1,0:T(8,128)(2,1)}, bf16[128,2048]{1,0:T(8,128)(2,1...) custom-call(bf16[64,2304]{1,0:T(8,128)(2,1)} %pad_maximum_fusion.own, ...), custom_call_target="tpu_custom_call" | custom-call | bytes 250000000 | tf_op jit(solution)/shard_map/attention_first/pallas_call | solution.py:1306
  130.5 1.2 multiply_reduce_fusion.1
  133.1 0.8 concatenate.64.own_ref
  133.9 167.8 %share_move_compute.1 = (bf16[1024,2176]{1,0:T(8,128)(2,1)}, bf16[1024,2176]{1,0:T(8,128)(2,1)}, bf16[1024,2048]{1,0:T(8,128)(2,1)}, bf16[1024,768]{1,0:T(8,128)...) custom-call(bf16[64,2176]{1,0:T(8,128)(2,1)} %concatenate.64.own_ref, ...), custom_call_target="tpu_custom_call" | custom-call | bytes 300000000 | tf_op jit(solution)/shard_map/share_move_compute/pallas_call | solution.py:1554
  301.7 0.7 concatenate.65.chance_ref
  302.4 1.1 pad_convert_fusion.rest_1_
  303.5 137.4 %attention_last.1 = (bf16[1024,2048]{1,0:T(8,128)(2,1)}, bf16[1408,256]{1,0:T(8,128)(2,1)}, bf16[256,1408]{1,0:T(8,128)(2,1)}, bf16[256,1408]{1,0:T(8,128)(2,1)}...) custom-call(bf16[2048,1536]{1,0:T(8,128)(2,1)} %get-tuple-element.67, ...), custom_call_target="tpu_custom_call" | custom-call | bytes 250000000 | tf_op jit(solution)/shard_map/attention_last/pallas_call | solution.py:1774
  441.0 1.0 multiply_reduce_fusion.2
  442.0 1.1 fusion.18
  443.1 0.3 copy.69
  443.4 0.5 reshape.123
  444.1 0.2 fusion.34
  444.4 1.2 multiply_reduce_fusion
  445.6 0.3 fusion.9
  446.1 0.2 fusion.8
  446.3 0.9 maximum_select_fusion.tokens_ref
  447.2 114.4 %last_exchange.1 = (bf16[512,256]{1,0:T(8,128)(2,1)}, bf16[3,256,512]{2,1,0:T(8,128)(2,1)}, bf16[256,1408]{1,0:T(8,128)(2,1)}, bf16[256,1408]{1,0:T(8,128)(2,1)}...) custom-call(bf16[128,2048]{1,0:T(8,128)(2,1)} %get-tuple-element.78., ...), custom_call_target="tpu_custom_call" | custom-call | bytes 300000000 | tf_op jit(solution)/shard_map/last_exchange/pallas_call | solution.py:2000
  561.5 11.3 %widen.1 = (bf16[256,2048]{1,0:T(8,128)(2,1)}, f32[256,2048]{1,0:T(8,128)}, f32[512,256]{1,0:T(8,128)}, f32[3,256,512]{2,1,0:T(8,128)}, f32[256,1408]{1,0:T(8,12...) custom-call(bf16[256,2048]{1,0:T(8,128)(2,1)} %get-tuple-element.89., ...), custom_call_target="tpu_custom_call" | custom-call | tf_op jit(solution)/shard_map/widen/pallas_call | solution.py:2034
  572.8 0.6 reshape.128
  573.4 0.9 copy.71
  574.4 0.6 copy.78
  575.0 0.6 slice_bitcast_fusion
  (77 shorter events, 2.2 us)
Async XLA Ops:
  0.6 131.8 %copy-start = (s32[1,256,4]{1,2,0:T(4,128)S(1)}, s32[1,256,4]{1,2,0:T(4,128)}, u32[]{:S(2)}) copy-start(s32[1,256,4]{1,2,0:T(4,128)} %param.19) | copy-start | bytes 12292
  0.7 3.6 copy-start.13
  4.1 127.6 %copy-start.10 = (f32[2048]{0:T(1024)}, f32[2048]{0:T(1024)S(1)}, u32[]{:S(2)}) copy-start(f32[2048]{0:T(1024)S(1)} %get-tuple-element.228) | copy-start | bytes 24580
  7.5 124.3 %copy-start.8 = (bf16[2048,8]{0,1:T(8,128)(2,1)S(1)}, bf16[2048,8]{0,1:T(8,128)(2,1)}, u32[]{:S(2)}) copy-start(bf16[2048,8]{0,1:T(8,128)(2,1)} %param.26) | copy-start | bytes 98308
  7.5 124.4 %copy-start.11 = (bf16[2048]{0:T(1024)(128)(2,1)S(1)}, bf16[2048]{0:T(1024)(128)(2,1)}, u32[]{:S(2)}) copy-start(bf16[2048]{0:T(1024)(128)(2,1)} %param.30) | copy-start | bytes 12292
  131.7 170.0 %copy-start.2 = (f32[64,2048]{1,0:T(8,128)}, f32[64,2048]{1,0:T(8,128)S(1)}, u32[]{:S(2)}) copy-start(f32[64,2048]{1,0:T(8,128)S(1)} %get-tuple-element.195.hidden_ref) | copy-start | bytes 1572868
  440.9 3.0 copy-start.6
  440.9 3.4 copy-start.3
  441.0 4.6 copy-start.4
  441.0 5.0 copy-start.12
  441.0 5.1 copy-start.5
  446.0 1.1 copy-start.7
  561.5 11.3 %copy-start.9 = (f32[224,128]{1,0:T(8,128)S(1)}, f32[224,128]{1,0:T(8,128)}, u32[]{:S(2)}) copy-start(f32[224,128]{1,0:T(8,128)} %get-tuple-element.104) | copy-start | bytes 344068
  561.5 14.1 %copy-start.1 = (s32[1,256,4]{1,2,0:T(4,128)S(1)}, s32[1,256,4]{1,2,0:T(4,128)}, u32[]{:S(2)}) copy-start(s32[1,256,4]{1,2,0:T(4,128)} %param.19) | copy-start | bytes 12292
